TPU v7x, 1024 devices: a whole 4x8x16 slice. The times are simulated.
1024 devices in a mesh: seq: 64 (over z, x), head: 16 (over y, core).
Axes of the slice: x: 4, y: 8, z: 16, core: 2. Of those that a mesh axis runs over, the one named last changes fastest.
Arguments:
- queries: bfloat16 [8192, 16, 64], P('seq', 'head'), may hold values from -6 to 6
- keys_values: bfloat16 [8192, 16, 128], P('seq', 'head'), may hold values from -6 to 6
- out_weight: bfloat16 [16, 64, 4096], P('head'), may hold values from -1 to 1
- out_grad: bfloat16 [8192, 4096], P('seq'), may hold values from -0.75 to 0.75
- block_order: int32 [64], replicated, may hold values from 0 to 63, each once
Outputs:
- mixed_out: bfloat16 [8192, 4096], P('seq', 'head')
- grad_queries: bfloat16 [8192, 16, 64], P('seq', 'head')
- grad_keys_values: bfloat16 [8192, 16, 128], P('seq', 'head')
Inputs may be any that keep to these rules, and one draw needn't show every extreme that they name: `block_order`: A permutation of the sequence blocks 0 to 63.
All inputs are finite; a program needn't handle non-finite values.
Results may differ from a plain program's by a relative error of at most 0.03.
Values may be sent and summed in bfloat16 or wider, within the bound.
No kernel may reach another device: no remote copies, remote signals or barrier semaphores. Data moves between devices by JAX's collectives and lax.ppermute only.
A program may use at most 32 MiB of HBM per device.

v0:
```python
import math

import jax
import jax.numpy as jnp
from jax import lax
from jax.sharding import Mesh
from jax.sharding import PartitionSpec as P

SEQ = ("seq_0", "seq_1")


def gather_axes(value, axes, dim):
    out = value
    for number in range(len(axes) - 1, -1, -1):
        out = lax.all_gather(out, axes[number], axis=dim, tiled=True)
    return out


def copy_for_each(value, axis):
    peers = lax.axis_size(axis)
    return lax.all_to_all(
        jnp.broadcast_to(value[None], (peers, *value.shape)), axis, 0, 0, tiled=True
    )


def laid_out(parts, dim):
    parts = jnp.moveaxis(parts, 0, dim)
    dims = parts.shape
    return parts.reshape(*dims[:dim], dims[dim] * dims[dim + 1], *dims[dim + 2 :])


def gather_directly(value, axis, dim):
    parts = copy_for_each(value, axis)
    return laid_out(parts, dim)


def side_by_side(arrays, axis, dim, along):
    widths = [a.shape[along] for a in arrays]
    both = jnp.concatenate(arrays, axis=along)
    out = lax.all_gather(both, axis, axis=dim, tiled=True)
    return tuple(jnp.split(out, [sum(widths[:k]) for k in range(1, len(widths))], axis=along))


def log_normalizer(scores, allowed):
    masked = jnp.where(allowed, scores, -jnp.inf)
    row_max = jnp.max(masked, axis=-1, keepdims=True)
    row_total = jnp.sum(jnp.exp(masked - row_max), axis=-1, keepdims=True)
    return (row_max + jnp.log(row_total))[..., 0]


def local(queries, keys_values, out_weight, out_grad, block_order):
    tok_rows = queries.shape[0]
    head_width = queries.shape[2]
    inv_root = 1.0 / math.sqrt(head_width)
    my_block = block_order[lax.axis_index(SEQ)]
    offsets = jnp.arange(tok_rows, dtype=jnp.int32)
    my_position = my_block * tok_rows + offsets
    all_position = (block_order[:, None] * tok_rows + offsets[None, :]).reshape(-1)
    gathered = gather_axes(keys_values, SEQ, 0)
    all_keys = gathered[:, :, :head_width]
    all_values = gathered[:, :, head_width:]
    allowed = (all_position[None, :] <= my_position[:, None])[None]
    scores = (
        jnp.einsum("qhd,khd->hqk", queries, all_keys, preferred_element_type=jnp.float32) * inv_root
    )
    log_total = log_normalizer(scores, allowed)
    probs_low = jnp.where(allowed, jnp.exp(scores - log_total[:, :, None]), 0.0).astype(
        jnp.bfloat16
    )
    attended = jnp.einsum(
        "hqk,khd->qhd", probs_low, all_values, preferred_element_type=jnp.float32
    ).astype(jnp.bfloat16)
    every_head = gather_directly(attended, "head", 1)
    column_weight = lax.all_to_all(out_weight, "head", split_axis=2, concat_axis=0, tiled=True)
    mixed_out = jnp.einsum(
        "qhd,hde->qe", every_head, column_weight, preferred_element_type=jnp.float32
    ).astype(jnp.bfloat16)
    grad_att = jnp.einsum(
        "qe,hde->qhd", out_grad, out_weight, preferred_element_type=jnp.float32
    ).astype(jnp.bfloat16)
    grad_dot = jnp.sum(grad_att.astype(jnp.float32) * attended.astype(jnp.float32), axis=2)
    dprob = jnp.einsum("qhd,khd->hqk", grad_att, all_values, preferred_element_type=jnp.float32)
    dscore = (probs_low.astype(jnp.float32) * (dprob - grad_dot.T[:, :, None])).astype(jnp.bfloat16)
    grad_queries = (
        jnp.einsum("hqk,khd->qhd", dscore, all_keys, preferred_element_type=jnp.float32) * inv_root
    ).astype(jnp.bfloat16)
    query_all, grad_all = side_by_side((queries, grad_att), SEQ, 0, 1)
    norm_all, dot_all = side_by_side((log_total.T, grad_dot), SEQ, 0, 1)
    own_keys = keys_values[:, :, :head_width]
    own_values = keys_values[:, :, head_width:]
    visible = (my_position[None, :] <= all_position[:, None])[None]
    back_scores = (
        jnp.einsum("qhd,khd->hqk", query_all, own_keys, preferred_element_type=jnp.float32)
        * inv_root
    )
    back_probs = jnp.where(visible, jnp.exp(back_scores - norm_all.T[:, :, None]), 0.0).astype(
        jnp.bfloat16
    )
    back_dprob = jnp.einsum(
        "qhd,khd->hqk", grad_all, own_values, preferred_element_type=jnp.float32
    )
    back_dscore = (back_probs.astype(jnp.float32) * (back_dprob - dot_all.T[:, :, None])).astype(
        jnp.bfloat16
    )
    grad_keys = (
        jnp.einsum("hqk,qhd->khd", back_dscore, query_all, preferred_element_type=jnp.float32)
        * inv_root
    )
    grad_values = jnp.einsum(
        "hqk,qhd->khd", back_probs, grad_all, preferred_element_type=jnp.float32
    )
    grad_keys_values = jnp.concatenate([grad_keys, grad_values], axis=2).astype(jnp.bfloat16)
    return (mixed_out, grad_queries, grad_keys_values)


def solution(mesh):
    finer = Mesh(mesh.devices.reshape(16, 4, mesh.shape["head"]), ("seq_0", "seq_1", "head"))
    in_specs = (
        P(SEQ, "head", None),
        P(SEQ, "head", None),
        P("head", None, None),
        P(SEQ, None),
        P(),
    )
    out_specs = (P(SEQ, "head"), P(SEQ, "head", None), P(SEQ, "head", None))
    return jax.shard_map(local, mesh=finer, in_specs=in_specs, out_specs=out_specs, check_vma=False)
```

profile of v0, /device:TPU:6, one launch (start us, length us, event | category | flops | bytes accessed | tf_op | source)
XLA Modules:
  0.0 265.9 jit_solution(8908116826531315372)
XLA Ops:
  7.2 0.0 copy-start
  7.2 0.0 all-gather.3.cloned.1.call-start
  7.2 24.3 %all_gather.12 = bf16[512,1,128]{2,0,1:T(8,128)(2,1)} all-gather(bf16[128,1,128]{2,0,1:T(8,128)(2,1)} %param.6), channel_id=1, replica_groups=mesh['seq_0'=16,'seq_1'=4,'head'=16] {'seq_1'}, dimensions={0}, use_global_device_ids=true | all-gather | bytes 163840 | tf_op jit(solution)/shard_map/all_gather | solution.py:15
  31.5 0.0 all-gather.3.cloned.1.call-update
  31.6 4.9 %copy.12 = bf16[1,64,4096]{1,0,2:T(2,128)(2,1)S(1)} copy(bf16[1,64,4096]{2,1,0:T(8,128)(2,1)} %param.7) | data formatting | bytes 1048576 | tf_op args[2]
  36.4 0.0 copy-start.4
  36.4 0.0 copy-start.7
  36.5 0.5 broadcast.54
  37.0 23.4 %reduce.5 = bf16[4096,64]{1,0:T(8,128)(2,1)} reduce(bf16[4096,1,64]{2,1,0:T(2,128)(2,1)S(1)} %bitcast.105, bf16[]{:T(256)} %broadcast.54), dimensions={1}, to_apply=%bitcast.93.reduce_sub_computation | reduce | bytes 1048578
  60.3 3.0 %reshape.219 = bf16[16,2,8192]{2,1,0:T(2,128)(2,1)} reshape(bf16[4096,64]{1,0:T(8,128)(2,1)} %reduce.5) | data formatting | bytes 1048576
  63.3 4.2 %all-to-all-start.1 = ((bf16[16,2,8192]{2,1,0:T(2,128)(2,1)}), bf16[16,2,8192]{2,1,0:T(2,128)(2,1)}, u32[]{:S(2)}, u32[]{:S(2)}) async-start(bf16[16,2,8192]{2,1,0:T(2,128)(2,1)} %reshape.219), calls=%async_computation.1 | async-start | bytes 1048576 | tf_op jit(solution)/shard_map/all_to_all | solution.py:74
  67.6 0.2 all-gather.5.cloned.1.call-start
  67.8 0.0 copy-done
  67.8 1.5 convolution_convert_fusion
  69.4 0.0 copy-done.4
  69.4 0.6 pad_maximum_fusion
  70.0 0.0 all-gather.5.cloned.1.call-update
  70.0 0.0 copy-done.7
  70.0 0.1 add_bitcast_fusion
  70.1 0.6 dynamic_slice.3
  71.4 0.0 copy-start.5
  71.4 12.2 %all-to-all-done.1 = bf16[16,2,8192]{2,1,0:T(2,128)(2,1)} async-done(((bf16[16,2,8192]{2,1,0:T(2,128)(2,1)}), bf16[16,2,8192]{2,1,0:T(2,128)(2,1)}, u32[]{:S(2)}, u32[]{:S(2)}) %all-to-all-start.1) | async-done | bytes 524320 | tf_op jit(solution)/shard_map/all_to_all | solution.py:74
  83.5 4.1 %reshape.220 = bf16[4096,1,64]{2,1,0:T(2,128)(2,1)S(1)} reshape(bf16[16,2,8192]{2,1,0:T(2,128)(2,1)} %all-to-all-done.1) | data formatting | bytes 1048576
  87.7 1.1 copy.18
  88.8 2.4 copy.14
  91.2 13.6 %all-gather.3.cloned.1.call-done = bf16[8192,1,128]{2,0,1:T(8,128)(2,1)} async-done(((bf16[512,1,128]{2,0,1:T(8,128)(2,1)}), bf16[8192,1,128]{2,0,1:T(8,128)(2,1)}) %all-gather.3.cloned.1.call-update) | async-done | bytes 2097168 | tf_op jit(solution)/shard_map/all_gather | solution.py:15
  104.7 0.0 copy-start.6
  104.7 2.8 %fusion.9 = (f32[128]{0:T(128)S(1)}, f32[128,8192]{1,0:T(8,128)S(1)}) fusion(s32[8192]{0:T(1024)S(1)} %add_bitcast_fusion, s32[128]{0:T(128)S(1)} %iota_add_fusion, bf16[8192,1,128]{2,0,1:T(8,128)(2,1)} %all-gather.3.cloned.1.call-done, bf16[128,1,64]{0,2,1:T(8,128)(2,1)S(1)} %copy-done.4), kind=kOutput, calls=%fused_computation.16 | convolution fusion | flops 138411904 | bytes 6341632 | tf_op jit(solution)/shard_map/qhd,khd->hqk/dot_general | solution.py:64
  107.5 0.0 copy-start.1
  107.5 1.0 exponential_reduce_fusion
  108.6 0.0 copy-done.6
  108.6 2.0 fusion.25
  110.6 0.0 copy-done.1
  110.6 0.8 broadcast_in_dim.14
  111.4 6.8 %all-to-all-start = ((bf16[16,128,1,64]{1,3,2,0:T(8,128)(2,1)}), bf16[16,128,1,64]{1,3,2,0:T(8,128)(2,1)S(1)}, u32[]{:S(2)}, u32[]{:S(2)}) async-start(bf16[16,128,1,64]{1,3,2,0:T(8,128)(2,1)} %broadcast_in_dim.14), calls=%async_computation | async-start | bytes 524288 | tf_op jit(solution)/shard_map/all_to_all | solution.py:21
  118.2 80.7 %all_gather.15 = f32[8192,2]{0,1:T(2,128)S(1)} all-gather(f32[128,2]{0,1:T(2,128)S(1)} %pad_maximum_fusion.2), channel_id=1, replica_groups=mesh['seq_0'=16,'seq_1'=4,'head'=16] {'seq_0','seq_1'}, dimensions={0}, use_global_device_ids=true | all-gather | bytes 66560 | tf_op jit(solution)/shard_map/all_gather | solution.py:40
  198.9 0.0 copy-done.5
  198.9 0.0 copy-start.3
  198.9 6.5 %fusion.21 = bf16[128,1,64]{0,2,1:T(8,128)(2,1)} fusion(bf16[8192,1,128]{2,0,1:T(8,128)(2,1)} %all-gather.3.cloned.1.call-done, bf16[128,64]{0,1:T(8,128)(2,1)S(1)} %convolution_convert_fusion, f32[128]{0:T(128)S(1)} %get-tuple-element.16, f32[128,8192]{1,0:T(8,128)} %copy-done.1, f32[128]{0:T(128)S(1)} %log_add_fusion, s32[8192]{0:T(1024)S(1)} %add_bitcast_fusion, ...), kind=kOutput, calls=%fused_computation.33 | convolution fusion | flops 276840448 | bytes 8455680 | tf_op jit(solution)/shard_map/hqk,khd->qhd/dot_general | solution.py:85
  205.4 0.1 fusion.35
  205.5 42.4 %all-gather.5.cloned.1.call-done = bf16[8192,2,64]{0,2,1:T(8,128)(2,1)} async-done(((bf16[128,2,64]{0,2,1:T(8,128)(2,1)}), bf16[8192,2,64]{0,2,1:T(8,128)(2,1)}) %all-gather.5.cloned.1.call-update) | async-done | bytes 2097168 | tf_op jit(solution)/shard_map/all_gather | solution.py:40
  247.9 0.0 copy-done.3
  247.9 0.0 copy-start.2
  247.9 4.4 %fusion.5 = bf16[8192,128]{1,0:T(8,128)(2,1)S(1)} fusion(f32[8192]{0:T(1024)S(1)} %bitcast.109, s32[128]{0:T(128)} %copy-done.5, s32[8192]{0:T(1024)S(1)} %add_bitcast_fusion, bf16[8192,2,64]{0,2,1:T(8,128)(2,1)} %all-gather.5.cloned.1.call-done, bf16[128,1,128]{2,0,1:T(8,128)(2,1)S(1)} %copy-done.3), kind=kOutput, calls=%fused_computation.9 | convolution fusion | flops 139460608 | bytes 3244544 | tf_op jit(solution)/shard_map/qhd,khd->hqk/dot_general | solution.py:93
  252.3 0.0 copy-done.2
  252.3 0.5 fusion.19
  252.8 3.5 %fusion.20 = bf16[128,1,64]{0,2,1:T(8,128)(2,1)S(1)} fusion(bf16[8192,128]{1,0:T(8,128)(2,1)S(1)} %fusion.5, f32[8192]{0:T(1024)S(1)} %bitcast.108, bf16[8192,2,64]{0,2,1:T(8,128)(2,1)} %all-gather.5.cloned.1.call-done, bf16[128,1,128]{2,0,1:T(8,128)(2,1)S(1)} %copy-done.3), kind=kOutput, calls=%fused_computation.32 | convolution fusion | flops 272646144 | bytes 4276224 | tf_op jit(solution)/shard_map/hqk,qhd->khd/dot_general | solution.py:106
  256.3 0.7 copy.15
  257.1 0.0 all-to-all-done
  257.1 1.9 fusion.13
  (5 shorter events, 0.0 us)
Async XLA Ops:
  7.2 60.7 %copy-start = (bf16[128,4096]{1,0:T(8,128)(2,1)S(1)}, bf16[128,4096]{1,0:T(8,128)(2,1)}, u32[]{:S(2)}) copy-start(bf16[128,4096]{1,0:T(8,128)(2,1)} %param.8) | copy-start | bytes 3145732
  7.2 97.6 %all-gather.3.cloned.1.call-start = ((), (), s32[]{:S(2)}) async-start(), calls=%async_computation.2 | async-start | bytes 2228224 | tf_op jit(solution)/shard_map/all_gather | solution.py:15
  36.4 32.9 %copy-start.4 = (bf16[128,1,64]{0,2,1:T(8,128)(2,1)S(1)}, bf16[128,1,64]{0,2,1:T(8,128)(2,1)}, u32[]{:S(2)}) copy-start(bf16[128,1,64]{0,2,1:T(8,128)(2,1)} %param.5) | copy-start | bytes 49156
  36.4 33.6 %copy-start.7 = (s32[64]{0:T(128)S(1)}, s32[64]{0:T(128)}, u32[]{:S(2)}) copy-start(s32[64]{0:T(128)} %param.9) | copy-start | bytes 772
  63.3 20.2 %all-to-all-start.1 = ((bf16[16,2,8192]{2,1,0:T(2,128)(2,1)}), bf16[16,2,8192]{2,1,0:T(2,128)(2,1)}, u32[]{:S(2)}, u32[]{:S(2)}) async-start(bf16[16,2,8192]{2,1,0:T(2,128)(2,1)} %reshape.219), calls=%async_computation.1 | async-start | bytes 1048576 | tf_op jit(solution)/shard_map/all_to_all | solution.py:74
  67.6 180.3 %all-gather.5.cloned.1.call-start = ((), (), s32[]{:S(2)}) async-start(), calls=%async_computation.3 | async-start | bytes 2129920 | tf_op jit(solution)/shard_map/all_gather | solution.py:40
  71.4 127.6 %copy-start.5 = (s32[128]{0:T(128)}, s32[128]{0:T(128)S(1)}, u32[]{:S(2)}) copy-start(s32[128]{0:T(128)S(1)} %iota_add_fusion) | copy-start | bytes 1540
  104.7 3.8 %copy-start.6 = (bf16[8192,1,128]{2,0,1:T(8,128)(2,1)S(1)}, bf16[8192,1,128]{2,0,1:T(8,128)(2,1)}, u32[]{:S(2)}) copy-start(bf16[8192,1,128]{2,0,1:T(8,128)(2,1)} %all-gather.3.cloned.1.call-done) | copy-start | bytes 6291460
  107.5 3.1 %copy-start.1 = (f32[128,8192]{1,0:T(8,128)}, f32[128,8192]{1,0:T(8,128)S(1)}, u32[]{:S(2)}) copy-start(f32[128,8192]{1,0:T(8,128)S(1)} %get-tuple-element.15) | copy-start | bytes 12582916
  111.4 145.7 %all-to-all-start = ((bf16[16,128,1,64]{1,3,2,0:T(8,128)(2,1)}), bf16[16,128,1,64]{1,3,2,0:T(8,128)(2,1)S(1)}, u32[]{:S(2)}, u32[]{:S(2)}) async-start(bf16[16,128,1,64]{1,3,2,0:T(8,128)(2,1)} %broadcast_in_dim.14), calls=%async_computation | async-start | bytes 524288 | tf_op jit(solution)/shard_map/all_to_all | solution.py:21
  198.9 49.0 %copy-start.3 = (bf16[128,1,128]{2,0,1:T(8,128)(2,1)S(1)}, bf16[128,1,128]{2,0,1:T(8,128)(2,1)}, u32[]{:S(2)}) copy-start(bf16[128,1,128]{2,0,1:T(8,128)(2,1)} %param.6) | copy-start | bytes 98308
  247.9 4.4 %copy-start.2 = (bf16[8192,2,64]{0,2,1:T(8,128)(2,1)S(1)}, bf16[8192,2,64]{0,2,1:T(8,128)(2,1)}, u32[]{:S(2)}) copy-start(bf16[8192,2,64]{0,2,1:T(8,128)(2,1)} %all-gather.5.cloned.1.call-done) | copy-start | bytes 6291460
Sparse Core Ops, SparseCore 0:
  31.7 73.0 all-gather.2
  109.4 138.4 all-gather.4
where the time goes:
time: 267 us; the launch traced here: 266 us
  blocking collectives  105 us (39%)
  waiting for transfers between devices  68.1 us (26%)
  other arithmetic  25.1 us (9%)
  matrix products  23.2 us (9%)
  local copies, waits for them, and re-layouts  18.2 us (7%)
  between operations  14.9 us (6%)
  starting transfers between devices  11.4 us (4%)
    all_gather x1, blocking collectives, side_by_side(): out = lax.all_gather(both, axis, axis=dim, tiled=True)  80.7 us
    all_gather x1, waiting for transfers between devices, side_by_side(): out = lax.all_gather(both, axis, axis=dim, tiled=True)  42.4 us
    all_gather x1, blocking collectives, gather_axes(): out = lax.all_gather(out, axes[number], axis=dim, tiled=True)  24.3 us
    unnamed x1, other arithmetic  23.4 us
    unnamed x22, local copies, waits for them, and re-layouts  14.4 us
    all_gather x1, waiting for transfers between devices, gather_axes(): out = lax.all_gather(out, axes[number], axis=dim, tiled=True)  13.6 us
    all_to_all x1, waiting for transfers between devices, local(): lax.all_to_all(out_weight, 'head', split_axis=2, concat_axis=0, tiled=True)  12.2 us
    all_to_all x1, starting transfers between devices, copy_for_each(): lax.all_to_all(jnp.broadcast_to(value[None], (peers, *value.shape)), axis...  6.85 us
  transfers between devices with their start and end apart: 4, of which 3 were waited for; matrix products, arithmetic and copies ran while one was open for 24% of the time, Pallas kernels for 0%

commit v1 on v0

v1 whole, which is shorter than its diff:
```python
import jax
import jax.numpy as jnp
from jax import lax
from jax.experimental import pallas as pl
from jax.experimental.pallas import tpu as pltpu
from jax.sharding import Mesh
from jax.sharding import PartitionSpec as P

GROUP = 8
SEQ = ("b", "a")
TOK = 128
HD = 64
ROWS = GROUP * TOK
STATS = 3 * GROUP
OUT_ROWS = HD + STATS
NEG = -1e30
INTERPRET = False
F32 = jnp.float32
BF16 = jnp.bfloat16


def nt(x, y):
    return lax.dot_general(x, y, (((1,), (1,)), ((), ())), preferred_element_type=F32)


def nn(x, y):
    return lax.dot_general(x, y, (((1,), (0,)), ((), ())), preferred_element_type=F32)


def lanes_below(x, flip=False):
    lane = lax.broadcasted_iota(jnp.int32, x.shape, x.ndim - 1)
    keep = lane >= HD if flip else lane < HD
    return jnp.where(keep, x, jnp.zeros_like(x))


def key_minus_query():
    key = lax.broadcasted_iota(jnp.int32, (TOK, TOK), 0)
    query = lax.broadcasted_iota(jnp.int32, (TOK, TOK), 1)
    return key - query


def forward_tile(order, place, qg_ref, kv_ref, out_ref, keys, values_t, stats):
    b, a = place[0], place[1]
    kv = kv_ref[...].reshape(ROWS, 2 * HD)
    keys[...] = lanes_below(kv)
    values_t[0:HD, :] = jnp.transpose(kv.astype(F32))[HD:, :].astype(BF16)
    values_t[HD:, :] = jnp.ones((16, ROWS), BF16)
    diff = key_minus_query()

    def step(i, carry):
        qg = qg_ref[i]
        scores = nt(keys[...], qg)
        query_block = order[b * GROUP + i]
        masked = []
        for j in range(GROUP):
            limit = (query_block - order[j * GROUP + a]) * TOK
            masked.append(jnp.where(diff <= limit, scores[j * TOK : (j + 1) * TOK], NEG))
        masked = jnp.concatenate(masked, axis=0)
        top = jnp.max(masked, axis=0, keepdims=True)
        probs = jnp.exp(masked - top).astype(BF16)
        summed = nn(values_t[...], probs)
        grad_t = jnp.transpose(qg.astype(F32))[HD:, :]
        part = summed[0:HD]
        out_ref[i, 0:HD, :] = part
        stats[pl.ds(i, 1), :] = top
        stats[pl.ds(GROUP + i, 1), :] = summed[HD : HD + 1]
        stats[pl.ds(2 * GROUP + i, 1), :] = jnp.sum(grad_t * part, axis=0, keepdims=True)
        return carry

    lax.fori_loop(0, GROUP, step, 0)
    for i in range(GROUP):
        out_ref[i, HD:, :] = stats[...]


def total_stats(parts_ref):
    top = parts_ref[0, HD : HD + GROUP, :]
    for p in range(1, GROUP):
        top = jnp.maximum(top, parts_ref[p, HD : HD + GROUP, :])
    total = jnp.zeros((GROUP, TOK), F32)
    dot = jnp.zeros((GROUP, TOK), F32)
    for p in range(GROUP):
        weight = jnp.exp(parts_ref[p, HD : HD + GROUP, :] - top)
        total += weight * parts_ref[p, HD + GROUP : HD + 2 * GROUP, :]
        dot += weight * parts_ref[p, HD + 2 * GROUP :, :]
    return top, total, dot / total


def join_parts(place, parts_ref, out_ref, tops, totals):
    a = place[1]
    top, total, _ = total_stats(parts_ref)
    tops[...] = top
    totals[...] = total
    own_top = tops[pl.ds(a, 1), :]
    own_total = totals[pl.ds(a, 1), :]
    acc = jnp.zeros((HD, TOK), F32)
    for p in range(GROUP):
        weight = jnp.exp(parts_ref[p, pl.ds(HD + a, 1), :] - own_top)
        acc += weight * parts_ref[p, 0:HD, :]
    out = (acc / own_total).astype(BF16)
    for h in range(out_ref.shape[0]):
        out_ref[h] = out


def backward_tile(
    order, place, qg_ref, kv_ref, parts_ref, dkv_ref, dq_ref, query_part, grad_part, dscores, norm_dot
):
    b, a = place[0], place[1]
    top, total, dot = total_stats(parts_ref)
    log_total = top + jnp.log(total)
    for i in range(GROUP):
        norm_dot[0:1, i * TOK : (i + 1) * TOK] = log_total[i : i + 1]
        norm_dot[1:2, i * TOK : (i + 1) * TOK] = dot[i : i + 1]
    qg = qg_ref[...].reshape(ROWS, 2 * HD)
    query_part[...] = lanes_below(qg)
    grad_part[...] = lanes_below(qg, True)
    diff = key_minus_query()

    def step(j, carry):
        kv = kv_ref[j]
        scores = nt(kv, query_part[...])
        dprob = nt(kv, grad_part[...])
        key_block = order[j * GROUP + a]
        logs = norm_dot[0:1, :]
        dots = norm_dot[1:2, :]
        allowed = jnp.concatenate(
            [diff <= (order[b * GROUP + i] - key_block) * TOK for i in range(GROUP)], axis=1
        )
        probs = jnp.where(allowed, jnp.exp(scores - logs), 0.0).astype(BF16)
        dscore = (probs.astype(F32) * (dprob - dots)).astype(BF16)
        dscores[pl.ds(pl.multiple_of(j * TOK, TOK), TOK), :] = dscore
        dkv = nn(dscore, query_part[...]) + nn(probs, grad_part[...])
        dkv_ref[j] = dkv.astype(BF16)
        return carry

    lax.fori_loop(0, GROUP, step, 0)
    keys_t = jnp.transpose(kv_ref[...].reshape(ROWS, 2 * HD).astype(F32))[0:HD, :].astype(BF16)
    dq = nn(keys_t, dscores[...]) * (HD**-0.5)
    for i in range(GROUP):
        dq_ref[i] = dq[:, i * TOK : (i + 1) * TOK].astype(BF16)


def smem():
    return pl.BlockSpec(memory_space=pltpu.SMEM)


def vmem():
    return pl.BlockSpec(memory_space=pltpu.VMEM)


def copies_for(value, axis):
    return jnp.broadcast_to(value[None], (lax.axis_size(axis), *value.shape))


def exchange(value, axis):
    return lax.all_to_all(value, axis, 0, 0, tiled=True)


def local(queries, keys_values, out_weight, out_grad, block_order):
    heads = lax.axis_size("head")
    place = jnp.stack([lax.axis_index("b"), lax.axis_index("a")]).astype(jnp.int32)
    kv_group = exchange(copies_for(keys_values[:, 0], "b"), "b")
    weight = out_weight[0]
    columns = weight.shape[1] // heads
    grad_att = lax.dot_general(
        out_grad, weight, (((1,), (1,)), ((), ())), preferred_element_type=F32
    ).astype(BF16)
    scaled = queries[:, 0] * jnp.asarray(HD**-0.5, BF16)
    qg_group = exchange(copies_for(jnp.concatenate([scaled, grad_att], axis=1), "a"), "a")
    column_weight = exchange(
        jnp.transpose(weight.reshape(HD, heads, columns), (1, 0, 2)), "head"
    )
    parts = pl.pallas_call(
        forward_tile,
        out_shape=jax.ShapeDtypeStruct((GROUP, OUT_ROWS, TOK), F32),
        in_specs=[smem(), smem(), vmem(), vmem()],
        out_specs=vmem(),
        scratch_shapes=[
            pltpu.VMEM((ROWS, 2 * HD), BF16),
            pltpu.VMEM((HD + 16, ROWS), BF16),
            pltpu.VMEM((STATS, TOK), F32),
        ],
        interpret=INTERPRET,
        name="forward_tile",
    )(block_order, place, qg_group, kv_group)
    parts = exchange(parts, "a")
    attended = pl.pallas_call(
        join_parts,
        out_shape=jax.ShapeDtypeStruct((heads, HD, TOK), BF16),
        in_specs=[smem(), vmem()],
        out_specs=vmem(),
        scratch_shapes=[pltpu.VMEM((GROUP, TOK), F32), pltpu.VMEM((GROUP, TOK), F32)],
        interpret=INTERPRET,
        name="join_parts",
    )(place, parts)
    every_head = exchange(attended, "head")
    dkv, dq = pl.pallas_call(
        backward_tile,
        out_shape=(
            jax.ShapeDtypeStruct((GROUP, TOK, 2 * HD), BF16),
            jax.ShapeDtypeStruct((GROUP, HD, TOK), BF16),
        ),
        in_specs=[smem(), smem(), vmem(), vmem(), vmem()],
        out_specs=(vmem(), vmem()),
        scratch_shapes=[
            pltpu.VMEM((ROWS, 2 * HD), BF16),
            pltpu.VMEM((ROWS, 2 * HD), BF16),
            pltpu.VMEM((ROWS, ROWS), BF16),
            pltpu.VMEM((8, ROWS), F32),
        ],
        interpret=INTERPRET,
        name="backward_tile",
    )(block_order, place, qg_group, kv_group, parts)
    dkv = exchange(dkv, "b")
    dq = exchange(dq, "a")
    grad_keys_values = jnp.sum(dkv.astype(F32), axis=0).astype(BF16)[:, None]
    grad_queries = jnp.transpose(jnp.sum(dq.astype(F32), axis=0)).astype(BF16)[:, None]
    mixed_out = lax.dot_general(
        every_head.reshape(heads * HD, TOK),
        column_weight.reshape(heads * HD, columns),
        (((0,), (0,)), ((), ())),
        preferred_element_type=F32,
    ).astype(BF16)
    return (mixed_out, grad_queries, grad_keys_values)


def solution(mesh):
    finer = Mesh(mesh.devices.reshape(GROUP, GROUP, mesh.shape["head"]), ("b", "a", "head"))
    in_specs = (
        P(SEQ, "head", None),
        P(SEQ, "head", None),
        P("head", None, None),
        P(SEQ, None),
        P(),
    )
    out_specs = (P(SEQ, "head"), P(SEQ, "head", None), P(SEQ, "head", None))
    return jax.shard_map(local, mesh=finer, in_specs=in_specs, out_specs=out_specs, check_vma=False)
```

time: 267 us -> 150 us (0.56)
  the two profiles are of different devices: /device:TPU:6 before, /device:TPU:1 now
where the time goes in v1:
time: 150 us; the launch traced here: 149 us
  waiting for transfers between devices  56.7 us (38%)
  starting transfers between devices  40.5 us (27%)
  blocking collectives  28.3 us (19%)
  Pallas kernels  14.3 us (10%)
  local copies, waits for them, and re-layouts  3.86 us (3%)
  other arithmetic  2.68 us (2%)
  matrix products  2.42 us (2%)
    all_to_all x5, waiting for transfers between devices, exchange(): return lax.all_to_all(value, axis, 0, 0, tiled=True)  56.7 us
    all_to_all x5, starting transfers between devices, exchange(): return lax.all_to_all(value, axis, 0, 0, tiled=True)  40.5 us
    all_to_all x2, blocking collectives, exchange(): return lax.all_to_all(value, axis, 0, 0, tiled=True)  28.3 us
    pallas_call x1, Pallas kernels, local(): pl.pallas_call(backward_tile, out_shape=(jax.ShapeDtypeStruct((GROUP, TOK...  6.34 us
    pallas_call x1, Pallas kernels, local(): pl.pallas_call(forward_tile, out_shape=jax.ShapeDtypeStruct((GROUP, OUT_R...  6.21 us
  transfers between devices with their start and end apart: 5, of which 5 were waited for; matrix products, arithmetic and copies ran while one was open for 2% of the time, Pallas kernels for 5%

profile of v1, /device:TPU:1, one launch (start us, length us, event | category | flops | bytes accessed | tf_op | source)
XLA Modules:
  0.0 149.5 jit_solution(10716650376252189667)
XLA Ops:
  0.6 0.0 copy-start
  0.6 0.8 multiply_bitcast_fusion
  1.5 0.4 copy-done
  1.9 1.5 %convolution_convert_fusion = bf16[128,64]{0,1:T(8,128)(2,1)S(1)} fusion(bf16[128,4096]{1,0:T(8,128)(2,1)S(1)} %copy-done, bf16[1,64,4096]{2,1,0:T(8,128)(2,1)} %param.7), kind=kOutput, calls=%fused_computation.2 | convolution fusion | flops 67117056 | bytes 1589248 | tf_op jit(solution)/shard_map/dot_general | solution.py:164
  3.4 0.1 copy.9
  3.6 0.0 copy-start.4
  3.6 12.6 %all_to_all.35.qg_ref = bf16[8,128,128]{2,1,0:T(8,128)(2,1)} all-to-all(bf16[8,128,128]{2,1,0:T(8,128)(2,1)S(1)} %broadcast_in_dim.19), channel_id=1, replica_groups=mesh['b'=8,'a'=8,'head'=16] {'a'}, dimensions={0} | all-to-all | bytes 524288 | tf_op jit(solution)/shard_map/all_to_all | solution.py:155
  16.2 0.0 copy-done.4
  16.2 0.7 broadcast_in_dim.21
  17.0 17.6 %all-to-all-start.1 = ((bf16[8,128,128]{2,1,0:T(8,128)(2,1)}), bf16[8,128,128]{2,1,0:T(8,128)(2,1)S(1)}, u32[]{:S(2)}, u32[]{:S(2)}) async-start(bf16[8,128,128]{2,1,0:T(8,128)(2,1)} %broadcast_in_dim.21), calls=%async_computation.1 | async-start | bytes 524288 | tf_op jit(solution)/shard_map/all_to_all | solution.py:155
  34.6 0.6 pad_add_fusion.place
  35.1 17.1 %all-to-all-done.1.kv_ref = bf16[8,128,128]{2,1,0:T(8,128)(2,1)S(1)} async-done(((bf16[8,128,128]{2,1,0:T(8,128)(2,1)}), bf16[8,128,128]{2,1,0:T(8,128)(2,1)S(1)}, u32[]{:S(2)}, u32[]{:S(2)}) %all-to-all-start.1) | async-done | bytes 262176 | tf_op jit(solution)/shard_map/all_to_all | solution.py:155
  52.2 0.0 copy-start.2
  52.2 0.7 copy-done.2
  52.9 6.2 %forward_tile.1 = f32[8,88,128]{2,1,0:T(8,128)} custom-call(s32[64]{0:T(128)} %order.3, s32[2]{0:T(128)} %pad_add_fusion.place, bf16[8,128,128]{2,1,0:T(8,128)(2,1)} %all_to_all.35.qg_ref, bf16[8,128,128]{2,1,0:T(8,128)(2,1)} %copy-done.2), custom_call_target="tpu_custom_call" | custom-call | tf_op jit(solution)/shard_map/forward_tile/pallas_call | solution.py:172
  59.2 0.0 copy-start.3
  59.2 3.6 %all-to-all-start.2 = ((f32[8,88,128]{2,1,0:T(8,128)}), f32[8,88,128]{2,1,0:T(8,128)S(1)}, u32[]{:S(2)}, u32[]{:S(2)}) async-start(f32[8,88,128]{2,1,0:T(8,128)} %forward_tile.1), calls=%async_computation.2 | async-start | bytes 720896 | tf_op jit(solution)/shard_map/all_to_all | solution.py:155
  62.7 0.0 copy-done.3
  62.7 0.1 copy.11
  62.9 1.0 copy.13
  63.8 5.3 %all-to-all-done.2.parts_ref = f32[8,88,128]{2,1,0:T(8,128)S(1)} async-done(((f32[8,88,128]{2,1,0:T(8,128)}), f32[8,88,128]{2,1,0:T(8,128)S(1)}, u32[]{:S(2)}, u32[]{:S(2)}) %all-to-all-start.2) | async-done | bytes 360480 | tf_op jit(solution)/shard_map/all_to_all | solution.py:155
  69.1 0.0 copy-start.1
  69.1 0.7 copy-done.1
  69.9 12.5 %all-to-all-start.4 = ((bf16[16,64,256]{2,1,0:T(8,128)(2,1)}), bf16[16,64,256]{2,1,0:T(8,128)(2,1)S(1)}, u32[]{:S(2)}, u32[]{:S(2)}) async-start(bf16[16,64,256]{2,1,0:T(8,128)(2,1)} %bitcast.24), calls=%async_computation.4 | async-start | bytes 1048576 | tf_op jit(solution)/shard_map/all_to_all | solution.py:155
  82.4 6.3 %backward_tile.1 = (bf16[8,128,128]{2,1,0:T(8,128)(2,1)}, bf16[8,64,128]{2,1,0:T(8,128)(2,1)}) custom-call(s32[64]{0:T(128)} %order.3, s32[2]{0:T(128)} %pad_add_fusion.place, bf16[8,128,128]{2,1,0:T(8,128)(2,1)} %all_to_all.35.qg_ref, bf16[8,128,128]{2,1,0:T(8,128)(2,1)} %copy-done.2, f32[8,88,128]{2,1,0:T(8,128)} %copy-done.1), custom_call_target="tpu_custom_call" | custom-call | tf_op jit(solution)/shard_map/backward_tile/pallas_call | solution.py:196
  88.8 10.9 %all-to-all-done.4 = bf16[16,64,256]{2,1,0:T(8,128)(2,1)S(1)} async-done(((bf16[16,64,256]{2,1,0:T(8,128)(2,1)}), bf16[16,64,256]{2,1,0:T(8,128)(2,1)S(1)}, u32[]{:S(2)}, u32[]{:S(2)}) %all-to-all-start.4) | async-done | bytes 524320 | tf_op jit(solution)/shard_map/all_to_all | solution.py:155
  99.6 3.4 %all-to-all-start.5 = ((bf16[8,64,128]{2,1,0:T(8,128)(2,1)}), bf16[8,64,128]{2,1,0:T(8,128)(2,1)S(1)}, u32[]{:S(2)}, u32[]{:S(2)}) async-start(bf16[8,64,128]{2,1,0:T(8,128)(2,1)} %get-tuple-element.5), calls=%async_computation.5 | async-start | bytes 262144 | tf_op jit(solution)/shard_map/all_to_all | solution.py:155
  103.0 1.8 %join_parts.1 = bf16[16,64,128]{2,1,0:T(8,128)(2,1)} custom-call(s32[2]{0:T(128)} %pad_add_fusion.place, f32[8,88,128]{2,1,0:T(8,128)} %copy-done.1), custom_call_target="tpu_custom_call" | custom-call | tf_op jit(solution)/shard_map/join_parts/pallas_call | solution.py:186
  104.8 3.6 %all-to-all-done.5 = bf16[8,64,128]{2,1,0:T(8,128)(2,1)S(1)} async-done(((bf16[8,64,128]{2,1,0:T(8,128)(2,1)}), bf16[8,64,128]{2,1,0:T(8,128)(2,1)S(1)}, u32[]{:S(2)}, u32[]{:S(2)}) %all-to-all-start.5) | async-done | bytes 131104 | tf_op jit(solution)/shard_map/all_to_all | solution.py:155
  108.4 15.7 %all_to_all.36 = bf16[16,64,128]{2,1,0:T(8,128)(2,1)S(1)} all-to-all(bf16[16,64,128]{2,1,0:T(8,128)(2,1)} %join_parts.1), channel_id=1, replica_groups=mesh['b'=8,'a'=8,'head'=16] {'head'}, dimensions={0} | all-to-all | bytes 524288 | tf_op jit(solution)/shard_map/all_to_all | solution.py:155
  124.1 3.4 %all-to-all-start.6 = ((bf16[8,128,128]{2,1,0:T(8,128)(2,1)}), bf16[8,128,128]{2,1,0:T(8,128)(2,1)S(1)}, u32[]{:S(2)}, u32[]{:S(2)}) async-start(bf16[8,128,128]{2,1,0:T(8,128)(2,1)} %get-tuple-element.6), calls=%async_computation.6 | async-start | bytes 524288 | tf_op jit(solution)/shard_map/all_to_all | solution.py:155
  127.5 0.6 reduce_sum.24
  128.1 0.9 fusion
  129.0 19.8 %all-to-all-done.6 = bf16[8,128,128]{2,1,0:T(8,128)(2,1)S(1)} async-done(((bf16[8,128,128]{2,1,0:T(8,128)(2,1)}), bf16[8,128,128]{2,1,0:T(8,128)(2,1)S(1)}, u32[]{:S(2)}, u32[]{:S(2)}) %all-to-all-start.6) | async-done | bytes 262176 | tf_op jit(solution)/shard_map/all_to_all | solution.py:155
  148.8 0.7 reduce_sum.25
  (2 shorter events, 0.0 us)
Async XLA Ops:
  0.6 1.2 copy-start
  3.6 12.6 %copy-start.4 = (bf16[128,1,128]{2,0,1:T(8,128)(2,1)S(1)}, bf16[128,1,128]{2,0,1:T(8,128)(2,1)}, u32[]{:S(2)}) copy-start(bf16[128,1,128]{2,0,1:T(8,128)(2,1)} %param.6) | copy-start | bytes 98308
  17.0 35.2 %all-to-all-start.1 = ((bf16[8,128,128]{2,1,0:T(8,128)(2,1)}), bf16[8,128,128]{2,1,0:T(8,128)(2,1)S(1)}, u32[]{:S(2)}, u32[]{:S(2)}) async-start(bf16[8,128,128]{2,1,0:T(8,128)(2,1)} %broadcast_in_dim.21), calls=%async_computation.1 | async-start | bytes 524288 | tf_op jit(solution)/shard_map/all_to_all | solution.py:155
  52.2 0.7 copy-start.2
  59.2 3.6 %copy-start.3 = (bf16[1,64,4096]{2,1,0:T(8,128)(2,1)S(1)}, bf16[1,64,4096]{2,1,0:T(8,128)(2,1)}, u32[]{:S(2)}) copy-start(bf16[1,64,4096]{2,1,0:T(8,128)(2,1)} %param.7) | copy-start | bytes 1572868
  59.2 10.0 %all-to-all-start.2 = ((f32[8,88,128]{2,1,0:T(8,128)}), f32[8,88,128]{2,1,0:T(8,128)S(1)}, u32[]{:S(2)}, u32[]{:S(2)}) async-start(f32[8,88,128]{2,1,0:T(8,128)} %forward_tile.1), calls=%async_computation.2 | async-start | bytes 720896 | tf_op jit(solution)/shard_map/all_to_all | solution.py:155
  69.1 0.7 copy-start.1
  69.9 29.7 %all-to-all-start.4 = ((bf16[16,64,256]{2,1,0:T(8,128)(2,1)}), bf16[16,64,256]{2,1,0:T(8,128)(2,1)S(1)}, u32[]{:S(2)}, u32[]{:S(2)}) async-start(bf16[16,64,256]{2,1,0:T(8,128)(2,1)} %bitcast.24), calls=%async_computation.4 | async-start | bytes 1048576 | tf_op jit(solution)/shard_map/all_to_all | solution.py:155
  99.6 8.7 %all-to-all-start.5 = ((bf16[8,64,128]{2,1,0:T(8,128)(2,1)}), bf16[8,64,128]{2,1,0:T(8,128)(2,1)S(1)}, u32[]{:S(2)}, u32[]{:S(2)}) async-start(bf16[8,64,128]{2,1,0:T(8,128)(2,1)} %get-tuple-element.5), calls=%async_computation.5 | async-start | bytes 262144 | tf_op jit(solution)/shard_map/all_to_all | solution.py:155
  124.1 24.8 %all-to-all-start.6 = ((bf16[8,128,128]{2,1,0:T(8,128)(2,1)}), bf16[8,128,128]{2,1,0:T(8,128)(2,1)S(1)}, u32[]{:S(2)}, u32[]{:S(2)}) async-start(bf16[8,128,128]{2,1,0:T(8,128)(2,1)} %get-tuple-element.6), calls=%async_computation.6 | async-start | bytes 524288 | tf_op jit(solution)/shard_map/all_to_all | solution.py:155

commit v2 on v1

--- a/solution.py
+++ b/solution.py
@@ -7,14 +7,17 @@
 from jax.sharding import PartitionSpec as P
 
 GROUP = 8
-SEQ = ("b", "a")
+SEQ = ("b", "zl", "x")
 TOK = 128
 HD = 64
 ROWS = GROUP * TOK
 STATS = 3 * GROUP
+QUARTERS = 4
+A = ("zl", "x")
 OUT_ROWS = HD + STATS
 NEG = -1e30
 INTERPRET = False
+PARAMS = pltpu.CompilerParams(vmem_limit_bytes=24 * 1024 * 1024)
 F32 = jnp.float32
 BF16 = jnp.bfloat16
 
@@ -85,8 +88,15 @@
     return top, total, dot / total
 
 
-def join_parts(place, parts_ref, out_ref, tops, totals):
-    a = place[1]
+def prepare(queries_ref, weight_ref, grad_ref, out_ref):
+    grad_att = nt(grad_ref[...], weight_ref[...]).astype(BF16)
+    scaled = queries_ref[...] * jnp.asarray(HD**-0.5, BF16)
+    out_ref[...] = jnp.concatenate([scaled, grad_att], axis=1)
+
+
+def join_parts(place, parts_ref, weight_ref, out_ref, tops, totals):
+    a, quarter = place[1], place[2]
+    rows = HD // QUARTERS
     top, total, _ = total_stats(parts_ref)
     tops[...] = top
     totals[...] = total
@@ -98,7 +108,29 @@
         acc += weight * parts_ref[p, 0:HD, :]
     out = (acc / own_total).astype(BF16)
     for h in range(out_ref.shape[0]):
-        out_ref[h] = out
+        out_ref[h, 0:HD, :] = out
+    own_rows = weight_ref[pl.ds(pl.multiple_of(quarter * rows, rows), rows), :]
+    for h in range(out_ref.shape[0]):
+        for half in range(2):
+            first = HD + half * rows
+            column = (2 * h + half) * TOK
+            out_ref[h, first : first + rows, :] = own_rows[:, column : column + TOK]
+
+
+def mix(parts_ref, weight_ref, out_ref, side):
+    heads = parts_ref.shape[0]
+    rows = HD // QUARTERS
+    for h in range(heads):
+        for quarter in range(QUARTERS):
+            first = h * HD + quarter * rows
+            for half in range(2):
+                side[first : first + rows, half * TOK : (half + 1) * TOK] = weight_ref[
+                    quarter, h, half * rows : (half + 1) * rows, :
+                ]
+    attended = parts_ref[:, 0:HD, :].reshape(heads * HD, TOK)
+    out_ref[...] = lax.dot_general(
+        attended, side[...], (((0,), (0,)), ((), ())), preferred_element_type=F32
+    ).astype(BF16)
 
 
 def backward_tile(
@@ -157,18 +189,23 @@
 
 def local(queries, keys_values, out_weight, out_grad, block_order):
     heads = lax.axis_size("head")
-    place = jnp.stack([lax.axis_index("b"), lax.axis_index("a")]).astype(jnp.int32)
+    place = jnp.stack(
+        [lax.axis_index("b"), lax.axis_index(A), lax.axis_index("x")]
+    ).astype(jnp.int32)
     kv_group = exchange(copies_for(keys_values[:, 0], "b"), "b")
     weight = out_weight[0]
     columns = weight.shape[1] // heads
-    grad_att = lax.dot_general(
-        out_grad, weight, (((1,), (1,)), ((), ())), preferred_element_type=F32
-    ).astype(BF16)
-    scaled = queries[:, 0] * jnp.asarray(HD**-0.5, BF16)
-    qg_group = exchange(copies_for(jnp.concatenate([scaled, grad_att], axis=1), "a"), "a")
-    column_weight = exchange(
-        jnp.transpose(weight.reshape(HD, heads, columns), (1, 0, 2)), "head"
-    )
+    query_grad = pl.pallas_call(
+        prepare,
+        out_shape=jax.ShapeDtypeStruct((TOK, 2 * HD), BF16),
+        in_specs=[vmem(), vmem(), vmem()],
+        out_specs=vmem(),
+        interpret=INTERPRET,
+        compiler_params=PARAMS,
+        name="prepare",
+    )(queries[:, 0], weight, out_grad)
+    qg_group = lax.all_gather(lax.all_gather(query_grad, "x"), "zl")
+    qg_group = qg_group.reshape(GROUP, TOK, 2 * HD)
     parts = pl.pallas_call(
         forward_tile,
         out_shape=jax.ShapeDtypeStruct((GROUP, OUT_ROWS, TOK), F32),
@@ -180,19 +217,32 @@
             pltpu.VMEM((STATS, TOK), F32),
         ],
         interpret=INTERPRET,
+        compiler_params=PARAMS,
         name="forward_tile",
     )(block_order, place, qg_group, kv_group)
-    parts = exchange(parts, "a")
-    attended = pl.pallas_call(
+    parts = exchange(parts, A)
+    mixed_parts = pl.pallas_call(
         join_parts,
-        out_shape=jax.ShapeDtypeStruct((heads, HD, TOK), BF16),
-        in_specs=[smem(), vmem()],
+        out_shape=jax.ShapeDtypeStruct((heads, HD + HD // QUARTERS * 2, TOK), BF16),
+        in_specs=[smem(), vmem(), vmem()],
         out_specs=vmem(),
         scratch_shapes=[pltpu.VMEM((GROUP, TOK), F32), pltpu.VMEM((GROUP, TOK), F32)],
         interpret=INTERPRET,
+        compiler_params=PARAMS,
         name="join_parts",
-    )(place, parts)
-    every_head = exchange(attended, "head")
+    )(place, parts, weight)
+    mixed_parts = exchange(mixed_parts, "head")
+    quarters = lax.all_gather(mixed_parts[:, HD:], "x")
+    mixed_out = pl.pallas_call(
+        mix,
+        out_shape=jax.ShapeDtypeStruct((TOK, columns), BF16),
+        in_specs=[vmem(), vmem()],
+        out_specs=vmem(),
+        scratch_shapes=[pltpu.VMEM((heads * HD, columns), BF16)],
+        interpret=INTERPRET,
+        compiler_params=PARAMS,
+        name="mix",
+    )(mixed_parts, quarters)
     dkv, dq = pl.pallas_call(
         backward_tile,
         out_shape=(
@@ -208,23 +258,18 @@
             pltpu.VMEM((8, ROWS), F32),
         ],
         interpret=INTERPRET,
+        compiler_params=PARAMS,
         name="backward_tile",
     )(block_order, place, qg_group, kv_group, parts)
     dkv = exchange(dkv, "b")
-    dq = exchange(dq, "a")
+    dq = exchange(dq, A)
     grad_keys_values = jnp.sum(dkv.astype(F32), axis=0).astype(BF16)[:, None]
     grad_queries = jnp.transpose(jnp.sum(dq.astype(F32), axis=0)).astype(BF16)[:, None]
-    mixed_out = lax.dot_general(
-        every_head.reshape(heads * HD, TOK),
-        column_weight.reshape(heads * HD, columns),
-        (((0,), (0,)), ((), ())),
-        preferred_element_type=F32,
-    ).astype(BF16)
     return (mixed_out, grad_queries, grad_keys_values)
 
 
 def solution(mesh):
-    finer = Mesh(mesh.devices.reshape(GROUP, GROUP, mesh.shape["head"]), ("b", "a", "head"))
+    finer = Mesh(mesh.devices.reshape(GROUP, 2, 4, mesh.shape["head"]), (*SEQ, "head"))
     in_specs = (
         P(SEQ, "head", None),
         P(SEQ, "head", None),

time: 150 us -> 132 us (0.88)
  waiting for transfers between devices: 56.7 us -> 12.8 us
  blocking collectives: 28.3 us -> 65.4 us
  starting transfers between devices: 40.5 us -> 34.4 us
  matrix products: 2.42 us -> 0 us
  Pallas kernels: 14.3 us -> 12.7 us
    all_to_all x5 -> x3, waiting for transfers between devices: 56.7 us -> 12.8 us  [exchange(): return lax.all_to_all(value, axis, 0, 0, tiled=True)]
    all_gather x0 -> x3, blocking collectives: none -> 26.7 us  [the longest x2 15.1 us: local(): qg_group = lax.all_gather(lax.all_gather(query_grad, 'x'), 'zl')]
    all_to_all x2, blocking collectives: 28.3 us -> 38.6 us  [exchange(): return lax.all_to_all(value, axis, 0, 0, tiled=True)]
    all_to_all x5 -> x3, starting transfers between devices: 40.5 us -> 34.4 us  [exchange(): return lax.all_to_all(value, axis, 0, 0, tiled=True)]
    dot_general x2 -> x0, matrix products: 2.42 us -> none  [the longest x1 1.52 us: local(): lax.dot_general(out_grad, weight, (((1,), (1,)), ((), ())), preferred_ele...]
  transfers between devices with their start and end apart: 5 -> 3, of which waited for: 5 -> 2; matrix products, arithmetic and copies ran while one was open for 2% -> 1% of each run, Pallas kernels for 5% -> 2%
where the time goes in v2:
time: 132 us; the launch traced here: 131 us
  blocking collectives  65.4 us (50%)
  starting transfers between devices  34.4 us (26%)
  waiting for transfers between devices  12.8 us (10%)
  Pallas kernels  12.7 us (10%)
  local copies, waits for them, and re-layouts  4.18 us (3%)
  other arithmetic  1.36 us (1%)
    all_to_all x2, blocking collectives, exchange(): return lax.all_to_all(value, axis, 0, 0, tiled=True)  38.6 us
    all_to_all x3, starting transfers between devices, exchange(): return lax.all_to_all(value, axis, 0, 0, tiled=True)  34.4 us
    all_gather x2, blocking collectives, local(): qg_group = lax.all_gather(lax.all_gather(query_grad, 'x'), 'zl')  15.1 us
    all_to_all x3, waiting for transfers between devices, exchange(): return lax.all_to_all(value, axis, 0, 0, tiled=True)  12.8 us
    all_gather x1, blocking collectives, local(): quarters = lax.all_gather(mixed_parts[:, HD:], 'x')  11.6 us
    pallas_call x1, Pallas kernels, local(): pl.pallas_call(backward_tile, out_shape=(jax.ShapeDtypeStruct((GROUP, TOK...  5.73 us
    pallas_call x1, Pallas kernels, local(): pl.pallas_call(forward_tile, out_shape=jax.ShapeDtypeStruct((GROUP, OUT_R...  4.94 us
  transfers between devices with their start and end apart: 3, of which 2 were waited for; matrix products, arithmetic and copies ran while one was open for 1% of the time, Pallas kernels for 2%

profile of v2, /device:TPU:1, one launch (start us, length us, event | category | flops | bytes accessed | tf_op | source)
XLA Modules:
  0.0 131.5 jit_solution(898139251300264678)
XLA Ops:
  0.6 0.0 copy-start
  0.6 1.5 %broadcast_in_dim.14 = bf16[8,128,128]{2,1,0:T(8,128)(2,1)} broadcast(bf16[128,128]{1,0:T(8,128)(2,1)} %bitcast.17), dimensions={1,2} | broadcast | bytes 294912 | tf_op jit(solution)/shard_map/broadcast_in_dim | solution.py:183
  2.2 19.3 %all-to-all-start = ((bf16[8,128,128]{2,1,0:T(8,128)(2,1)}), bf16[8,128,128]{2,1,0:T(8,128)(2,1)S(1)}, u32[]{:S(2)}, u32[]{:S(2)}) async-start(bf16[8,128,128]{2,1,0:T(8,128)(2,1)} %broadcast_in_dim.14), calls=%async_computation | async-start | bytes 524288 | tf_op jit(solution)/shard_map/all_to_all | solution.py:187
  21.5 0.0 copy-start.3
  21.5 0.7 copy-done.3
  22.2 0.1 copy.9
  22.3 0.0 copy-done
  22.3 0.0 copy-start.1
  22.3 1.2 copy-done.1
  23.6 0.5 prepare.1
  24.0 10.4 %all-gather = bf16[512,128]{1,0:T(8,128)(2,1)S(1)} all-gather(bf16[128,128]{1,0:T(8,128)(2,1)S(1)} %prepare.1), channel_id=2, replica_groups=mesh['b'=8,'zl'=2,'x'=4,'head'=16] {'x'}, dimensions={0}, use_global_device_ids=true | all-gather | bytes 163840 | tf_op jit(solution)/shard_map/all_gather | solution.py:207
  34.4 4.8 %all-gather.1.qg_ref = bf16[8,128,128]{2,1,0:T(8,128)(2,1)S(1)} all-gather(bf16[4,128,128]{2,1,0:T(8,128)(2,1)S(1)} %bitcast.16), channel_id=3, replica_groups=mesh['b'=8,'zl'=2,'x'=4,'head'=16] {'zl'}, dimensions={0}, use_global_device_ids=true | all-gather | bytes 393216 | tf_op jit(solution)/shard_map/all_gather | solution.py:207
  39.2 0.0 copy-start.2
  39.2 0.1 pad_add_fusion.place
  39.2 0.0 all-to-all-done.kv_ref
  39.2 0.6 copy-done.2
  39.8 4.9 %forward_tile.1 = f32[8,88,128]{2,1,0:T(8,128)S(1)} custom-call(s32[64]{0:T(128)S(1)} %copy-done.2, s32[3]{0:T(128)S(1)} %pad_add_fusion.place, bf16[8,128,128]{2,1,0:T(8,128)(2,1)S(1)} %all-gather.1.qg_ref, bf16[8,128,128]{2,1,0:T(8,128)(2,1)S(1)} %all-to-all-done.kv_ref), custom_call_target="tpu_custom_call" | custom-call | tf_op jit(solution)/shard_map/forward_tile/pallas_call | solution.py:209
  44.8 11.4 %all_to_all.25.parts_ref = f32[8,88,128]{2,1,0:T(8,128)S(1)} all-to-all(f32[8,88,128]{2,1,0:T(8,128)S(1)} %forward_tile.1), channel_id=1, replica_groups=mesh['b'=8,'zl'=2,'x'=4,'head'=16] {'zl','x'}, dimensions={0} | all-to-all | bytes 720896 | tf_op jit(solution)/shard_map/all_to_all | solution.py:187
  56.1 5.7 %backward_tile.1 = (bf16[8,128,128]{2,1,0:T(8,128)(2,1)}, bf16[8,64,128]{2,1,0:T(8,128)(2,1)}) custom-call(s32[64]{0:T(128)S(1)} %copy-done.2, s32[3]{0:T(128)S(1)} %pad_add_fusion.place, bf16[8,128,128]{2,1,0:T(8,128)(2,1)S(1)} %all-gather.1.qg_ref, bf16[8,128,128]{2,1,0:T(8,128)(2,1)S(1)} %all-to-all-done.kv_ref, f32[8,88,128]{2,1,0:T(8,128)S(1)} %all_to_all.25.parts_ref), custom_call_target="tpu_custom_call" | custom-call | tf_op jit(solution)/shard_map/backward_tile/pallas_call | solution.py:246
  61.9 3.4 %all-to-all-start.3 = ((bf16[8,64,128]{2,1,0:T(8,128)(2,1)}), bf16[8,64,128]{2,1,0:T(8,128)(2,1)S(1)}, u32[]{:S(2)}, u32[]{:S(2)}) async-start(bf16[8,64,128]{2,1,0:T(8,128)(2,1)} %get-tuple-element.5), calls=%async_computation.3 | async-start | bytes 262144 | tf_op jit(solution)/shard_map/all_to_all | solution.py:187
  65.3 0.6 join_parts.1
  65.9 4.8 %all-to-all-done.3 = bf16[8,64,128]{2,1,0:T(8,128)(2,1)S(1)} async-done(((bf16[8,64,128]{2,1,0:T(8,128)(2,1)}), bf16[8,64,128]{2,1,0:T(8,128)(2,1)S(1)}, u32[]{:S(2)}, u32[]{:S(2)}) %all-to-all-start.3) | async-done | bytes 131104 | tf_op jit(solution)/shard_map/all_to_all | solution.py:187
  70.6 27.2 %all_to_all.26.parts_ref = bf16[16,96,128]{2,1,0:T(8,128)(2,1)S(1)} all-to-all(bf16[16,96,128]{2,1,0:T(8,128)(2,1)S(1)} %join_parts.1), channel_id=1, replica_groups=mesh['b'=8,'zl'=2,'x'=4,'head'=16] {'head'}, dimensions={0} | all-to-all | bytes 786432 | tf_op jit(solution)/shard_map/all_to_all | solution.py:187
  97.9 11.7 %all-to-all-start.4 = ((bf16[8,128,128]{2,1,0:T(8,128)(2,1)}), bf16[8,128,128]{2,1,0:T(8,128)(2,1)S(1)}, u32[]{:S(2)}, u32[]{:S(2)}) async-start(bf16[8,128,128]{2,1,0:T(8,128)(2,1)} %get-tuple-element.6), calls=%async_computation.4 | async-start | bytes 524288 | tf_op jit(solution)/shard_map/all_to_all | solution.py:187
  109.6 0.6 reduce_sum.24
  110.2 11.6 %all-gather.2 = bf16[64,32,128]{2,1,0:T(8,128)(2,1)S(1)} all-gather(bf16[16,32,128]{2,1,0:T(8,128)(2,1)S(1)} %slice.4), channel_id=4, replica_groups=mesh['b'=8,'zl'=2,'x'=4,'head'=16] {'x'}, dimensions={0}, use_global_device_ids=true | all-gather | bytes 655360 | tf_op jit(solution)/shard_map/all_gather | solution.py:235
  121.8 1.0 mix.1
  122.8 8.0 %all-to-all-done.4 = bf16[8,128,128]{2,1,0:T(8,128)(2,1)S(1)} async-done(((bf16[8,128,128]{2,1,0:T(8,128)(2,1)}), bf16[8,128,128]{2,1,0:T(8,128)(2,1)S(1)}, u32[]{:S(2)}, u32[]{:S(2)}) %all-to-all-start.4) | async-done | bytes 262176 | tf_op jit(solution)/shard_map/all_to_all | solution.py:187
  130.8 0.7 reduce_sum.25
  (1 shorter events, 0.0 us)
Async XLA Ops:
  0.6 21.7 %copy-start = (bf16[1,64,4096]{2,1,0:T(8,128)(2,1)S(1)}, bf16[1,64,4096]{2,1,0:T(8,128)(2,1)}, u32[]{:S(2)}) copy-start(bf16[1,64,4096]{2,1,0:T(8,128)(2,1)} %param.7) | copy-start | bytes 1572868
  2.2 37.1 %all-to-all-start = ((bf16[8,128,128]{2,1,0:T(8,128)(2,1)}), bf16[8,128,128]{2,1,0:T(8,128)(2,1)S(1)}, u32[]{:S(2)}, u32[]{:S(2)}) async-start(bf16[8,128,128]{2,1,0:T(8,128)(2,1)} %broadcast_in_dim.14), calls=%async_computation | async-start | bytes 524288 | tf_op jit(solution)/shard_map/all_to_all | solution.py:187
  21.5 0.7 copy-start.3
  22.3 1.2 copy-start.1
  39.2 0.7 copy-start.2
  61.9 8.7 %all-to-all-start.3 = ((bf16[8,64,128]{2,1,0:T(8,128)(2,1)}), bf16[8,64,128]{2,1,0:T(8,128)(2,1)S(1)}, u32[]{:S(2)}, u32[]{:S(2)}) async-start(bf16[8,64,128]{2,1,0:T(8,128)(2,1)} %get-tuple-element.5), calls=%async_computation.3 | async-start | bytes 262144 | tf_op jit(solution)/shard_map/all_to_all | solution.py:187
  97.9 33.0 %all-to-all-start.4 = ((bf16[8,128,128]{2,1,0:T(8,128)(2,1)}), bf16[8,128,128]{2,1,0:T(8,128)(2,1)S(1)}, u32[]{:S(2)}, u32[]{:S(2)}) async-start(bf16[8,128,128]{2,1,0:T(8,128)(2,1)} %get-tuple-element.6), calls=%async_computation.4 | async-start | bytes 524288 | tf_op jit(solution)/shard_map/all_to_all | solution.py:187

commit v3 on v2

--- a/solution.py
+++ b/solution.py
@@ -11,11 +11,12 @@
 TOK = 128
 HD = 64
 ROWS = GROUP * TOK
-STATS = 3 * GROUP
+OUT, CENTRED, PLAIN, STATS = 0, HD, 2 * HD, 3 * HD
+STAT_ROWS = 48
+OUT_ROWS = STATS + STAT_ROWS
 QUARTERS = 4
 A = ("zl", "x")
-OUT_ROWS = HD + STATS
-NEG = -1e30
+NEG = -(2.0**100)
 INTERPRET = False
 PARAMS = pltpu.CompilerParams(vmem_limit_bytes=24 * 1024 * 1024)
 F32 = jnp.float32
@@ -42,12 +43,19 @@
     return key - query
 
 
-def forward_tile(order, place, qg_ref, kv_ref, out_ref, keys, values_t, stats):
+def split(value):
+    high = value.astype(BF16).astype(F32)
+    return high, value - high
+
+
+def forward_tile(order, place, qg_ref, kv_ref, out_ref, keys, values, kv_t, stats):
     b, a = place[0], place[1]
     kv = kv_ref[...].reshape(ROWS, 2 * HD)
     keys[...] = lanes_below(kv)
-    values_t[0:HD, :] = jnp.transpose(kv.astype(F32))[HD:, :].astype(BF16)
-    values_t[HD:, :] = jnp.ones((16, ROWS), BF16)
+    values[...] = lanes_below(kv, True)
+    kv_t[0 : 2 * HD, :] = jnp.transpose(kv.astype(F32)).astype(BF16)
+    kv_t[2 * HD :, :] = jnp.ones((16, ROWS), BF16)
+    stats[...] = jnp.zeros((STAT_ROWS, TOK), F32)
     diff = key_minus_query()
 
     def step(i, carry):
@@ -59,54 +67,81 @@
             limit = (query_block - order[j * GROUP + a]) * TOK
             masked.append(jnp.where(diff <= limit, scores[j * TOK : (j + 1) * TOK], NEG))
         masked = jnp.concatenate(masked, axis=0)
-        top = jnp.max(masked, axis=0, keepdims=True)
+        top = jnp.max(masked, axis=0, keepdims=True).astype(BF16).astype(F32)
         probs = jnp.exp(masked - top).astype(BF16)
-        summed = nn(values_t[...], probs)
+        summed = nn(kv_t[...], probs)
         grad_t = jnp.transpose(qg.astype(F32))[HD:, :]
-        part = summed[0:HD]
-        out_ref[i, 0:HD, :] = part
-        stats[pl.ds(i, 1), :] = top
-        stats[pl.ds(GROUP + i, 1), :] = summed[HD : HD + 1]
-        stats[pl.ds(2 * GROUP + i, 1), :] = jnp.sum(grad_t * part, axis=0, keepdims=True)
+        part = summed[HD : 2 * HD]
+        total = summed[2 * HD : 2 * HD + 1]
+        dot = jnp.sum(grad_t * part, axis=0, keepdims=True)
+        dprob = nt(values[...], qg)
+        dscore = (probs.astype(F32) * (dprob - dot / total)).astype(BF16)
+        out_ref[i, OUT : OUT + HD, :] = part.astype(BF16)
+        out_ref[i, CENTRED : CENTRED + HD, :] = nn(kv_t[0:HD, :], dscore).astype(BF16)
+        out_ref[i, PLAIN : PLAIN + HD, :] = summed[0:HD].astype(BF16)
+        rows = (top, *split(total), *split(dot))
+        for k, row in enumerate(rows):
+            stats[pl.ds(k * GROUP + i, 1), :] = row
         return carry
 
     lax.fori_loop(0, GROUP, step, 0)
     for i in range(GROUP):
-        out_ref[i, HD:, :] = stats[...]
-
-
-def total_stats(parts_ref):
-    top = parts_ref[0, HD : HD + GROUP, :]
+        out_ref[i, STATS:, :] = stats[...].astype(BF16)
+
+
+def part_stats(parts_ref):
+    tops, totals, dots = [], [], []
+    for p in range(GROUP):
+        rows = parts_ref[p, STATS:, :].astype(F32)
+        tops.append(rows[0:GROUP])
+        totals.append(rows[GROUP : 2 * GROUP] + rows[2 * GROUP : 3 * GROUP])
+        dots.append(rows[3 * GROUP : 4 * GROUP] + rows[4 * GROUP : 5 * GROUP])
+    return tops, totals, dots
+
+
+def joined(tops, totals, dots):
+    top = tops[0]
     for p in range(1, GROUP):
-        top = jnp.maximum(top, parts_ref[p, HD : HD + GROUP, :])
-    total = jnp.zeros((GROUP, TOK), F32)
-    dot = jnp.zeros((GROUP, TOK), F32)
-    for p in range(GROUP):
-        weight = jnp.exp(parts_ref[p, HD : HD + GROUP, :] - top)
-        total += weight * parts_ref[p, HD + GROUP : HD + 2 * GROUP, :]
-        dot += weight * parts_ref[p, HD + 2 * GROUP :, :]
-    return top, total, dot / total
-
-
-def prepare(queries_ref, weight_ref, grad_ref, out_ref):
-    grad_att = nt(grad_ref[...], weight_ref[...]).astype(BF16)
-    scaled = queries_ref[...] * jnp.asarray(HD**-0.5, BF16)
-    out_ref[...] = jnp.concatenate([scaled, grad_att], axis=1)
-
-
-def join_parts(place, parts_ref, weight_ref, out_ref, tops, totals):
+        top = jnp.maximum(top, tops[p])
+    weights = [jnp.exp(tops[p] - top) for p in range(GROUP)]
+    total = sum(weights[p] * totals[p] for p in range(GROUP))
+    dot = sum(weights[p] * dots[p] for p in range(GROUP))
+    return top, total, dot / total, weights
+
+
+def prepare(queries_hbm, weight_hbm, grad_hbm, out_ref, queries_t, weight, grad, sems):
+    pairs = ((queries_hbm, queries_t), (weight_hbm, weight), (grad_hbm, grad))
+    loads = [pltpu.make_async_copy(*pair, sems.at[k]) for k, pair in enumerate(pairs)]
+    for load in loads:
+        load.start()
+    for load in loads:
+        load.wait()
+    grad_att = nt(grad[...], weight[...])
+    scaled = jnp.transpose(queries_t[...].astype(F32)) * HD**-0.5
+    out_ref[...] = jnp.concatenate([scaled, grad_att], axis=1).astype(BF16)
+
+
+def join_parts(place, parts_ref, weight_ref, out_ref, dq_ref, own):
     a, quarter = place[1], place[2]
     rows = HD // QUARTERS
-    top, total, _ = total_stats(parts_ref)
-    tops[...] = top
-    totals[...] = total
-    own_top = tops[pl.ds(a, 1), :]
-    own_total = totals[pl.ds(a, 1), :]
-    acc = jnp.zeros((HD, TOK), F32)
+    tops, totals, dots = part_stats(parts_ref)
+    _, total, dot, weights = joined(tops, totals, dots)
+    own[0:GROUP, :] = 1.0 / total
     for p in range(GROUP):
-        weight = jnp.exp(parts_ref[p, pl.ds(HD + a, 1), :] - own_top)
-        acc += weight * parts_ref[p, 0:HD, :]
-    out = (acc / own_total).astype(BF16)
+        shift = dot - dots[p] / totals[p]
+        own[(2 * p + 1) * GROUP : (2 * p + 2) * GROUP, :] = weights[p]
+        own[(2 * p + 2) * GROUP : (2 * p + 3) * GROUP, :] = weights[p] * shift
+    attended = jnp.zeros((HD, TOK), F32)
+    dq = jnp.zeros((HD, TOK), F32)
+    for p in range(GROUP):
+        weight = own[pl.ds((2 * p + 1) * GROUP + a, 1), :]
+        shifted = own[pl.ds((2 * p + 2) * GROUP + a, 1), :]
+        attended += weight * parts_ref[p, OUT : OUT + HD, :].astype(F32)
+        dq += weight * parts_ref[p, CENTRED : CENTRED + HD, :].astype(F32)
+        dq -= shifted * parts_ref[p, PLAIN : PLAIN + HD, :].astype(F32)
+    scale = own[pl.ds(a, 1), :]
+    dq_ref[...] = (dq * (scale * HD**-0.5)).astype(BF16)
+    out = (attended * scale).astype(BF16)
     for h in range(out_ref.shape[0]):
         out_ref[h, 0:HD, :] = out
     own_rows = weight_ref[pl.ds(pl.multiple_of(quarter * rows, rows), rows), :]
@@ -134,10 +169,10 @@
 
 
 def backward_tile(
-    order, place, qg_ref, kv_ref, parts_ref, dkv_ref, dq_ref, query_part, grad_part, dscores, norm_dot
+    order, place, qg_ref, kv_ref, parts_ref, dkv_ref, query_part, grad_part, norm_dot
 ):
     b, a = place[0], place[1]
-    top, total, dot = total_stats(parts_ref)
+    top, total, dot, _ = joined(*part_stats(parts_ref))
     log_total = top + jnp.log(total)
     for i in range(GROUP):
         norm_dot[0:1, i * TOK : (i + 1) * TOK] = log_total[i : i + 1]
@@ -159,16 +194,11 @@
         )
         probs = jnp.where(allowed, jnp.exp(scores - logs), 0.0).astype(BF16)
         dscore = (probs.astype(F32) * (dprob - dots)).astype(BF16)
-        dscores[pl.ds(pl.multiple_of(j * TOK, TOK), TOK), :] = dscore
         dkv = nn(dscore, query_part[...]) + nn(probs, grad_part[...])
         dkv_ref[j] = dkv.astype(BF16)
         return carry
 
     lax.fori_loop(0, GROUP, step, 0)
-    keys_t = jnp.transpose(kv_ref[...].reshape(ROWS, 2 * HD).astype(F32))[0:HD, :].astype(BF16)
-    dq = nn(keys_t, dscores[...]) * (HD**-0.5)
-    for i in range(GROUP):
-        dq_ref[i] = dq[:, i * TOK : (i + 1) * TOK].astype(BF16)
 
 
 def smem():
@@ -198,35 +228,45 @@
     query_grad = pl.pallas_call(
         prepare,
         out_shape=jax.ShapeDtypeStruct((TOK, 2 * HD), BF16),
-        in_specs=[vmem(), vmem(), vmem()],
+        in_specs=[pl.BlockSpec(memory_space=pltpu.HBM)] * 3,
         out_specs=vmem(),
+        scratch_shapes=[
+            pltpu.VMEM((HD, TOK), BF16),
+            pltpu.VMEM(weight.shape, BF16),
+            pltpu.VMEM(out_grad.shape, BF16),
+            pltpu.SemaphoreType.DMA((3,)),
+        ],
         interpret=INTERPRET,
         compiler_params=PARAMS,
         name="prepare",
-    )(queries[:, 0], weight, out_grad)
+    )(jnp.transpose(queries[:, 0]), weight, out_grad)
     qg_group = lax.all_gather(lax.all_gather(query_grad, "x"), "zl")
     qg_group = qg_group.reshape(GROUP, TOK, 2 * HD)
     parts = pl.pallas_call(
         forward_tile,
-        out_shape=jax.ShapeDtypeStruct((GROUP, OUT_ROWS, TOK), F32),
+        out_shape=jax.ShapeDtypeStruct((GROUP, OUT_ROWS, TOK), BF16),
         in_specs=[smem(), smem(), vmem(), vmem()],
         out_specs=vmem(),
         scratch_shapes=[
             pltpu.VMEM((ROWS, 2 * HD), BF16),
-            pltpu.VMEM((HD + 16, ROWS), BF16),
-            pltpu.VMEM((STATS, TOK), F32),
+            pltpu.VMEM((ROWS, 2 * HD), BF16),
+            pltpu.VMEM((2 * HD + 16, ROWS), BF16),
+            pltpu.VMEM((STAT_ROWS, TOK), F32),
         ],
         interpret=INTERPRET,
         compiler_params=PARAMS,
         name="forward_tile",
     )(block_order, place, qg_group, kv_group)
     parts = exchange(parts, A)
-    mixed_parts = pl.pallas_call(
+    mixed_parts, grad_queries = pl.pallas_call(
         join_parts,
-        out_shape=jax.ShapeDtypeStruct((heads, HD + HD // QUARTERS * 2, TOK), BF16),
+        out_shape=(
+            jax.ShapeDtypeStruct((heads, HD + HD // QUARTERS * 2, TOK), BF16),
+            jax.ShapeDtypeStruct((HD, TOK), BF16),
+        ),
         in_specs=[smem(), vmem(), vmem()],
-        out_specs=vmem(),
-        scratch_shapes=[pltpu.VMEM((GROUP, TOK), F32), pltpu.VMEM((GROUP, TOK), F32)],
+        out_specs=(vmem(), vmem()),
+        scratch_shapes=[pltpu.VMEM(((2 * GROUP + 1) * GROUP, TOK), F32)],
         interpret=INTERPRET,
         compiler_params=PARAMS,
         name="join_parts",
@@ -243,18 +283,14 @@
         compiler_params=PARAMS,
         name="mix",
     )(mixed_parts, quarters)
-    dkv, dq = pl.pallas_call(
+    dkv = pl.pallas_call(
         backward_tile,
-        out_shape=(
-            jax.ShapeDtypeStruct((GROUP, TOK, 2 * HD), BF16),
-            jax.ShapeDtypeStruct((GROUP, HD, TOK), BF16),
-        ),
+        out_shape=jax.ShapeDtypeStruct((GROUP, TOK, 2 * HD), BF16),
         in_specs=[smem(), smem(), vmem(), vmem(), vmem()],
-        out_specs=(vmem(), vmem()),
+        out_specs=vmem(),
         scratch_shapes=[
             pltpu.VMEM((ROWS, 2 * HD), BF16),
             pltpu.VMEM((ROWS, 2 * HD), BF16),
-            pltpu.VMEM((ROWS, ROWS), BF16),
             pltpu.VMEM((8, ROWS), F32),
         ],
         interpret=INTERPRET,
@@ -262,10 +298,8 @@
         name="backward_tile",
     )(block_order, place, qg_group, kv_group, parts)
     dkv = exchange(dkv, "b")
-    dq = exchange(dq, A)
     grad_keys_values = jnp.sum(dkv.astype(F32), axis=0).astype(BF16)[:, None]
-    grad_queries = jnp.transpose(jnp.sum(dq.astype(F32), axis=0)).astype(BF16)[:, None]
-    return (mixed_out, grad_queries, grad_keys_values)
+    return (mixed_out, jnp.transpose(grad_queries)[:, None], grad_keys_values)
 
 
 def solution(mesh):

time: 132 us -> 122 us (0.924)
  blocking collectives: 65.4 us -> 38.8 us
  starting transfers between devices: 34.4 us -> 42.8 us
  waiting for transfers between devices: 12.8 us -> 17.8 us
  Pallas kernels: 12.7 us -> 16.2 us
    all_to_all x2 -> x1, blocking collectives: 38.6 us -> 12 us  [exchange(): return lax.all_to_all(value, axis, 0, 0, tiled=True)]
    all_to_all x3, starting transfers between devices: 34.4 us -> 42.8 us  [exchange(): return lax.all_to_all(value, axis, 0, 0, tiled=True)]
    all_to_all x3, waiting for transfers between devices: 12.8 us -> 17.8 us  [exchange(): return lax.all_to_all(value, axis, 0, 0, tiled=True)]
    pallas_call x1, Pallas kernels: 4.94 us -> 7.98 us  [local(): pl.pallas_call(forward_tile, out_shape=jax.ShapeDtypeStruct((GROUP, OUT_R...]
  transfers between devices with their start and end apart: 3 -> 3, of which waited for: 2 -> 2; matrix products, arithmetic and copies ran while one was open for 1% -> 0% of each run, Pallas kernels for 2% -> 6%
where the time goes in v3:
time: 122 us; the launch traced here: 121 us
  starting transfers between devices  42.8 us (35%)
  blocking collectives  38.8 us (32%)
  waiting for transfers between devices  17.8 us (15%)
  Pallas kernels  16.2 us (13%)
  local copies, waits for them, and re-layouts  4.05 us (3%)
    all_to_all x3, starting transfers between devices, exchange(): return lax.all_to_all(value, axis, 0, 0, tiled=True)  42.8 us
    all_to_all x3, waiting for transfers between devices, exchange(): return lax.all_to_all(value, axis, 0, 0, tiled=True)  17.8 us
    all_gather x2, blocking collectives, local(): qg_group = lax.all_gather(lax.all_gather(query_grad, 'x'), 'zl')  15.1 us
    all_to_all x1, blocking collectives, exchange(): return lax.all_to_all(value, axis, 0, 0, tiled=True)  12 us
    all_gather x1, blocking collectives, local(): quarters = lax.all_gather(mixed_parts[:, HD:], 'x')  11.6 us
    pallas_call x1, Pallas kernels, local(): pl.pallas_call(forward_tile, out_shape=jax.ShapeDtypeStruct((GROUP, OUT_R...  7.98 us
    pallas_call x1, Pallas kernels, local(): pl.pallas_call(backward_tile, out_shape=jax.ShapeDtypeStruct((GROUP, TOK,...  5.22 us
    unnamed x8, local copies, waits for them, and re-layouts  2.5 us
  transfers between devices with their start and end apart: 3, of which 2 were waited for; matrix products, arithmetic and copies ran while one was open for 0% of the time, Pallas kernels for 6%

profile of v3, /device:TPU:1, one launch (start us, length us, event | category | flops | bytes accessed | tf_op | source)
XLA Modules:
  0.0 121.2 jit_solution(3271855479227115983)
XLA Ops:
  0.6 0.0 copy-start
  0.6 1.5 %broadcast_in_dim.14 = bf16[8,128,128]{2,1,0:T(8,128)(2,1)} broadcast(bf16[128,128]{1,0:T(8,128)(2,1)} %bitcast.19), dimensions={1,2} | broadcast | bytes 294912 | tf_op jit(solution)/shard_map/broadcast_in_dim | solution.py:213
  2.2 19.3 %all-to-all-start = ((bf16[8,128,128]{2,1,0:T(8,128)(2,1)}), bf16[8,128,128]{2,1,0:T(8,128)(2,1)S(1)}, u32[]{:S(2)}, u32[]{:S(2)}) async-start(bf16[8,128,128]{2,1,0:T(8,128)(2,1)} %broadcast_in_dim.14), calls=%async_computation | async-start | bytes 524288 | tf_op jit(solution)/shard_map/all_to_all | solution.py:217
  21.5 0.0 copy-start.2
  21.5 0.0 copy-done
  21.5 0.7 copy-done.2
  22.2 0.0 copy-start.1
  22.2 1.2 %copy-done.1 = bf16[128,4096]{1,0:T(8,128)(2,1)S(1)} copy-done((bf16[128,4096]{1,0:T(8,128)(2,1)S(1)}, bf16[128,4096]{1,0:T(8,128)(2,1)}, u32[]{:S(2)}) %copy-start.1) | copy-done | bytes 1048600
  23.4 0.6 prepare.1
  24.1 10.4 %all-gather = bf16[512,128]{1,0:T(8,128)(2,1)S(1)} all-gather(bf16[128,128]{1,0:T(8,128)(2,1)S(1)} %prepare.1), channel_id=2, replica_groups=mesh['b'=8,'zl'=2,'x'=4,'head'=16] {'x'}, dimensions={0}, use_global_device_ids=true | all-gather | bytes 163840 | tf_op jit(solution)/shard_map/all_gather | solution.py:243
  34.4 4.8 %all-gather.1.qg_ref = bf16[8,128,128]{2,1,0:T(8,128)(2,1)S(1)} all-gather(bf16[4,128,128]{2,1,0:T(8,128)(2,1)S(1)} %bitcast.18), channel_id=3, replica_groups=mesh['b'=8,'zl'=2,'x'=4,'head'=16] {'zl'}, dimensions={0}, use_global_device_ids=true | all-gather | bytes 393216 | tf_op jit(solution)/shard_map/all_gather | solution.py:243
  39.2 0.0 copy-start.3
  39.2 0.1 pad_add_fusion.place
  39.3 0.0 all-to-all-done.kv_ref
  39.3 0.6 copy-done.3
  39.8 8.0 %forward_tile.1 = bf16[8,240,128]{2,1,0:T(8,128)(2,1)S(1)} custom-call(s32[64]{0:T(128)S(1)} %copy-done.3, s32[3]{0:T(128)S(1)} %pad_add_fusion.place, bf16[8,128,128]{2,1,0:T(8,128)(2,1)S(1)} %all-gather.1.qg_ref, bf16[8,128,128]{2,1,0:T(8,128)(2,1)S(1)} %all-to-all-done.kv_ref), custom_call_target="tpu_custom_call" | custom-call | tf_op jit(solution)/shard_map/forward_tile/pallas_call | solution.py:245
  47.8 12.0 %all_to_all.20.parts_ref = bf16[8,240,128]{2,1,0:T(8,128)(2,1)S(1)} all-to-all(bf16[8,240,128]{2,1,0:T(8,128)(2,1)S(1)} %forward_tile.1), channel_id=1, replica_groups=mesh['b'=8,'zl'=2,'x'=4,'head'=16] {'zl','x'}, dimensions={0} | all-to-all | bytes 983040 | tf_op jit(solution)/shard_map/all_to_all | solution.py:217
  59.8 1.4 %join_parts.1 = (bf16[16,96,128]{2,1,0:T(8,128)(2,1)}, bf16[64,128]{1,0:T(8,128)(2,1)}) custom-call(s32[3]{0:T(128)S(1)} %pad_add_fusion.place, bf16[8,240,128]{2,1,0:T(8,128)(2,1)S(1)} %all_to_all.20.parts_ref, bf16[64,4096]{1,0:T(8,128)(2,1)S(1)} %bitcast.15), custom_call_target="tpu_custom_call" | custom-call | tf_op jit(solution)/shard_map/join_parts/pallas_call | solution.py:261
  61.3 11.8 %all-to-all-start.2 = ((bf16[16,96,128]{2,1,0:T(8,128)(2,1)}), bf16[16,96,128]{2,1,0:T(8,128)(2,1)S(1)}, u32[]{:S(2)}, u32[]{:S(2)}) async-start(bf16[16,96,128]{2,1,0:T(8,128)(2,1)} %get-tuple-element.5), calls=%async_computation.2 | async-start | bytes 786432 | tf_op jit(solution)/shard_map/all_to_all | solution.py:217
  73.1 5.2 %backward_tile.1 = bf16[8,128,128]{2,1,0:T(8,128)(2,1)} custom-call(s32[64]{0:T(128)S(1)} %copy-done.3, s32[3]{0:T(128)S(1)} %pad_add_fusion.place, bf16[8,128,128]{2,1,0:T(8,128)(2,1)S(1)} %all-gather.1.qg_ref, bf16[8,128,128]{2,1,0:T(8,128)(2,1)S(1)} %all-to-all-done.kv_ref, bf16[8,240,128]{2,1,0:T(8,128)(2,1)S(1)} %all_to_all.20.parts_ref), custom_call_target="tpu_custom_call" | custom-call | tf_op jit(solution)/shard_map/backward_tile/pallas_call | solution.py:286
  78.3 9.3 %all-to-all-done.2.parts_ref = bf16[16,96,128]{2,1,0:T(8,128)(2,1)S(1)} async-done(((bf16[16,96,128]{2,1,0:T(8,128)(2,1)}), bf16[16,96,128]{2,1,0:T(8,128)(2,1)S(1)}, u32[]{:S(2)}, u32[]{:S(2)}) %all-to-all-start.2) | async-done | bytes 393248 | tf_op jit(solution)/shard_map/all_to_all | solution.py:217
  87.6 11.7 %all-to-all-start.3 = ((bf16[8,128,128]{2,1,0:T(8,128)(2,1)}), bf16[8,128,128]{2,1,0:T(8,128)(2,1)S(1)}, u32[]{:S(2)}, u32[]{:S(2)}) async-start(bf16[8,128,128]{2,1,0:T(8,128)(2,1)} %backward_tile.1), calls=%async_computation.3 | async-start | bytes 524288 | tf_op jit(solution)/shard_map/all_to_all | solution.py:217
  99.4 11.6 %all-gather.2 = bf16[64,32,128]{2,1,0:T(8,128)(2,1)S(1)} all-gather(bf16[16,32,128]{2,1,0:T(8,128)(2,1)S(1)} %slice.4), channel_id=4, replica_groups=mesh['b'=8,'zl'=2,'x'=4,'head'=16] {'x'}, dimensions={0}, use_global_device_ids=true | all-gather | bytes 655360 | tf_op jit(solution)/shard_map/all_gather | solution.py:275
  111.0 1.0 mix.1
  111.9 8.6 %all-to-all-done.3 = bf16[8,128,128]{2,1,0:T(8,128)(2,1)S(1)} async-done(((bf16[8,128,128]{2,1,0:T(8,128)(2,1)}), bf16[8,128,128]{2,1,0:T(8,128)(2,1)S(1)}, u32[]{:S(2)}, u32[]{:S(2)}) %all-to-all-start.3) | async-done | bytes 262176 | tf_op jit(solution)/shard_map/all_to_all | solution.py:217
  120.5 0.7 reduce_sum.12
  (1 shorter events, 0.0 us)
Async XLA Ops:
  0.6 20.9 %copy-start = (bf16[1,64,4096]{2,1,0:T(8,128)(2,1)S(1)}, bf16[1,64,4096]{2,1,0:T(8,128)(2,1)}, u32[]{:S(2)}) copy-start(bf16[1,64,4096]{2,1,0:T(8,128)(2,1)} %param.7) | copy-start | bytes 1572868
  2.2 37.1 %all-to-all-start = ((bf16[8,128,128]{2,1,0:T(8,128)(2,1)}), bf16[8,128,128]{2,1,0:T(8,128)(2,1)S(1)}, u32[]{:S(2)}, u32[]{:S(2)}) async-start(bf16[8,128,128]{2,1,0:T(8,128)(2,1)} %broadcast_in_dim.14), calls=%async_computation | async-start | bytes 524288 | tf_op jit(solution)/shard_map/all_to_all | solution.py:217
  21.5 0.7 copy-start.2
  22.2 1.2 %copy-start.1 = (bf16[128,4096]{1,0:T(8,128)(2,1)S(1)}, bf16[128,4096]{1,0:T(8,128)(2,1)}, u32[]{:S(2)}) copy-start(bf16[128,4096]{1,0:T(8,128)(2,1)} %grad_hbm.1) | copy-start | bytes 3145732
  39.2 0.7 copy-start.3
  61.3 26.3 %all-to-all-start.2 = ((bf16[16,96,128]{2,1,0:T(8,128)(2,1)}), bf16[16,96,128]{2,1,0:T(8,128)(2,1)S(1)}, u32[]{:S(2)}, u32[]{:S(2)}) async-start(bf16[16,96,128]{2,1,0:T(8,128)(2,1)} %get-tuple-element.5), calls=%async_computation.2 | async-start | bytes 786432 | tf_op jit(solution)/shard_map/all_to_all | solution.py:217
  87.6 32.9 %all-to-all-start.3 = ((bf16[8,128,128]{2,1,0:T(8,128)(2,1)}), bf16[8,128,128]{2,1,0:T(8,128)(2,1)S(1)}, u32[]{:S(2)}, u32[]{:S(2)}) async-start(bf16[8,128,128]{2,1,0:T(8,128)(2,1)} %backward_tile.1), calls=%async_computation.3 | async-start | bytes 524288 | tf_op jit(solution)/shard_map/all_to_all | solution.py:217

commit v4 on v3

--- a/solution.py
+++ b/solution.py
@@ -15,6 +15,7 @@
 STAT_ROWS = 48
 OUT_ROWS = STATS + STAT_ROWS
 QUARTERS = 4
+WIDE = 4
 A = ("zl", "x")
 NEG = -(2.0**100)
 INTERPRET = False
@@ -37,10 +38,17 @@
     return jnp.where(keep, x, jnp.zeros_like(x))
 
 
-def key_minus_query():
+def fill_caps(caps):
     key = lax.broadcasted_iota(jnp.int32, (TOK, TOK), 0)
     query = lax.broadcasted_iota(jnp.int32, (TOK, TOK), 1)
-    return key - query
+    caps[0:TOK, :] = jnp.full((TOK, TOK), NEG, F32)
+    caps[TOK : 2 * TOK, :] = jnp.where(key <= query, -NEG, NEG)
+    caps[2 * TOK :, :] = jnp.full((TOK, TOK), -NEG, F32)
+
+
+def cap_for(caps, key_block, query_block):
+    later = jnp.clip(query_block - key_block, -1, 1) + 1
+    return caps[pl.ds(pl.multiple_of(later * TOK, TOK), TOK), :]
 
 
 def split(value):
@@ -48,7 +56,7 @@
     return high, value - high
 
 
-def forward_tile(order, place, qg_ref, kv_ref, out_ref, keys, values, kv_t, stats):
+def forward_tile(order, place, qg_ref, kv_ref, out_ref, keys, values, kv_t, stats, caps):
     b, a = place[0], place[1]
     kv = kv_ref[...].reshape(ROWS, 2 * HD)
     keys[...] = lanes_below(kv)
@@ -56,16 +64,18 @@
     kv_t[0 : 2 * HD, :] = jnp.transpose(kv.astype(F32)).astype(BF16)
     kv_t[2 * HD :, :] = jnp.ones((16, ROWS), BF16)
     stats[...] = jnp.zeros((STAT_ROWS, TOK), F32)
-    diff = key_minus_query()
-
-    def step(i, carry):
-        qg = qg_ref[i]
+    fill_caps(caps)
+    for first in range(0, GROUP, WIDE):
+        blocks = range(first, first + WIDE)
+        qg = qg_ref[first : first + WIDE].reshape(WIDE * TOK, 2 * HD)
         scores = nt(keys[...], qg)
-        query_block = order[b * GROUP + i]
         masked = []
         for j in range(GROUP):
-            limit = (query_block - order[j * GROUP + a]) * TOK
-            masked.append(jnp.where(diff <= limit, scores[j * TOK : (j + 1) * TOK], NEG))
+            key_block = order[j * GROUP + a]
+            cap = jnp.concatenate(
+                [cap_for(caps, key_block, order[b * GROUP + i]) for i in blocks], axis=1
+            )
+            masked.append(jnp.minimum(scores[j * TOK : (j + 1) * TOK], cap))
         masked = jnp.concatenate(masked, axis=0)
         top = jnp.max(masked, axis=0, keepdims=True).astype(BF16).astype(F32)
         probs = jnp.exp(masked - top).astype(BF16)
@@ -75,16 +85,16 @@
         total = summed[2 * HD : 2 * HD + 1]
         dot = jnp.sum(grad_t * part, axis=0, keepdims=True)
         dprob = nt(values[...], qg)
-        dscore = (probs.astype(F32) * (dprob - dot / total)).astype(BF16)
-        out_ref[i, OUT : OUT + HD, :] = part.astype(BF16)
-        out_ref[i, CENTRED : CENTRED + HD, :] = nn(kv_t[0:HD, :], dscore).astype(BF16)
-        out_ref[i, PLAIN : PLAIN + HD, :] = summed[0:HD].astype(BF16)
+        dscore = probs * (dprob - dot / total).astype(BF16)
+        centred = nn(kv_t[0:HD, :], dscore)
         rows = (top, *split(total), *split(dot))
-        for k, row in enumerate(rows):
-            stats[pl.ds(k * GROUP + i, 1), :] = row
-        return carry
-
-    lax.fori_loop(0, GROUP, step, 0)
+        for i in blocks:
+            lanes = slice((i - first) * TOK, (i - first + 1) * TOK)
+            out_ref[i, OUT : OUT + HD, :] = part[:, lanes].astype(BF16)
+            out_ref[i, CENTRED : CENTRED + HD, :] = centred[:, lanes].astype(BF16)
+            out_ref[i, PLAIN : PLAIN + HD, :] = summed[0:HD, lanes].astype(BF16)
+            for k, row in enumerate(rows):
+                stats[k * GROUP + i : k * GROUP + i + 1, :] = row[:, lanes]
     for i in range(GROUP):
         out_ref[i, STATS:, :] = stats[...].astype(BF16)
 
@@ -109,16 +119,21 @@
     return top, total, dot / total, weights
 
 
-def prepare(queries_hbm, weight_hbm, grad_hbm, out_ref, queries_t, weight, grad, sems):
-    pairs = ((queries_hbm, queries_t), (weight_hbm, weight), (grad_hbm, grad))
+def prepare(
+    queries_hbm, kv_hbm, weight_hbm, grad_hbm, qg_ref, copies_ref, queries_t, kv, weight, grad, sems
+):
+    pairs = ((kv_hbm, kv), (weight_hbm, weight), (grad_hbm, grad), (queries_hbm, queries_t))
     loads = [pltpu.make_async_copy(*pair, sems.at[k]) for k, pair in enumerate(pairs)]
     for load in loads:
         load.start()
-    for load in loads:
+    loads[0].wait()
+    for p in range(GROUP):
+        copies_ref[p] = kv[...]
+    for load in loads[1:]:
         load.wait()
     grad_att = nt(grad[...], weight[...])
     scaled = jnp.transpose(queries_t[...].astype(F32)) * HD**-0.5
-    out_ref[...] = jnp.concatenate([scaled, grad_att], axis=1).astype(BF16)
+    qg_ref[...] = jnp.concatenate([scaled, grad_att], axis=1).astype(BF16)
 
 
 def join_parts(place, parts_ref, weight_ref, out_ref, dq_ref, own):
@@ -169,7 +184,7 @@
 
 
 def backward_tile(
-    order, place, qg_ref, kv_ref, parts_ref, dkv_ref, query_part, grad_part, norm_dot
+    order, place, qg_ref, kv_ref, parts_ref, dkv_ref, query_part, grad_part, norm_dot, caps
 ):
     b, a = place[0], place[1]
     top, total, dot, _ = joined(*part_stats(parts_ref))
@@ -180,25 +195,19 @@
     qg = qg_ref[...].reshape(ROWS, 2 * HD)
     query_part[...] = lanes_below(qg)
     grad_part[...] = lanes_below(qg, True)
-    diff = key_minus_query()
-
-    def step(j, carry):
+    fill_caps(caps)
+    for j in range(GROUP):
         kv = kv_ref[j]
-        scores = nt(kv, query_part[...])
+        key_block = order[j * GROUP + a]
+        cap = jnp.concatenate(
+            [cap_for(caps, key_block, order[b * GROUP + i]) for i in range(GROUP)], axis=1
+        )
+        masked = jnp.minimum(nt(kv, query_part[...]), cap)
+        probs = jnp.exp(masked - norm_dot[0:1, :]).astype(BF16)
         dprob = nt(kv, grad_part[...])
-        key_block = order[j * GROUP + a]
-        logs = norm_dot[0:1, :]
-        dots = norm_dot[1:2, :]
-        allowed = jnp.concatenate(
-            [diff <= (order[b * GROUP + i] - key_block) * TOK for i in range(GROUP)], axis=1
-        )
-        probs = jnp.where(allowed, jnp.exp(scores - logs), 0.0).astype(BF16)
-        dscore = (probs.astype(F32) * (dprob - dots)).astype(BF16)
+        dscore = probs * (dprob - norm_dot[1:2, :]).astype(BF16)
         dkv = nn(dscore, query_part[...]) + nn(probs, grad_part[...])
         dkv_ref[j] = dkv.astype(BF16)
-        return carry
-
-    lax.fori_loop(0, GROUP, step, 0)
 
 
 def smem():
@@ -207,10 +216,6 @@
 
 def vmem():
     return pl.BlockSpec(memory_space=pltpu.VMEM)
-
-
-def copies_for(value, axis):
-    return jnp.broadcast_to(value[None], (lax.axis_size(axis), *value.shape))
 
 
 def exchange(value, axis):
@@ -222,25 +227,31 @@
     place = jnp.stack(
         [lax.axis_index("b"), lax.axis_index(A), lax.axis_index("x")]
     ).astype(jnp.int32)
-    kv_group = exchange(copies_for(keys_values[:, 0], "b"), "b")
     weight = out_weight[0]
     columns = weight.shape[1] // heads
-    query_grad = pl.pallas_call(
+    query_grad, kv_copies = pl.pallas_call(
         prepare,
-        out_shape=jax.ShapeDtypeStruct((TOK, 2 * HD), BF16),
-        in_specs=[pl.BlockSpec(memory_space=pltpu.HBM)] * 3,
-        out_specs=vmem(),
+        out_shape=(
+            jax.ShapeDtypeStruct((TOK, 2 * HD), BF16),
+            jax.ShapeDtypeStruct((GROUP, TOK, 2 * HD), BF16),
+        ),
+        in_specs=[pl.BlockSpec(memory_space=pltpu.HBM)] * 4,
+        out_specs=(vmem(), vmem()),
         scratch_shapes=[
             pltpu.VMEM((HD, TOK), BF16),
+            pltpu.VMEM((TOK, 2 * HD), BF16),
             pltpu.VMEM(weight.shape, BF16),
             pltpu.VMEM(out_grad.shape, BF16),
-            pltpu.SemaphoreType.DMA((3,)),
+            pltpu.SemaphoreType.DMA((4,)),
         ],
         interpret=INTERPRET,
-        compiler_params=PARAMS,
         name="prepare",
-    )(jnp.transpose(queries[:, 0]), weight, out_grad)
-    qg_group = lax.all_gather(lax.all_gather(query_grad, "x"), "zl")
+    )(jnp.transpose(queries[:, 0]), keys_values[:, 0], weight, out_grad)
+    kv_group = exchange(kv_copies, "b")
+    qg_group = query_grad
+    for pairs in ([[0, 1], [2, 3]], [[0, 3], [1, 2]]):
+        qg_group = lax.all_gather(qg_group, "x", tiled=True, axis_index_groups=pairs)
+    qg_group = lax.all_gather(qg_group, "zl")
     qg_group = qg_group.reshape(GROUP, TOK, 2 * HD)
     parts = pl.pallas_call(
         forward_tile,
@@ -252,6 +263,7 @@
             pltpu.VMEM((ROWS, 2 * HD), BF16),
             pltpu.VMEM((2 * HD + 16, ROWS), BF16),
             pltpu.VMEM((STAT_ROWS, TOK), F32),
+            pltpu.VMEM((3 * TOK, TOK), F32),
         ],
         interpret=INTERPRET,
         compiler_params=PARAMS,
@@ -292,6 +304,7 @@
             pltpu.VMEM((ROWS, 2 * HD), BF16),
             pltpu.VMEM((ROWS, 2 * HD), BF16),
             pltpu.VMEM((8, ROWS), F32),
+            pltpu.VMEM((3 * TOK, TOK), F32),
         ],
         interpret=INTERPRET,
         compiler_params=PARAMS,

time: 122 us -> 114 us (0.934)
  Pallas kernels: 16.2 us -> 12 us
  starting transfers between devices: 42.8 us -> 38.9 us
  local copies, waits for them, and re-layouts: 4.05 us -> 0.56 us
  blocking collectives: 38.8 us -> 41.5 us
  waiting for transfers between devices: 17.8 us -> 19.5 us
    pallas_call x1, Pallas kernels: 7.98 us -> 3.39 us  [local(): pl.pallas_call(forward_tile, out_shape=jax.ShapeDtypeStruct((GROUP, OUT_R...]
    all_to_all x3, starting transfers between devices: 42.8 us -> 38.9 us  [exchange(): return lax.all_to_all(value, axis, 0, 0, tiled=True)]
    unnamed x8 -> x6, local copies, waits for them, and re-layouts: 2.5 us -> 0.55 us
    pallas_call x1, Pallas kernels: 0.63 us -> 2.55 us  [local(): pl.pallas_call(prepare, out_shape=(jax.ShapeDtypeStruct((TOK, 2 * HD), BF...]
    all_gather x2 -> x3, blocking collectives: 15.1 us -> 17 us  [the longest x2 8.7 us: local(): lax.all_gather(qg_group, 'x', tiled=True, axis_index_groups=pairs)]
    all_to_all x3, waiting for transfers between devices: 17.8 us -> 19.5 us  [exchange(): return lax.all_to_all(value, axis, 0, 0, tiled=True)]
    broadcast_in_dim x1 -> x0, local copies, waits for them, and re-layouts: 1.54 us -> none  [copies_for(): return jnp.broadcast_to(value[None], (lax.axis_size(axis), *value.shape))]
    pallas_call x1, Pallas kernels: 5.22 us -> 3.7 us  [local(): pl.pallas_call(backward_tile, out_shape=jax.ShapeDtypeStruct((GROUP, TOK,...]
  transfers between devices with their start and end apart: 3 -> 3, of which waited for: 2 -> 3; matrix products, arithmetic and copies ran while one was open for 0% -> 0% of each run, Pallas kernels for 6% -> 4%
where the time goes in v4:
time: 114 us
  blocking collectives  41.5 us (36%)
  starting transfers between devices  38.9 us (34%)
  waiting for transfers between devices  19.5 us (17%)
  Pallas kernels  12 us (11%)
    all_to_all x3, starting transfers between devices, exchange(): return lax.all_to_all(value, axis, 0, 0, tiled=True)  38.9 us
    all_to_all x3, waiting for transfers between devices, exchange(): return lax.all_to_all(value, axis, 0, 0, tiled=True)  19.5 us
    all_to_all x1, blocking collectives, exchange(): return lax.all_to_all(value, axis, 0, 0, tiled=True)  12.9 us
    all_gather x1, blocking collectives, local(): quarters = lax.all_gather(mixed_parts[:, HD:], 'x')  11.6 us
    all_gather x2, blocking collectives, local(): lax.all_gather(qg_group, 'x', tiled=True, axis_index_groups=pairs)  8.7 us
    all_gather x1, blocking collectives, local(): qg_group = lax.all_gather(qg_group, 'zl')  8.27 us
    pallas_call x1, Pallas kernels, local(): pl.pallas_call(backward_tile, out_shape=jax.ShapeDtypeStruct((GROUP, TOK,...  3.7 us
    pallas_call x1, Pallas kernels, local(): pl.pallas_call(forward_tile, out_shape=jax.ShapeDtypeStruct((GROUP, OUT_R...  3.39 us
  transfers between devices with their start and end apart: 3, of which 3 were waited for; matrix products, arithmetic and copies ran while one was open for 0% of the time, Pallas kernels for 4%

profile of v4, /device:TPU:1, one launch (start us, length us, event | category | flops | bytes accessed | tf_op | source)
XLA Modules:
  0.0 113.9 jit_solution(272244504913563129)
XLA Ops:
  0.6 2.5 %prepare.1 = (bf16[128,128]{1,0:T(8,128)(2,1)}, bf16[8,128,128]{2,1,0:T(8,128)(2,1)}) custom-call(bf16[64,128]{1,0:T(8,128)(2,1)} %bitcast.21, bf16[128,128]{1,0:T(8,128)(2,1)} %bitcast.19, bf16[64,4096]{1,0:T(8,128)(2,1)} %bitcast.16, bf16[128,4096]{1,0:T(8,128)(2,1)} %grad_hbm.1), custom_call_target="tpu_custom_call" | custom-call | tf_op jit(solution)/shard_map/prepare/pallas_call | solution.py:232
  3.2 0.0 copy-start.2
  3.2 19.3 %all-to-all-start = ((bf16[8,128,128]{2,1,0:T(8,128)(2,1)}), bf16[8,128,128]{2,1,0:T(8,128)(2,1)S(1)}, u32[]{:S(2)}, u32[]{:S(2)}) async-start(bf16[8,128,128]{2,1,0:T(8,128)(2,1)} %get-tuple-element.8), calls=%async_computation | async-start | bytes 524288 | tf_op jit(solution)/shard_map/all_to_all | solution.py:222
  22.5 0.0 copy-done.2
  22.5 3.4 %all_gather.18 = bf16[256,128]{1,0:T(8,128)(2,1)S(1)} all-gather(bf16[128,128]{1,0:T(8,128)(2,1)S(1)} %copy-done.2), channel_id=1, replica_groups={{0,16},{32,48},{1,17},{33,49},{2,18},{34,50},{3,19},{35,51},{4,20},{36,..., dimensions={0}, use_global_device_ids=true | all-gather | bytes 98304 | tf_op jit(solution)/shard_map/all_gather | solution.py:253
  25.9 5.3 %all_gather.19 = bf16[512,128]{1,0:T(8,128)(2,1)S(1)} all-gather(bf16[256,128]{1,0:T(8,128)(2,1)S(1)} %all_gather.18), channel_id=1, replica_groups={{0,48},{16,32},{1,49},{17,33},{2,50},{18,34},{3,51},{19,35},{4,52},{20,..., dimensions={0}, use_global_device_ids=true | all-gather | bytes 196608 | tf_op jit(solution)/shard_map/all_gather | solution.py:253
  31.2 8.3 %all-gather = bf16[1024,128]{1,0:T(8,128)(2,1)S(1)} all-gather(bf16[512,128]{1,0:T(8,128)(2,1)S(1)} %all_gather.19), channel_id=2, replica_groups=mesh['b'=8,'zl'=2,'x'=4,'head'=16] {'zl'}, dimensions={0}, use_global_device_ids=true | all-gather | bytes 393216 | tf_op jit(solution)/shard_map/all_gather | solution.py:254
  39.5 0.1 pad_add_fusion.place
  39.6 0.0 copy-start.1
  39.6 0.1 all-to-all-done.kv_ref
  39.7 0.5 copy-done.1
  40.2 3.4 %forward_tile.1 = bf16[8,240,128]{2,1,0:T(8,128)(2,1)S(1)} custom-call(s32[64]{0:T(128)S(1)} %copy-done.1, s32[3]{0:T(128)S(1)} %pad_add_fusion.place, bf16[8,128,128]{2,1,0:T(8,128)(2,1)S(1)} %bitcast.14, bf16[8,128,128]{2,1,0:T(8,128)(2,1)S(1)} %all-to-all-done.kv_ref), custom_call_target="tpu_custom_call" | custom-call | tf_op jit(solution)/shard_map/forward_tile/pallas_call | solution.py:256
  43.6 0.0 copy-start
  43.6 12.9 %all_to_all.20.parts_ref = bf16[8,240,128]{2,1,0:T(8,128)(2,1)S(1)} all-to-all(bf16[8,240,128]{2,1,0:T(8,128)(2,1)S(1)} %forward_tile.1), channel_id=1, replica_groups=mesh['b'=8,'zl'=2,'x'=4,'head'=16] {'zl','x'}, dimensions={0} | all-to-all | bytes 983040 | tf_op jit(solution)/shard_map/all_to_all | solution.py:222
  56.6 0.0 copy-done
  56.6 1.4 %join_parts.1 = (bf16[16,96,128]{2,1,0:T(8,128)(2,1)}, bf16[64,128]{1,0:T(8,128)(2,1)}) custom-call(s32[3]{0:T(128)S(1)} %pad_add_fusion.place, bf16[8,240,128]{2,1,0:T(8,128)(2,1)S(1)} %all_to_all.20.parts_ref, bf16[64,4096]{1,0:T(8,128)(2,1)S(1)} %bitcast.17), custom_call_target="tpu_custom_call" | custom-call | tf_op jit(solution)/shard_map/join_parts/pallas_call | solution.py:273
  58.0 12.6 %all-to-all-start.2 = ((bf16[16,96,128]{2,1,0:T(8,128)(2,1)}), bf16[16,96,128]{2,1,0:T(8,128)(2,1)S(1)}, u32[]{:S(2)}, u32[]{:S(2)}) async-start(bf16[16,96,128]{2,1,0:T(8,128)(2,1)} %get-tuple-element.9), calls=%async_computation.2 | async-start | bytes 786432 | tf_op jit(solution)/shard_map/all_to_all | solution.py:222
  70.6 3.7 %backward_tile.1 = bf16[8,128,128]{2,1,0:T(8,128)(2,1)} custom-call(s32[64]{0:T(128)S(1)} %copy-done.1, s32[3]{0:T(128)S(1)} %pad_add_fusion.place, bf16[8,128,128]{2,1,0:T(8,128)(2,1)S(1)} %bitcast.15, bf16[8,128,128]{2,1,0:T(8,128)(2,1)S(1)} %all-to-all-done.kv_ref, bf16[8,240,128]{2,1,0:T(8,128)(2,1)S(1)} %all_to_all.20.parts_ref), custom_call_target="tpu_custom_call" | custom-call | tf_op jit(solution)/shard_map/backward_tile/pallas_call | solution.py:298
  74.3 10.8 %all-to-all-done.2.parts_ref = bf16[16,96,128]{2,1,0:T(8,128)(2,1)S(1)} async-done(((bf16[16,96,128]{2,1,0:T(8,128)(2,1)}), bf16[16,96,128]{2,1,0:T(8,128)(2,1)S(1)}, u32[]{:S(2)}, u32[]{:S(2)}) %all-to-all-start.2) | async-done | bytes 393248 | tf_op jit(solution)/shard_map/all_to_all | solution.py:222
  85.1 7.0 %all-to-all-start.3 = ((bf16[8,128,128]{2,1,0:T(8,128)(2,1)}), bf16[8,128,128]{2,1,0:T(8,128)(2,1)S(1)}, u32[]{:S(2)}, u32[]{:S(2)}) async-start(bf16[8,128,128]{2,1,0:T(8,128)(2,1)} %backward_tile.1), calls=%async_computation.3 | async-start | bytes 524288 | tf_op jit(solution)/shard_map/all_to_all | solution.py:222
  92.1 11.6 %all-gather.1 = bf16[64,32,128]{2,1,0:T(8,128)(2,1)S(1)} all-gather(bf16[16,32,128]{2,1,0:T(8,128)(2,1)S(1)} %slice.4), channel_id=3, replica_groups=mesh['b'=8,'zl'=2,'x'=4,'head'=16] {'x'}, dimensions={0}, use_global_device_ids=true | all-gather | bytes 655360 | tf_op jit(solution)/shard_map/all_gather | solution.py:287
  103.7 1.0 mix.1
  104.7 8.6 %all-to-all-done.3 = bf16[8,128,128]{2,1,0:T(8,128)(2,1)S(1)} async-done(((bf16[8,128,128]{2,1,0:T(8,128)(2,1)}), bf16[8,128,128]{2,1,0:T(8,128)(2,1)S(1)}, u32[]{:S(2)}, u32[]{:S(2)}) %all-to-all-start.3) | async-done | bytes 262176 | tf_op jit(solution)/shard_map/all_to_all | solution.py:222
  113.2 0.7 reduce_sum.12
  (1 shorter events, 0.0 us)
Async XLA Ops:
  3.2 19.3 %copy-start.2 = (bf16[128,128]{1,0:T(8,128)(2,1)S(1)}, bf16[128,128]{1,0:T(8,128)(2,1)}, u32[]{:S(2)}) copy-start(bf16[128,128]{1,0:T(8,128)(2,1)} %get-tuple-element.7) | copy-start | bytes 98308
  3.2 36.5 %all-to-all-start = ((bf16[8,128,128]{2,1,0:T(8,128)(2,1)}), bf16[8,128,128]{2,1,0:T(8,128)(2,1)S(1)}, u32[]{:S(2)}, u32[]{:S(2)}) async-start(bf16[8,128,128]{2,1,0:T(8,128)(2,1)} %get-tuple-element.8), calls=%async_computation | async-start | bytes 524288 | tf_op jit(solution)/shard_map/all_to_all | solution.py:222
  39.6 0.7 copy-start.1
  43.6 12.9 %copy-start = (bf16[1,64,4096]{2,1,0:T(8,128)(2,1)S(1)}, bf16[1,64,4096]{2,1,0:T(8,128)(2,1)}, u32[]{:S(2)}) copy-start(bf16[1,64,4096]{2,1,0:T(8,128)(2,1)} %param.7) | copy-start | bytes 1572868
  58.0 27.1 %all-to-all-start.2 = ((bf16[16,96,128]{2,1,0:T(8,128)(2,1)}), bf16[16,96,128]{2,1,0:T(8,128)(2,1)S(1)}, u32[]{:S(2)}, u32[]{:S(2)}) async-start(bf16[16,96,128]{2,1,0:T(8,128)(2,1)} %get-tuple-element.9), calls=%async_computation.2 | async-start | bytes 786432 | tf_op jit(solution)/shard_map/all_to_all | solution.py:222
  85.1 28.1 %all-to-all-start.3 = ((bf16[8,128,128]{2,1,0:T(8,128)(2,1)}), bf16[8,128,128]{2,1,0:T(8,128)(2,1)S(1)}, u32[]{:S(2)}, u32[]{:S(2)}) async-start(bf16[8,128,128]{2,1,0:T(8,128)(2,1)} %backward_tile.1), calls=%async_computation.3 | async-start | bytes 524288 | tf_op jit(solution)/shard_map/all_to_all | solution.py:222

commit v5 on v4

--- a/solution.py
+++ b/solution.py
@@ -15,8 +15,10 @@
 STAT_ROWS = 48
 OUT_ROWS = STATS + STAT_ROWS
 QUARTERS = 4
-WIDE = 4
+WIDE = 8
 A = ("zl", "x")
+GATHERED = [(g % 2) * 4 + g // 2 for g in range(GROUP)]
+B_AT, A_AT, X_AT = 64, 65, 66
 NEG = -(2.0**100)
 INTERPRET = False
 PARAMS = pltpu.CompilerParams(vmem_limit_bytes=24 * 1024 * 1024)
@@ -56,8 +58,8 @@
     return high, value - high
 
 
-def forward_tile(order, place, qg_ref, kv_ref, out_ref, keys, values, kv_t, stats, caps):
-    b, a = place[0], place[1]
+def forward_tile(order, qg_ref, kv_ref, out_ref, keys, values, kv_t, stats, caps):
+    b, a = order[B_AT], order[A_AT]
     kv = kv_ref[...].reshape(ROWS, 2 * HD)
     keys[...] = lanes_below(kv)
     values[...] = lanes_below(kv, True)
@@ -73,7 +75,7 @@
         for j in range(GROUP):
             key_block = order[j * GROUP + a]
             cap = jnp.concatenate(
-                [cap_for(caps, key_block, order[b * GROUP + i]) for i in blocks], axis=1
+                [cap_for(caps, key_block, order[b * GROUP + GATHERED[g]]) for g in blocks], axis=1
             )
             masked.append(jnp.minimum(scores[j * TOK : (j + 1) * TOK], cap))
         masked = jnp.concatenate(masked, axis=0)
@@ -88,8 +90,9 @@
         dscore = probs * (dprob - dot / total).astype(BF16)
         centred = nn(kv_t[0:HD, :], dscore)
         rows = (top, *split(total), *split(dot))
-        for i in blocks:
-            lanes = slice((i - first) * TOK, (i - first + 1) * TOK)
+        for g in blocks:
+            i = GATHERED[g]
+            lanes = slice((g - first) * TOK, (g - first + 1) * TOK)
             out_ref[i, OUT : OUT + HD, :] = part[:, lanes].astype(BF16)
             out_ref[i, CENTRED : CENTRED + HD, :] = centred[:, lanes].astype(BF16)
             out_ref[i, PLAIN : PLAIN + HD, :] = summed[0:HD, lanes].astype(BF16)
@@ -136,27 +139,18 @@
     qg_ref[...] = jnp.concatenate([scaled, grad_att], axis=1).astype(BF16)
 
 
-def join_parts(place, parts_ref, weight_ref, out_ref, dq_ref, own):
-    a, quarter = place[1], place[2]
+def join_parts(order, parts_ref, weight_ref, out_ref, own):
+    a, quarter = order[A_AT], order[X_AT]
     rows = HD // QUARTERS
     tops, totals, dots = part_stats(parts_ref)
-    _, total, dot, weights = joined(tops, totals, dots)
-    own[0:GROUP, :] = 1.0 / total
-    for p in range(GROUP):
-        shift = dot - dots[p] / totals[p]
-        own[(2 * p + 1) * GROUP : (2 * p + 2) * GROUP, :] = weights[p]
-        own[(2 * p + 2) * GROUP : (2 * p + 3) * GROUP, :] = weights[p] * shift
+    _, total, _, weights = joined(tops, totals, dots)
+    for p in range(GROUP):
+        own[p * GROUP : (p + 1) * GROUP, :] = weights[p] / total
     attended = jnp.zeros((HD, TOK), F32)
-    dq = jnp.zeros((HD, TOK), F32)
-    for p in range(GROUP):
-        weight = own[pl.ds((2 * p + 1) * GROUP + a, 1), :]
-        shifted = own[pl.ds((2 * p + 2) * GROUP + a, 1), :]
+    for p in range(GROUP):
+        weight = own[pl.ds(p * GROUP + a, 1), :]
         attended += weight * parts_ref[p, OUT : OUT + HD, :].astype(F32)
-        dq += weight * parts_ref[p, CENTRED : CENTRED + HD, :].astype(F32)
-        dq -= shifted * parts_ref[p, PLAIN : PLAIN + HD, :].astype(F32)
-    scale = own[pl.ds(a, 1), :]
-    dq_ref[...] = (dq * (scale * HD**-0.5)).astype(BF16)
-    out = (attended * scale).astype(BF16)
+    out = attended.astype(BF16)
     for h in range(out_ref.shape[0]):
         out_ref[h, 0:HD, :] = out
     own_rows = weight_ref[pl.ds(pl.multiple_of(quarter * rows, rows), rows), :]
@@ -167,8 +161,22 @@
             out_ref[h, first : first + rows, :] = own_rows[:, column : column + TOK]
 
 
-def mix(parts_ref, weight_ref, out_ref, side):
-    heads = parts_ref.shape[0]
+def mix(order, parts_ref, mixed_ref, weight_ref, out_ref, dq_ref, side, own):
+    a = order[A_AT]
+    tops, totals, dots = part_stats(parts_ref)
+    _, total, dot, weights = joined(tops, totals, dots)
+    for p in range(GROUP):
+        scaled = weights[p] / total * HD**-0.5
+        own[2 * p * GROUP : (2 * p + 1) * GROUP, :] = scaled
+        own[(2 * p + 1) * GROUP : (2 * p + 2) * GROUP, :] = scaled * (dot - dots[p] / totals[p])
+    dq = jnp.zeros((HD, TOK), F32)
+    for p in range(GROUP):
+        weight = own[pl.ds(2 * p * GROUP + a, 1), :]
+        shifted = own[pl.ds((2 * p + 1) * GROUP + a, 1), :]
+        dq += weight * parts_ref[p, CENTRED : CENTRED + HD, :].astype(F32)
+        dq -= shifted * parts_ref[p, PLAIN : PLAIN + HD, :].astype(F32)
+    dq_ref[...] = dq.astype(BF16)
+    heads = mixed_ref.shape[0]
     rows = HD // QUARTERS
     for h in range(heads):
         for quarter in range(QUARTERS):
@@ -177,21 +185,21 @@
                 side[first : first + rows, half * TOK : (half + 1) * TOK] = weight_ref[
                     quarter, h, half * rows : (half + 1) * rows, :
                 ]
-    attended = parts_ref[:, 0:HD, :].reshape(heads * HD, TOK)
+    attended = mixed_ref[:, 0:HD, :].reshape(heads * HD, TOK)
     out_ref[...] = lax.dot_general(
         attended, side[...], (((0,), (0,)), ((), ())), preferred_element_type=F32
     ).astype(BF16)
 
 
 def backward_tile(
-    order, place, qg_ref, kv_ref, parts_ref, dkv_ref, query_part, grad_part, norm_dot, caps
+    order, qg_ref, kv_ref, parts_ref, dkv_ref, query_part, grad_part, norm_dot, caps
 ):
-    b, a = place[0], place[1]
+    b, a = order[B_AT], order[A_AT]
     top, total, dot, _ = joined(*part_stats(parts_ref))
     log_total = top + jnp.log(total)
-    for i in range(GROUP):
-        norm_dot[0:1, i * TOK : (i + 1) * TOK] = log_total[i : i + 1]
-        norm_dot[1:2, i * TOK : (i + 1) * TOK] = dot[i : i + 1]
+    for g, i in enumerate(GATHERED):
+        norm_dot[0:1, g * TOK : (g + 1) * TOK] = log_total[i : i + 1]
+        norm_dot[1:2, g * TOK : (g + 1) * TOK] = dot[i : i + 1]
     qg = qg_ref[...].reshape(ROWS, 2 * HD)
     query_part[...] = lanes_below(qg)
     grad_part[...] = lanes_below(qg, True)
@@ -200,7 +208,7 @@
         kv = kv_ref[j]
         key_block = order[j * GROUP + a]
         cap = jnp.concatenate(
-            [cap_for(caps, key_block, order[b * GROUP + i]) for i in range(GROUP)], axis=1
+            [cap_for(caps, key_block, order[b * GROUP + i]) for i in GATHERED], axis=1
         )
         masked = jnp.minimum(nt(kv, query_part[...]), cap)
         probs = jnp.exp(masked - norm_dot[0:1, :]).astype(BF16)
@@ -224,9 +232,8 @@
 
 def local(queries, keys_values, out_weight, out_grad, block_order):
     heads = lax.axis_size("head")
-    place = jnp.stack(
-        [lax.axis_index("b"), lax.axis_index(A), lax.axis_index("x")]
-    ).astype(jnp.int32)
+    place = [lax.axis_index("b"), lax.axis_index(A), lax.axis_index("x")]
+    order = jnp.concatenate([block_order, jnp.stack(place).astype(jnp.int32)])
     weight = out_weight[0]
     columns = weight.shape[1] // heads
     query_grad, kv_copies = pl.pallas_call(
@@ -248,15 +255,14 @@
         name="prepare",
     )(jnp.transpose(queries[:, 0]), keys_values[:, 0], weight, out_grad)
     kv_group = exchange(kv_copies, "b")
-    qg_group = query_grad
+    qg_group = lax.all_gather(query_grad, "zl", tiled=True)
     for pairs in ([[0, 1], [2, 3]], [[0, 3], [1, 2]]):
         qg_group = lax.all_gather(qg_group, "x", tiled=True, axis_index_groups=pairs)
-    qg_group = lax.all_gather(qg_group, "zl")
     qg_group = qg_group.reshape(GROUP, TOK, 2 * HD)
     parts = pl.pallas_call(
         forward_tile,
         out_shape=jax.ShapeDtypeStruct((GROUP, OUT_ROWS, TOK), BF16),
-        in_specs=[smem(), smem(), vmem(), vmem()],
+        in_specs=[smem(), vmem(), vmem()],
         out_specs=vmem(),
         scratch_shapes=[
             pltpu.VMEM((ROWS, 2 * HD), BF16),
@@ -268,37 +274,40 @@
         interpret=INTERPRET,
         compiler_params=PARAMS,
         name="forward_tile",
-    )(block_order, place, qg_group, kv_group)
+    )(order, qg_group, kv_group)
     parts = exchange(parts, A)
-    mixed_parts, grad_queries = pl.pallas_call(
+    mixed_parts = pl.pallas_call(
         join_parts,
+        out_shape=jax.ShapeDtypeStruct((heads, HD + HD // QUARTERS * 2, TOK), BF16),
+        in_specs=[smem(), vmem(), vmem()],
+        out_specs=vmem(),
+        scratch_shapes=[pltpu.VMEM((GROUP * GROUP, TOK), F32)],
+        interpret=INTERPRET,
+        compiler_params=PARAMS,
+        name="join_parts",
+    )(order, parts, weight)
+    mixed_parts = exchange(mixed_parts, "head")
+    quarters = lax.all_gather(mixed_parts[:, HD:], "x")
+    mixed_out, grad_queries = pl.pallas_call(
+        mix,
         out_shape=(
-            jax.ShapeDtypeStruct((heads, HD + HD // QUARTERS * 2, TOK), BF16),
+            jax.ShapeDtypeStruct((TOK, columns), BF16),
             jax.ShapeDtypeStruct((HD, TOK), BF16),
         ),
-        in_specs=[smem(), vmem(), vmem()],
+        in_specs=[smem(), vmem(), vmem(), vmem()],
         out_specs=(vmem(), vmem()),
-        scratch_shapes=[pltpu.VMEM(((2 * GROUP + 1) * GROUP, TOK), F32)],
-        interpret=INTERPRET,
-        compiler_params=PARAMS,
-        name="join_parts",
-    )(place, parts, weight)
-    mixed_parts = exchange(mixed_parts, "head")
-    quarters = lax.all_gather(mixed_parts[:, HD:], "x")
-    mixed_out = pl.pallas_call(
-        mix,
-        out_shape=jax.ShapeDtypeStruct((TOK, columns), BF16),
-        in_specs=[vmem(), vmem()],
-        out_specs=vmem(),
-        scratch_shapes=[pltpu.VMEM((heads * HD, columns), BF16)],
+        scratch_shapes=[
+            pltpu.VMEM((heads * HD, columns), BF16),
+            pltpu.VMEM((2 * GROUP * GROUP, TOK), F32),
+        ],
         interpret=INTERPRET,
         compiler_params=PARAMS,
         name="mix",
-    )(mixed_parts, quarters)
+    )(order, parts, mixed_parts, quarters)
     dkv = pl.pallas_call(
         backward_tile,
         out_shape=jax.ShapeDtypeStruct((GROUP, TOK, 2 * HD), BF16),
-        in_specs=[smem(), smem(), vmem(), vmem(), vmem()],
+        in_specs=[smem(), vmem(), vmem(), vmem()],
         out_specs=vmem(),
         scratch_shapes=[
             pltpu.VMEM((ROWS, 2 * HD), BF16),
@@ -309,7 +318,7 @@
         interpret=INTERPRET,
         compiler_params=PARAMS,
         name="backward_tile",
-    )(block_order, place, qg_group, kv_group, parts)
+    )(order, qg_group, kv_group, parts)
     dkv = exchange(dkv, "b")
     grad_keys_values = jnp.sum(dkv.astype(F32), axis=0).astype(BF16)[:, None]
     return (mixed_out, jnp.transpose(grad_queries)[:, None], grad_keys_values)

time: 114 us -> 123 us (1.079)
  starting transfers between devices: 38.9 us -> 45.8 us
  blocking collectives: 41.5 us -> 42.8 us
    all_to_all x3, starting transfers between devices: 38.9 us -> 45.8 us  [exchange(): return lax.all_to_all(value, axis, 0, 0, tiled=True)]
    all_gather x1, blocking collectives: 8.27 us -> 10.5 us  [local(): qg_group = lax.all_gather(query_grad, 'zl', tiled=True)]
    all_to_all x1, blocking collectives: 12.9 us -> 11 us  [exchange(): return lax.all_to_all(value, axis, 0, 0, tiled=True)]
  transfers between devices with their start and end apart: 3 -> 3, of which waited for: 3 -> 2; matrix products, arithmetic and copies ran while one was open for 0% -> 0% of each run, Pallas kernels for 4% -> 4%
where the time goes in v5:
time: 123 us; the launch traced here: 122 us
  starting transfers between devices  45.8 us (37%)
  blocking collectives  42.8 us (35%)
  waiting for transfers between devices  18.8 us (15%)
  Pallas kernels  12.5 us (10%)
    all_to_all x3, starting transfers between devices, exchange(): return lax.all_to_all(value, axis, 0, 0, tiled=True)  45.8 us
    all_to_all x3, waiting for transfers between devices, exchange(): return lax.all_to_all(value, axis, 0, 0, tiled=True)  18.8 us
    all_gather x1, blocking collectives, local(): quarters = lax.all_gather(mixed_parts[:, HD:], 'x')  11.6 us
    all_to_all x1, blocking collectives, exchange(): return lax.all_to_all(value, axis, 0, 0, tiled=True)  11 us
    all_gather x1, blocking collectives, local(): qg_group = lax.all_gather(query_grad, 'zl', tiled=True)  10.5 us
    all_gather x2, blocking collectives, local(): lax.all_gather(qg_group, 'x', tiled=True, axis_index_groups=pairs)  9.74 us
    pallas_call x1, Pallas kernels, local(): pl.pallas_call(backward_tile, out_shape=jax.ShapeDtypeStruct((GROUP, TOK,...  3.75 us
    pallas_call x1, Pallas kernels, local(): pl.pallas_call(forward_tile, out_shape=jax.ShapeDtypeStruct((GROUP, OUT_R...  3.33 us
  transfers between devices with their start and end apart: 3, of which 2 were waited for; matrix products, arithmetic and copies ran while one was open for 0% of the time, Pallas kernels for 4%

profile of v5, /device:TPU:1, one launch (start us, length us, event | category | flops | bytes accessed | tf_op | source)
XLA Modules:
  0.0 122.0 jit_solution(14925567158232101468)
XLA Ops:
  0.6 2.5 %prepare.1 = (bf16[128,128]{1,0:T(8,128)(2,1)}, bf16[8,128,128]{2,1,0:T(8,128)(2,1)}) custom-call(bf16[64,128]{1,0:T(8,128)(2,1)} %bitcast.21, bf16[128,128]{1,0:T(8,128)(2,1)} %bitcast.19, bf16[64,4096]{1,0:T(8,128)(2,1)} %bitcast.16, bf16[128,4096]{1,0:T(8,128)(2,1)} %grad_hbm.1), custom_call_target="tpu_custom_call" | custom-call | tf_op jit(solution)/shard_map/prepare/pallas_call | solution.py:239
  3.2 0.0 copy-start.1
  3.2 19.3 %all-to-all-start = ((bf16[8,128,128]{2,1,0:T(8,128)(2,1)}), bf16[8,128,128]{2,1,0:T(8,128)(2,1)S(1)}, u32[]{:S(2)}, u32[]{:S(2)}) async-start(bf16[8,128,128]{2,1,0:T(8,128)(2,1)} %get-tuple-element.8), calls=%async_computation | async-start | bytes 524288 | tf_op jit(solution)/shard_map/all_to_all | solution.py:230
  22.5 0.0 copy-done.1
  22.5 10.5 %all_gather.15 = bf16[256,128]{1,0:T(8,128)(2,1)S(1)} all-gather(bf16[128,128]{1,0:T(8,128)(2,1)S(1)} %copy-done.1), channel_id=1, replica_groups=mesh['b'=8,'zl'=2,'x'=4,'head'=16] {'zl'}, dimensions={0}, use_global_device_ids=true | all-gather | bytes 98304 | tf_op jit(solution)/shard_map/all_gather | solution.py:258
  33.0 3.8 %all_gather.16 = bf16[512,128]{1,0:T(8,128)(2,1)S(1)} all-gather(bf16[256,128]{1,0:T(8,128)(2,1)S(1)} %all_gather.15), channel_id=1, replica_groups={{0,16},{32,48},{1,17},{33,49},{2,18},{34,50},{3,19},{35,51},{4,20},{36,..., dimensions={0}, use_global_device_ids=true | all-gather | bytes 196608 | tf_op jit(solution)/shard_map/all_gather | solution.py:260
  36.7 6.0 %all_gather.17 = bf16[1024,128]{1,0:T(8,128)(2,1)S(1)} all-gather(bf16[512,128]{1,0:T(8,128)(2,1)S(1)} %all_gather.16), channel_id=1, replica_groups={{0,48},{16,32},{1,49},{17,33},{2,50},{18,34},{3,51},{19,35},{4,52},{20,..., dimensions={0}, use_global_device_ids=true | all-gather | bytes 393216 | tf_op jit(solution)/shard_map/all_gather | solution.py:260
  42.7 0.0 copy-start.2
  42.7 0.7 copy-done.2
  43.4 0.1 pad_add_fusion.order
  43.4 0.0 all-to-all-done.kv_ref
  43.4 3.3 %forward_tile.1 = bf16[8,240,128]{2,1,0:T(8,128)(2,1)S(1)} custom-call(s32[67]{0:T(128)S(1)} %pad_add_fusion.order, bf16[8,128,128]{2,1,0:T(8,128)(2,1)S(1)} %bitcast.14, bf16[8,128,128]{2,1,0:T(8,128)(2,1)S(1)} %all-to-all-done.kv_ref), custom_call_target="tpu_custom_call" | custom-call | tf_op jit(solution)/shard_map/forward_tile/pallas_call | solution.py:262
  46.8 0.0 copy-start
  46.8 11.0 %all_to_all.20.parts_ref = bf16[8,240,128]{2,1,0:T(8,128)(2,1)S(1)} all-to-all(bf16[8,240,128]{2,1,0:T(8,128)(2,1)S(1)} %forward_tile.1), channel_id=1, replica_groups=mesh['b'=8,'zl'=2,'x'=4,'head'=16] {'zl','x'}, dimensions={0} | all-to-all | bytes 983040 | tf_op jit(solution)/shard_map/all_to_all | solution.py:230
  57.8 0.0 copy-done
  57.8 1.4 %join_parts.1 = bf16[16,96,128]{2,1,0:T(8,128)(2,1)} custom-call(s32[67]{0:T(128)S(1)} %pad_add_fusion.order, bf16[8,240,128]{2,1,0:T(8,128)(2,1)S(1)} %all_to_all.20.parts_ref, bf16[64,4096]{1,0:T(8,128)(2,1)S(1)} %bitcast.17), custom_call_target="tpu_custom_call" | custom-call | tf_op jit(solution)/shard_map/join_parts/pallas_call | solution.py:279
  59.2 13.7 %all-to-all-start.2 = ((bf16[16,96,128]{2,1,0:T(8,128)(2,1)}), bf16[16,96,128]{2,1,0:T(8,128)(2,1)S(1)}, u32[]{:S(2)}, u32[]{:S(2)}) async-start(bf16[16,96,128]{2,1,0:T(8,128)(2,1)} %join_parts.1), calls=%async_computation.2 | async-start | bytes 786432 | tf_op jit(solution)/shard_map/all_to_all | solution.py:230
  72.9 3.7 %backward_tile.1 = bf16[8,128,128]{2,1,0:T(8,128)(2,1)} custom-call(s32[67]{0:T(128)S(1)} %pad_add_fusion.order, bf16[8,128,128]{2,1,0:T(8,128)(2,1)S(1)} %bitcast.15, bf16[8,128,128]{2,1,0:T(8,128)(2,1)S(1)} %all-to-all-done.kv_ref, bf16[8,240,128]{2,1,0:T(8,128)(2,1)S(1)} %all_to_all.20.parts_ref), custom_call_target="tpu_custom_call" | custom-call | tf_op jit(solution)/shard_map/backward_tile/pallas_call | solution.py:307
  76.7 10.7 %all-to-all-done.2.mixed_ref = bf16[16,96,128]{2,1,0:T(8,128)(2,1)S(1)} async-done(((bf16[16,96,128]{2,1,0:T(8,128)(2,1)}), bf16[16,96,128]{2,1,0:T(8,128)(2,1)S(1)}, u32[]{:S(2)}, u32[]{:S(2)}) %all-to-all-start.2) | async-done | bytes 393248 | tf_op jit(solution)/shard_map/all_to_all | solution.py:230
  87.4 12.8 %all-to-all-start.3 = ((bf16[8,128,128]{2,1,0:T(8,128)(2,1)}), bf16[8,128,128]{2,1,0:T(8,128)(2,1)S(1)}, u32[]{:S(2)}, u32[]{:S(2)}) async-start(bf16[8,128,128]{2,1,0:T(8,128)(2,1)} %backward_tile.1), calls=%async_computation.3 | async-start | bytes 524288 | tf_op jit(solution)/shard_map/all_to_all | solution.py:230
  100.2 11.6 %all-gather = bf16[64,32,128]{2,1,0:T(8,128)(2,1)S(1)} all-gather(bf16[16,32,128]{2,1,0:T(8,128)(2,1)S(1)} %slice.4), channel_id=2, replica_groups=mesh['b'=8,'zl'=2,'x'=4,'head'=16] {'x'}, dimensions={0}, use_global_device_ids=true | all-gather | bytes 655360 | tf_op jit(solution)/shard_map/all_gather | solution.py:290
  111.8 1.5 %mix.1 = (bf16[128,256]{1,0:T(8,128)(2,1)}, bf16[64,128]{1,0:T(8,128)(2,1)}) custom-call(s32[67]{0:T(128)S(1)} %pad_add_fusion.order, bf16[8,240,128]{2,1,0:T(8,128)(2,1)S(1)} %all_to_all.20.parts_ref, bf16[16,96,128]{2,1,0:T(8,128)(2,1)S(1)} %all-to-all-done.2.mixed_ref, bf16[4,16,32,128]{3,2,1,0:T(8,128)(2,1)S(1)} %bitcast.18), custom_call_target="tpu_custom_call" | custom-call | tf_op jit(solution)/shard_map/mix/pallas_call | solution.py:291
  113.3 8.0 %all-to-all-done.3 = bf16[8,128,128]{2,1,0:T(8,128)(2,1)S(1)} async-done(((bf16[8,128,128]{2,1,0:T(8,128)(2,1)}), bf16[8,128,128]{2,1,0:T(8,128)(2,1)S(1)}, u32[]{:S(2)}, u32[]{:S(2)}) %all-to-all-start.3) | async-done | bytes 262176 | tf_op jit(solution)/shard_map/all_to_all | solution.py:230
  121.4 0.7 reduce_sum.12
  (1 shorter events, 0.0 us)
Async XLA Ops:
  3.2 19.3 %copy-start.1 = (bf16[128,128]{1,0:T(8,128)(2,1)S(1)}, bf16[128,128]{1,0:T(8,128)(2,1)}, u32[]{:S(2)}) copy-start(bf16[128,128]{1,0:T(8,128)(2,1)} %get-tuple-element.7) | copy-start | bytes 98308
  3.2 40.2 %all-to-all-start = ((bf16[8,128,128]{2,1,0:T(8,128)(2,1)}), bf16[8,128,128]{2,1,0:T(8,128)(2,1)S(1)}, u32[]{:S(2)}, u32[]{:S(2)}) async-start(bf16[8,128,128]{2,1,0:T(8,128)(2,1)} %get-tuple-element.8), calls=%async_computation | async-start | bytes 524288 | tf_op jit(solution)/shard_map/all_to_all | solution.py:230
  42.7 0.7 copy-start.2
  46.8 11.0 %copy-start = (bf16[1,64,4096]{2,1,0:T(8,128)(2,1)S(1)}, bf16[1,64,4096]{2,1,0:T(8,128)(2,1)}, u32[]{:S(2)}) copy-start(bf16[1,64,4096]{2,1,0:T(8,128)(2,1)} %param.7) | copy-start | bytes 1572868
  59.2 28.2 %all-to-all-start.2 = ((bf16[16,96,128]{2,1,0:T(8,128)(2,1)}), bf16[16,96,128]{2,1,0:T(8,128)(2,1)S(1)}, u32[]{:S(2)}, u32[]{:S(2)}) async-start(bf16[16,96,128]{2,1,0:T(8,128)(2,1)} %join_parts.1), calls=%async_computation.2 | async-start | bytes 786432 | tf_op jit(solution)/shard_map/all_to_all | solution.py:230
  87.4 33.9 %all-to-all-start.3 = ((bf16[8,128,128]{2,1,0:T(8,128)(2,1)}), bf16[8,128,128]{2,1,0:T(8,128)(2,1)S(1)}, u32[]{:S(2)}, u32[]{:S(2)}) async-start(bf16[8,128,128]{2,1,0:T(8,128)(2,1)} %backward_tile.1), calls=%async_computation.3 | async-start | bytes 524288 | tf_op jit(solution)/shard_map/all_to_all | solution.py:230

commit v6 on v5

--- a/solution.py
+++ b/solution.py
@@ -17,7 +17,8 @@
 QUARTERS = 4
 WIDE = 8
 A = ("zl", "x")
-GATHERED = [(g % 2) * 4 + g // 2 for g in range(GROUP)]
+HEAD = ("y", "c")
+GATHERED = range(GROUP)
 B_AT, A_AT, X_AT = 64, 65, 66
 NEG = -(2.0**100)
 INTERPRET = False
@@ -151,14 +152,13 @@
         weight = own[pl.ds(p * GROUP + a, 1), :]
         attended += weight * parts_ref[p, OUT : OUT + HD, :].astype(F32)
     out = attended.astype(BF16)
-    for h in range(out_ref.shape[0]):
-        out_ref[h, 0:HD, :] = out
     own_rows = weight_ref[pl.ds(pl.multiple_of(quarter * rows, rows), rows), :]
-    for h in range(out_ref.shape[0]):
-        for half in range(2):
-            first = HD + half * rows
-            column = (2 * h + half) * TOK
-            out_ref[h, first : first + rows, :] = own_rows[:, column : column + TOK]
+    for y in range(out_ref.shape[0]):
+        out_ref[y, 0:HD, :] = out
+        for k in range(4):
+            first = HD + k * rows
+            column = (4 * y + k) * TOK
+            out_ref[y, first : first + rows, :] = own_rows[:, column : column + TOK]
 
 
 def mix(order, parts_ref, mixed_ref, weight_ref, out_ref, dq_ref, side, own):
@@ -176,16 +176,17 @@
         dq += weight * parts_ref[p, CENTRED : CENTRED + HD, :].astype(F32)
         dq -= shifted * parts_ref[p, PLAIN : PLAIN + HD, :].astype(F32)
     dq_ref[...] = dq.astype(BF16)
-    heads = mixed_ref.shape[0]
+    cores, chips = mixed_ref.shape[:2]
     rows = HD // QUARTERS
-    for h in range(heads):
-        for quarter in range(QUARTERS):
-            first = h * HD + quarter * rows
-            for half in range(2):
-                side[first : first + rows, half * TOK : (half + 1) * TOK] = weight_ref[
-                    quarter, h, half * rows : (half + 1) * rows, :
-                ]
-    attended = mixed_ref[:, 0:HD, :].reshape(heads * HD, TOK)
+    for c in range(cores):
+        for y in range(chips):
+            for quarter in range(QUARTERS):
+                first = (c * chips + y) * HD + quarter * rows
+                for half in range(2):
+                    side[first : first + rows, half * TOK : (half + 1) * TOK] = weight_ref[
+                        quarter, c, y, half * rows : (half + 1) * rows, :
+                    ]
+    attended = mixed_ref[:, :, 0:HD, :].reshape(cores * chips * HD, TOK)
     out_ref[...] = lax.dot_general(
         attended, side[...], (((0,), (0,)), ((), ())), preferred_element_type=F32
     ).astype(BF16)
@@ -231,8 +232,9 @@
 
 
 def local(queries, keys_values, out_weight, out_grad, block_order):
-    heads = lax.axis_size("head")
-    place = [lax.axis_index("b"), lax.axis_index(A), lax.axis_index("x")]
+    chips = lax.axis_size("y")
+    heads = chips * lax.axis_size("c")
+    place = [lax.axis_index(name) for name in ("b", A, "x")]
     order = jnp.concatenate([block_order, jnp.stack(place).astype(jnp.int32)])
     weight = out_weight[0]
     columns = weight.shape[1] // heads
@@ -255,9 +257,10 @@
         name="prepare",
     )(jnp.transpose(queries[:, 0]), keys_values[:, 0], weight, out_grad)
     kv_group = exchange(kv_copies, "b")
-    qg_group = lax.all_gather(query_grad, "zl", tiled=True)
+    qg_group = query_grad
     for pairs in ([[0, 1], [2, 3]], [[0, 3], [1, 2]]):
         qg_group = lax.all_gather(qg_group, "x", tiled=True, axis_index_groups=pairs)
+    qg_group = lax.all_gather(qg_group, "zl")
     qg_group = qg_group.reshape(GROUP, TOK, 2 * HD)
     parts = pl.pallas_call(
         forward_tile,
@@ -278,7 +281,7 @@
     parts = exchange(parts, A)
     mixed_parts = pl.pallas_call(
         join_parts,
-        out_shape=jax.ShapeDtypeStruct((heads, HD + HD // QUARTERS * 2, TOK), BF16),
+        out_shape=jax.ShapeDtypeStruct((chips, 2 * HD, TOK), BF16),
         in_specs=[smem(), vmem(), vmem()],
         out_specs=vmem(),
         scratch_shapes=[pltpu.VMEM((GROUP * GROUP, TOK), F32)],
@@ -286,8 +289,13 @@
         compiler_params=PARAMS,
         name="join_parts",
     )(order, parts, weight)
-    mixed_parts = exchange(mixed_parts, "head")
-    quarters = lax.all_gather(mixed_parts[:, HD:], "x")
+    mixed_parts = exchange(mixed_parts, "y")
+    every_head = lax.all_gather(mixed_parts, "c")
+    own_side = 2 * HD // QUARTERS
+    quarters = lax.dynamic_slice_in_dim(
+        every_head, HD + lax.axis_index("c") * own_side, own_side, axis=2
+    )
+    quarters = lax.all_gather(quarters, "x")
     mixed_out, grad_queries = pl.pallas_call(
         mix,
         out_shape=(
@@ -303,7 +311,7 @@
         interpret=INTERPRET,
         compiler_params=PARAMS,
         name="mix",
-    )(order, parts, mixed_parts, quarters)
+    )(order, parts, every_head, quarters)
     dkv = pl.pallas_call(
         backward_tile,
         out_shape=jax.ShapeDtypeStruct((GROUP, TOK, 2 * HD), BF16),
@@ -325,13 +333,13 @@
 
 
 def solution(mesh):
-    finer = Mesh(mesh.devices.reshape(GROUP, 2, 4, mesh.shape["head"]), (*SEQ, "head"))
+    finer = Mesh(mesh.devices.reshape(GROUP, 2, 4, mesh.shape["head"] // 2, 2), (*SEQ, *HEAD))
     in_specs = (
-        P(SEQ, "head", None),
-        P(SEQ, "head", None),
-        P("head", None, None),
+        P(SEQ, HEAD, None),
+        P(SEQ, HEAD, None),
+        P(HEAD, None, None),
         P(SEQ, None),
         P(),
     )
-    out_specs = (P(SEQ, "head"), P(SEQ, "head", None), P(SEQ, "head", None))
+    out_specs = (P(SEQ, HEAD), P(SEQ, HEAD, None), P(SEQ, HEAD, None))
     return jax.shard_map(local, mesh=finer, in_specs=in_specs, out_specs=out_specs, check_vma=False)

time: 123 us -> 104 us (0.85)
  the two profiles are of different devices: /device:TPU:1 before, /device:TPU:6 now
where the time goes in v6:
time: 104 us
  blocking collectives  45.5 us (44%)
  starting transfers between devices  33.1 us (32%)
  Pallas kernels  12.4 us (12%)
  waiting for transfers between devices  10.4 us (10%)
    all_to_all x3, starting transfers between devices, exchange(): return lax.all_to_all(value, axis, 0, 0, tiled=True)  33.1 us
    all_to_all x1, blocking collectives, exchange(): return lax.all_to_all(value, axis, 0, 0, tiled=True)  13.8 us
    all_gather x1, blocking collectives, local(): quarters = lax.all_gather(quarters, 'x')  12.8 us
    all_gather x2, blocking collectives, local(): lax.all_gather(qg_group, 'x', tiled=True, axis_index_groups=pairs)  10.7 us
    all_to_all x3, waiting for transfers between devices, exchange(): return lax.all_to_all(value, axis, 0, 0, tiled=True)  10.4 us
    all_gather x1, blocking collectives, local(): qg_group = lax.all_gather(qg_group, 'zl')  6.07 us
    pallas_call x1, Pallas kernels, local(): pl.pallas_call(backward_tile, out_shape=jax.ShapeDtypeStruct((GROUP, TOK,...  3.72 us
    pallas_call x1, Pallas kernels, local(): pl.pallas_call(forward_tile, out_shape=jax.ShapeDtypeStruct((GROUP, OUT_R...  3.32 us
  transfers between devices with their start and end apart: 3, of which 3 were waited for; matrix products, arithmetic and copies ran while one was open for 0% of the time, Pallas kernels for 5%

profile of v6, /device:TPU:6, one launch (start us, length us, event | category | flops | bytes accessed | tf_op | source)
XLA Modules:
  0.0 103.5 jit_solution(18217153470364659644)
XLA Ops:
  0.6 2.5 %prepare.1 = (bf16[128,128]{1,0:T(8,128)(2,1)}, bf16[8,128,128]{2,1,0:T(8,128)(2,1)}) custom-call(bf16[64,128]{1,0:T(8,128)(2,1)} %bitcast.24, bf16[128,128]{1,0:T(8,128)(2,1)} %bitcast.22, bf16[64,4096]{1,0:T(8,128)(2,1)} %bitcast.19, bf16[128,4096]{1,0:T(8,128)(2,1)} %grad_hbm.1), custom_call_target="tpu_custom_call" | custom-call | tf_op jit(solution)/shard_map/prepare/pallas_call | solution.py:241
  3.2 0.0 copy-start.1
  3.2 18.8 %all-to-all-start = ((bf16[8,128,128]{2,1,0:T(8,128)(2,1)}), bf16[8,128,128]{2,1,0:T(8,128)(2,1)S(1)}, u32[]{:S(2)}, u32[]{:S(2)}) async-start(bf16[8,128,128]{2,1,0:T(8,128)(2,1)} %get-tuple-element.8), calls=%async_computation | async-start | bytes 524288 | tf_op jit(solution)/shard_map/all_to_all | solution.py:231
  22.0 0.0 copy-done.1
  22.0 4.6 %all_gather.24 = bf16[256,128]{1,0:T(8,128)(2,1)S(1)} all-gather(bf16[128,128]{1,0:T(8,128)(2,1)S(1)} %copy-done.1), channel_id=1, replica_groups={{0,16},{32,48},{1,17},{33,49},{2,18},{34,50},{3,19},{35,51},{4,20},{36,..., dimensions={0}, use_global_device_ids=true | all-gather | bytes 98304 | tf_op jit(solution)/shard_map/all_gather | solution.py:262
  26.5 6.1 %all_gather.25 = bf16[512,128]{1,0:T(8,128)(2,1)S(1)} all-gather(bf16[256,128]{1,0:T(8,128)(2,1)S(1)} %all_gather.24), channel_id=1, replica_groups={{0,48},{16,32},{1,49},{17,33},{2,50},{18,34},{3,51},{19,35},{4,52},{20,..., dimensions={0}, use_global_device_ids=true | all-gather | bytes 196608 | tf_op jit(solution)/shard_map/all_gather | solution.py:262
  32.7 6.1 %all-gather = bf16[1024,128]{1,0:T(8,128)(2,1)S(1)} all-gather(bf16[512,128]{1,0:T(8,128)(2,1)S(1)} %all_gather.25), channel_id=2, replica_groups=mesh['b'=8,'zl'=2,'x'=4,'y'=8,'c'=2] {'zl'}, dimensions={0}, use_global_device_ids=true | all-gather | bytes 393216 | tf_op jit(solution)/shard_map/all_gather | solution.py:263
  38.7 0.0 copy-start.2
  38.7 0.7 copy-done.2
  39.4 0.1 pad_add_fusion.order
  39.5 2.0 %all-to-all-done.kv_ref = bf16[8,128,128]{2,1,0:T(8,128)(2,1)S(1)} async-done(((bf16[8,128,128]{2,1,0:T(8,128)(2,1)}), bf16[8,128,128]{2,1,0:T(8,128)(2,1)S(1)}, u32[]{:S(2)}, u32[]{:S(2)}) %all-to-all-start) | async-done | bytes 262176 | tf_op jit(solution)/shard_map/all_to_all | solution.py:231
  41.4 3.3 %forward_tile.1 = bf16[8,240,128]{2,1,0:T(8,128)(2,1)S(1)} custom-call(s32[67]{0:T(128)S(1)} %pad_add_fusion.order, bf16[8,128,128]{2,1,0:T(8,128)(2,1)S(1)} %bitcast.17, bf16[8,128,128]{2,1,0:T(8,128)(2,1)S(1)} %all-to-all-done.kv_ref), custom_call_target="tpu_custom_call" | custom-call | tf_op jit(solution)/shard_map/forward_tile/pallas_call | solution.py:265
  44.8 0.0 copy-start
  44.8 13.8 %all_to_all.20.parts_ref = bf16[8,240,128]{2,1,0:T(8,128)(2,1)S(1)} all-to-all(bf16[8,240,128]{2,1,0:T(8,128)(2,1)S(1)} %forward_tile.1), channel_id=1, replica_groups=mesh['b'=8,'zl'=2,'x'=4,'y'=8,'c'=2] {'zl','x'}, dimensions={0} | all-to-all | bytes 983040 | tf_op jit(solution)/shard_map/all_to_all | solution.py:231
  58.6 0.0 copy-done
  58.6 1.3 %join_parts.1 = bf16[8,128,128]{2,1,0:T(8,128)(2,1)} custom-call(s32[67]{0:T(128)S(1)} %pad_add_fusion.order, bf16[8,240,128]{2,1,0:T(8,128)(2,1)S(1)} %all_to_all.20.parts_ref, bf16[64,4096]{1,0:T(8,128)(2,1)S(1)} %bitcast.20), custom_call_target="tpu_custom_call" | custom-call | tf_op jit(solution)/shard_map/join_parts/pallas_call | solution.py:282
  59.9 7.1 %all-to-all-start.2 = ((bf16[8,128,128]{2,1,0:T(8,128)(2,1)}), bf16[8,128,128]{2,1,0:T(8,128)(2,1)S(1)}, u32[]{:S(2)}, u32[]{:S(2)}) async-start(bf16[8,128,128]{2,1,0:T(8,128)(2,1)} %join_parts.1), calls=%async_computation.2 | async-start | bytes 524288 | tf_op jit(solution)/shard_map/all_to_all | solution.py:231
  67.0 3.7 %backward_tile.1 = bf16[8,128,128]{2,1,0:T(8,128)(2,1)} custom-call(s32[67]{0:T(128)S(1)} %pad_add_fusion.order, bf16[8,128,128]{2,1,0:T(8,128)(2,1)S(1)} %bitcast.18, bf16[8,128,128]{2,1,0:T(8,128)(2,1)S(1)} %all-to-all-done.kv_ref, bf16[8,240,128]{2,1,0:T(8,128)(2,1)S(1)} %all_to_all.20.parts_ref), custom_call_target="tpu_custom_call" | custom-call | tf_op jit(solution)/shard_map/backward_tile/pallas_call | solution.py:315
  70.7 6.8 %all-to-all-done.2 = bf16[8,128,128]{2,1,0:T(8,128)(2,1)S(1)} async-done(((bf16[8,128,128]{2,1,0:T(8,128)(2,1)}), bf16[8,128,128]{2,1,0:T(8,128)(2,1)S(1)}, u32[]{:S(2)}, u32[]{:S(2)}) %all-to-all-start.2) | async-done | bytes 262176 | tf_op jit(solution)/shard_map/all_to_all | solution.py:231
  77.5 7.3 %all-to-all-start.3 = ((bf16[8,128,128]{2,1,0:T(8,128)(2,1)}), bf16[8,128,128]{2,1,0:T(8,128)(2,1)S(1)}, u32[]{:S(2)}, u32[]{:S(2)}) async-start(bf16[8,128,128]{2,1,0:T(8,128)(2,1)} %backward_tile.1), calls=%async_computation.3 | async-start | bytes 524288 | tf_op jit(solution)/shard_map/all_to_all | solution.py:231
  84.7 2.2 %all-gather.1 = bf16[16,128,128]{2,1,0:T(8,128)(2,1)S(1)} all-gather(bf16[8,128,128]{2,1,0:T(8,128)(2,1)S(1)} %all-to-all-done.2), channel_id=3, replica_groups=mesh['b'=8,'zl'=2,'x'=4,'y'=8,'c'=2] {'c'}, dimensions={0}, use_global_device_ids=true | all-gather | bytes 786432 | tf_op jit(solution)/shard_map/all_gather | solution.py:293
  86.9 12.8 %all-gather.2 = bf16[8,8,32,128]{3,2,1,0:T(8,128)(2,1)S(1)} all-gather(bf16[2,8,32,128]{3,2,1,0:T(8,128)(2,1)S(1)} %constant_dynamic-slice_fusion), channel_id=4, replica_groups=mesh['b'=8,'zl'=2,'x'=4,'y'=8,'c'=2] {'x'}, dimensions={0}, use_global_device_ids=true | all-gather | bytes 655360 | tf_op jit(solution)/shard_map/all_gather | solution.py:298
  99.7 1.5 %mix.1 = (bf16[128,256]{1,0:T(8,128)(2,1)}, bf16[64,128]{1,0:T(8,128)(2,1)}) custom-call(s32[67]{0:T(128)S(1)} %pad_add_fusion.order, bf16[8,240,128]{2,1,0:T(8,128)(2,1)S(1)} %all_to_all.20.parts_ref, bf16[2,8,128,128]{3,2,1,0:T(8,128)(2,1)S(1)} %bitcast.16, bf16[4,2,8,32,128]{4,3,2,1,0:T(8,128)(2,1)S(1)} %bitcast.21), custom_call_target="tpu_custom_call" | custom-call | tf_op jit(solution)/shard_map/mix/pallas_call | solution.py:299
  101.2 1.7 %all-to-all-done.3 = bf16[8,128,128]{2,1,0:T(8,128)(2,1)S(1)} async-done(((bf16[8,128,128]{2,1,0:T(8,128)(2,1)}), bf16[8,128,128]{2,1,0:T(8,128)(2,1)S(1)}, u32[]{:S(2)}, u32[]{:S(2)}) %all-to-all-start.3) | async-done | bytes 262176 | tf_op jit(solution)/shard_map/all_to_all | solution.py:231
  102.9 0.7 reduce_sum.12
  (1 shorter events, 0.0 us)
Async XLA Ops:
  3.2 18.8 %copy-start.1 = (bf16[128,128]{1,0:T(8,128)(2,1)S(1)}, bf16[128,128]{1,0:T(8,128)(2,1)}, u32[]{:S(2)}) copy-start(bf16[128,128]{1,0:T(8,128)(2,1)} %get-tuple-element.7) | copy-start | bytes 98308
  3.2 38.3 %all-to-all-start = ((bf16[8,128,128]{2,1,0:T(8,128)(2,1)}), bf16[8,128,128]{2,1,0:T(8,128)(2,1)S(1)}, u32[]{:S(2)}, u32[]{:S(2)}) async-start(bf16[8,128,128]{2,1,0:T(8,128)(2,1)} %get-tuple-element.8), calls=%async_computation | async-start | bytes 524288 | tf_op jit(solution)/shard_map/all_to_all | solution.py:231
  38.7 0.7 copy-start.2
  44.8 13.8 %copy-start = (bf16[1,64,4096]{2,1,0:T(8,128)(2,1)S(1)}, bf16[1,64,4096]{2,1,0:T(8,128)(2,1)}, u32[]{:S(2)}) copy-start(bf16[1,64,4096]{2,1,0:T(8,128)(2,1)} %param.7) | copy-start | bytes 1572868
  59.9 17.6 %all-to-all-start.2 = ((bf16[8,128,128]{2,1,0:T(8,128)(2,1)}), bf16[8,128,128]{2,1,0:T(8,128)(2,1)S(1)}, u32[]{:S(2)}, u32[]{:S(2)}) async-start(bf16[8,128,128]{2,1,0:T(8,128)(2,1)} %join_parts.1), calls=%async_computation.2 | async-start | bytes 524288 | tf_op jit(solution)/shard_map/all_to_all | solution.py:231
  77.5 25.4 %all-to-all-start.3 = ((bf16[8,128,128]{2,1,0:T(8,128)(2,1)}), bf16[8,128,128]{2,1,0:T(8,128)(2,1)S(1)}, u32[]{:S(2)}, u32[]{:S(2)}) async-start(bf16[8,128,128]{2,1,0:T(8,128)(2,1)} %backward_tile.1), calls=%async_computation.3 | async-start | bytes 524288 | tf_op jit(solution)/shard_map/all_to_all | solution.py:231

commit v7 on v6

--- a/solution.py
+++ b/solution.py
@@ -12,7 +12,7 @@
 HD = 64
 ROWS = GROUP * TOK
 OUT, CENTRED, PLAIN, STATS = 0, HD, 2 * HD, 3 * HD
-STAT_ROWS = 48
+STAT_ROWS = 32
 OUT_ROWS = STATS + STAT_ROWS
 QUARTERS = 4
 WIDE = 8
@@ -80,23 +80,25 @@
             )
             masked.append(jnp.minimum(scores[j * TOK : (j + 1) * TOK], cap))
         masked = jnp.concatenate(masked, axis=0)
-        top = jnp.max(masked, axis=0, keepdims=True).astype(BF16).astype(F32)
+        top = jnp.max(masked, axis=0, keepdims=True)
         probs = jnp.exp(masked - top).astype(BF16)
         summed = nn(kv_t[...], probs)
         grad_t = jnp.transpose(qg.astype(F32))[HD:, :]
-        part = summed[HD : 2 * HD]
         total = summed[2 * HD : 2 * HD + 1]
+        share = 1.0 / total
+        part = summed[HD : 2 * HD] * share
         dot = jnp.sum(grad_t * part, axis=0, keepdims=True)
         dprob = nt(values[...], qg)
-        dscore = probs * (dprob - dot / total).astype(BF16)
-        centred = nn(kv_t[0:HD, :], dscore)
-        rows = (top, *split(total), *split(dot))
+        dscore = probs * (dprob - dot).astype(BF16)
+        centred = nn(kv_t[0:HD, :], dscore) * share
+        plain = summed[0:HD] * share
+        rows = (*split(top + jnp.log(total)), *split(dot))
         for g in blocks:
             i = GATHERED[g]
             lanes = slice((g - first) * TOK, (g - first + 1) * TOK)
             out_ref[i, OUT : OUT + HD, :] = part[:, lanes].astype(BF16)
             out_ref[i, CENTRED : CENTRED + HD, :] = centred[:, lanes].astype(BF16)
-            out_ref[i, PLAIN : PLAIN + HD, :] = summed[0:HD, lanes].astype(BF16)
+            out_ref[i, PLAIN : PLAIN + HD, :] = plain[:, lanes].astype(BF16)
             for k, row in enumerate(rows):
                 stats[k * GROUP + i : k * GROUP + i + 1, :] = row[:, lanes]
     for i in range(GROUP):
@@ -104,23 +106,23 @@
 
 
 def part_stats(parts_ref):
-    tops, totals, dots = [], [], []
+    logs, dots = [], []
     for p in range(GROUP):
         rows = parts_ref[p, STATS:, :].astype(F32)
-        tops.append(rows[0:GROUP])
-        totals.append(rows[GROUP : 2 * GROUP] + rows[2 * GROUP : 3 * GROUP])
-        dots.append(rows[3 * GROUP : 4 * GROUP] + rows[4 * GROUP : 5 * GROUP])
-    return tops, totals, dots
-
-
-def joined(tops, totals, dots):
-    top = tops[0]
+        logs.append(rows[0:GROUP] + rows[GROUP : 2 * GROUP])
+        dots.append(rows[2 * GROUP : 3 * GROUP] + rows[3 * GROUP :])
+    return logs, dots
+
+
+def joined(logs, dots):
+    top = logs[0]
     for p in range(1, GROUP):
-        top = jnp.maximum(top, tops[p])
-    weights = [jnp.exp(tops[p] - top) for p in range(GROUP)]
-    total = sum(weights[p] * totals[p] for p in range(GROUP))
+        top = jnp.maximum(top, logs[p])
+    weights = [jnp.exp(logs[p] - top) for p in range(GROUP)]
+    total = sum(weights)
+    weights = [weight / total for weight in weights]
     dot = sum(weights[p] * dots[p] for p in range(GROUP))
-    return top, total, dot / total, weights
+    return top + jnp.log(total), dot, weights
 
 
 def prepare(
@@ -143,10 +145,9 @@
 def join_parts(order, parts_ref, weight_ref, out_ref, own):
     a, quarter = order[A_AT], order[X_AT]
     rows = HD // QUARTERS
-    tops, totals, dots = part_stats(parts_ref)
-    _, total, _, weights = joined(tops, totals, dots)
-    for p in range(GROUP):
-        own[p * GROUP : (p + 1) * GROUP, :] = weights[p] / total
+    _, _, weights = joined(*part_stats(parts_ref))
+    for p in range(GROUP):
+        own[p * GROUP : (p + 1) * GROUP, :] = weights[p]
     attended = jnp.zeros((HD, TOK), F32)
     for p in range(GROUP):
         weight = own[pl.ds(p * GROUP + a, 1), :]
@@ -161,21 +162,7 @@
             out_ref[y, first : first + rows, :] = own_rows[:, column : column + TOK]
 
 
-def mix(order, parts_ref, mixed_ref, weight_ref, out_ref, dq_ref, side, own):
-    a = order[A_AT]
-    tops, totals, dots = part_stats(parts_ref)
-    _, total, dot, weights = joined(tops, totals, dots)
-    for p in range(GROUP):
-        scaled = weights[p] / total * HD**-0.5
-        own[2 * p * GROUP : (2 * p + 1) * GROUP, :] = scaled
-        own[(2 * p + 1) * GROUP : (2 * p + 2) * GROUP, :] = scaled * (dot - dots[p] / totals[p])
-    dq = jnp.zeros((HD, TOK), F32)
-    for p in range(GROUP):
-        weight = own[pl.ds(2 * p * GROUP + a, 1), :]
-        shifted = own[pl.ds((2 * p + 1) * GROUP + a, 1), :]
-        dq += weight * parts_ref[p, CENTRED : CENTRED + HD, :].astype(F32)
-        dq -= shifted * parts_ref[p, PLAIN : PLAIN + HD, :].astype(F32)
-    dq_ref[...] = dq.astype(BF16)
+def mix(mixed_ref, weight_ref, out_ref, side):
     cores, chips = mixed_ref.shape[:2]
     rows = HD // QUARTERS
     for c in range(cores):
@@ -193,11 +180,22 @@
 
 
 def backward_tile(
-    order, qg_ref, kv_ref, parts_ref, dkv_ref, query_part, grad_part, norm_dot, caps
+    order, qg_ref, kv_ref, parts_ref, dkv_ref, dq_ref, query_part, grad_part, norm_dot, caps, own
 ):
     b, a = order[B_AT], order[A_AT]
-    top, total, dot, _ = joined(*part_stats(parts_ref))
-    log_total = top + jnp.log(total)
+    logs, dots = part_stats(parts_ref)
+    log_total, dot, weights = joined(logs, dots)
+    for p in range(GROUP):
+        scaled = weights[p] * HD**-0.5
+        own[2 * p * GROUP : (2 * p + 1) * GROUP, :] = scaled
+        own[(2 * p + 1) * GROUP : (2 * p + 2) * GROUP, :] = scaled * (dot - dots[p])
+    dq = jnp.zeros((HD, TOK), F32)
+    for p in range(GROUP):
+        weight = own[pl.ds(2 * p * GROUP + a, 1), :]
+        shifted = own[pl.ds((2 * p + 1) * GROUP + a, 1), :]
+        dq += weight * parts_ref[p, CENTRED : CENTRED + HD, :].astype(F32)
+        dq -= shifted * parts_ref[p, PLAIN : PLAIN + HD, :].astype(F32)
+    dq_ref[...] = dq.astype(BF16)
     for g, i in enumerate(GATHERED):
         norm_dot[0:1, g * TOK : (g + 1) * TOK] = log_total[i : i + 1]
         norm_dot[1:2, g * TOK : (g + 1) * TOK] = dot[i : i + 1]
@@ -296,32 +294,30 @@
         every_head, HD + lax.axis_index("c") * own_side, own_side, axis=2
     )
     quarters = lax.all_gather(quarters, "x")
-    mixed_out, grad_queries = pl.pallas_call(
+    mixed_out = pl.pallas_call(
         mix,
+        out_shape=jax.ShapeDtypeStruct((TOK, columns), BF16),
+        in_specs=[vmem(), vmem()],
+        out_specs=vmem(),
+        scratch_shapes=[pltpu.VMEM((heads * HD, columns), BF16)],
+        interpret=INTERPRET,
+        compiler_params=PARAMS,
+        name="mix",
+    )(every_head, quarters)
+    dkv, grad_queries = pl.pallas_call(
+        backward_tile,
         out_shape=(
-            jax.ShapeDtypeStruct((TOK, columns), BF16),
+            jax.ShapeDtypeStruct((GROUP, TOK, 2 * HD), BF16),
             jax.ShapeDtypeStruct((HD, TOK), BF16),
         ),
         in_specs=[smem(), vmem(), vmem(), vmem()],
         out_specs=(vmem(), vmem()),
         scratch_shapes=[
-            pltpu.VMEM((heads * HD, columns), BF16),
-            pltpu.VMEM((2 * GROUP * GROUP, TOK), F32),
-        ],
-        interpret=INTERPRET,
-        compiler_params=PARAMS,
-        name="mix",
-    )(order, parts, every_head, quarters)
-    dkv = pl.pallas_call(
-        backward_tile,
-        out_shape=jax.ShapeDtypeStruct((GROUP, TOK, 2 * HD), BF16),
-        in_specs=[smem(), vmem(), vmem(), vmem()],
-        out_specs=vmem(),
-        scratch_shapes=[
             pltpu.VMEM((ROWS, 2 * HD), BF16),
             pltpu.VMEM((ROWS, 2 * HD), BF16),
             pltpu.VMEM((8, ROWS), F32),
             pltpu.VMEM((3 * TOK, TOK), F32),
+            pltpu.VMEM((2 * GROUP * GROUP, TOK), F32),
         ],
         interpret=INTERPRET,
         compiler_params=PARAMS,

time: 104 us -> 104 us (level)
  no operation moved by 1% of the time
where the time goes in v7:
time: 104 us; the launch traced here: 103 us
  blocking collectives  45.4 us (44%)
  starting transfers between devices  33.2 us (32%)
  Pallas kernels  11.7 us (11%)
  waiting for transfers between devices  10.4 us (10%)
    all_to_all x3, starting transfers between devices, exchange(): return lax.all_to_all(value, axis, 0, 0, tiled=True)  33.2 us
    all_to_all x1, blocking collectives, exchange(): return lax.all_to_all(value, axis, 0, 0, tiled=True)  13.7 us
    all_gather x1, blocking collectives, local(): quarters = lax.all_gather(quarters, 'x')  12.8 us
    all_gather x2, blocking collectives, local(): lax.all_gather(qg_group, 'x', tiled=True, axis_index_groups=pairs)  10.7 us
    all_to_all x3, waiting for transfers between devices, exchange(): return lax.all_to_all(value, axis, 0, 0, tiled=True)  10.4 us
    all_gather x1, blocking collectives, local(): qg_group = lax.all_gather(qg_group, 'zl')  6.07 us
    pallas_call x1, Pallas kernels, local(): pl.pallas_call(backward_tile, out_shape=(jax.ShapeDtypeStruct((GROUP, TOK...  3.71 us
    pallas_call x1, Pallas kernels, local(): pl.pallas_call(forward_tile, out_shape=jax.ShapeDtypeStruct((GROUP, OUT_R...  3.14 us
  transfers between devices with their start and end apart: 3, of which 3 were waited for; matrix products, arithmetic and copies ran while one was open for 0% of the time, Pallas kernels for 5%

profile of v7, /device:TPU:6, one launch (start us, length us, event | category | flops | bytes accessed | tf_op | source)
XLA Modules:
  0.0 102.7 jit_solution(7137981192301753745)
XLA Ops:
  0.6 2.5 %prepare.1 = (bf16[128,128]{1,0:T(8,128)(2,1)}, bf16[8,128,128]{2,1,0:T(8,128)(2,1)}) custom-call(bf16[64,128]{1,0:T(8,128)(2,1)} %bitcast.24, bf16[128,128]{1,0:T(8,128)(2,1)} %bitcast.22, bf16[64,4096]{1,0:T(8,128)(2,1)} %bitcast.19, bf16[128,4096]{1,0:T(8,128)(2,1)} %grad_hbm.1), custom_call_target="tpu_custom_call" | custom-call | tf_op jit(solution)/shard_map/prepare/pallas_call | solution.py:239
  3.2 0.0 copy-start.1
  3.2 18.8 %all-to-all-start = ((bf16[8,128,128]{2,1,0:T(8,128)(2,1)}), bf16[8,128,128]{2,1,0:T(8,128)(2,1)S(1)}, u32[]{:S(2)}, u32[]{:S(2)}) async-start(bf16[8,128,128]{2,1,0:T(8,128)(2,1)} %get-tuple-element.8), calls=%async_computation | async-start | bytes 524288 | tf_op jit(solution)/shard_map/all_to_all | solution.py:229
  22.0 0.0 copy-done.1
  22.0 4.6 %all_gather.24 = bf16[256,128]{1,0:T(8,128)(2,1)S(1)} all-gather(bf16[128,128]{1,0:T(8,128)(2,1)S(1)} %copy-done.1), channel_id=1, replica_groups={{0,16},{32,48},{1,17},{33,49},{2,18},{34,50},{3,19},{35,51},{4,20},{36,..., dimensions={0}, use_global_device_ids=true | all-gather | bytes 98304 | tf_op jit(solution)/shard_map/all_gather | solution.py:260
  26.5 6.1 %all_gather.25 = bf16[512,128]{1,0:T(8,128)(2,1)S(1)} all-gather(bf16[256,128]{1,0:T(8,128)(2,1)S(1)} %all_gather.24), channel_id=1, replica_groups={{0,48},{16,32},{1,49},{17,33},{2,50},{18,34},{3,51},{19,35},{4,52},{20,..., dimensions={0}, use_global_device_ids=true | all-gather | bytes 196608 | tf_op jit(solution)/shard_map/all_gather | solution.py:260
  32.7 6.1 %all-gather = bf16[1024,128]{1,0:T(8,128)(2,1)S(1)} all-gather(bf16[512,128]{1,0:T(8,128)(2,1)S(1)} %all_gather.25), channel_id=2, replica_groups=mesh['b'=8,'zl'=2,'x'=4,'y'=8,'c'=2] {'zl'}, dimensions={0}, use_global_device_ids=true | all-gather | bytes 393216 | tf_op jit(solution)/shard_map/all_gather | solution.py:261
  38.7 0.0 copy-start.2
  38.7 0.7 copy-done.2
  39.4 0.1 pad_add_fusion.order
  39.5 2.0 %all-to-all-done.kv_ref = bf16[8,128,128]{2,1,0:T(8,128)(2,1)S(1)} async-done(((bf16[8,128,128]{2,1,0:T(8,128)(2,1)}), bf16[8,128,128]{2,1,0:T(8,128)(2,1)S(1)}, u32[]{:S(2)}, u32[]{:S(2)}) %all-to-all-start) | async-done | bytes 262176 | tf_op jit(solution)/shard_map/all_to_all | solution.py:229
  41.5 3.1 %forward_tile.1 = bf16[8,224,128]{2,1,0:T(8,128)(2,1)S(1)} custom-call(s32[67]{0:T(128)S(1)} %pad_add_fusion.order, bf16[8,128,128]{2,1,0:T(8,128)(2,1)S(1)} %bitcast.17, bf16[8,128,128]{2,1,0:T(8,128)(2,1)S(1)} %all-to-all-done.kv_ref), custom_call_target="tpu_custom_call" | custom-call | tf_op jit(solution)/shard_map/forward_tile/pallas_call | solution.py:263
  44.6 0.0 copy-start
  44.6 13.7 %all_to_all.20.parts_ref = bf16[8,224,128]{2,1,0:T(8,128)(2,1)S(1)} all-to-all(bf16[8,224,128]{2,1,0:T(8,128)(2,1)S(1)} %forward_tile.1), channel_id=1, replica_groups=mesh['b'=8,'zl'=2,'x'=4,'y'=8,'c'=2] {'zl','x'}, dimensions={0} | all-to-all | bytes 917504 | tf_op jit(solution)/shard_map/all_to_all | solution.py:229
  58.3 0.0 copy-done
  58.3 1.3 %join_parts.1 = bf16[8,128,128]{2,1,0:T(8,128)(2,1)} custom-call(s32[67]{0:T(128)S(1)} %pad_add_fusion.order, bf16[8,224,128]{2,1,0:T(8,128)(2,1)S(1)} %all_to_all.20.parts_ref, bf16[64,4096]{1,0:T(8,128)(2,1)S(1)} %bitcast.20), custom_call_target="tpu_custom_call" | custom-call | tf_op jit(solution)/shard_map/join_parts/pallas_call | solution.py:280
  59.6 7.1 %all-to-all-start.2 = ((bf16[8,128,128]{2,1,0:T(8,128)(2,1)}), bf16[8,128,128]{2,1,0:T(8,128)(2,1)S(1)}, u32[]{:S(2)}, u32[]{:S(2)}) async-start(bf16[8,128,128]{2,1,0:T(8,128)(2,1)} %join_parts.1), calls=%async_computation.2 | async-start | bytes 524288 | tf_op jit(solution)/shard_map/all_to_all | solution.py:229
  66.7 3.7 %backward_tile.1 = (bf16[8,128,128]{2,1,0:T(8,128)(2,1)}, bf16[64,128]{1,0:T(8,128)(2,1)}) custom-call(s32[67]{0:T(128)S(1)} %pad_add_fusion.order, bf16[8,128,128]{2,1,0:T(8,128)(2,1)S(1)} %bitcast.18, bf16[8,128,128]{2,1,0:T(8,128)(2,1)S(1)} %all-to-all-done.kv_ref, bf16[8,224,128]{2,1,0:T(8,128)(2,1)S(1)} %all_to_all.20.parts_ref), custom_call_target="tpu_custom_call" | custom-call | tf_op jit(solution)/shard_map/backward_tile/pallas_call | solution.py:307
  70.4 6.8 %all-to-all-done.2 = bf16[8,128,128]{2,1,0:T(8,128)(2,1)S(1)} async-done(((bf16[8,128,128]{2,1,0:T(8,128)(2,1)}), bf16[8,128,128]{2,1,0:T(8,128)(2,1)S(1)}, u32[]{:S(2)}, u32[]{:S(2)}) %all-to-all-start.2) | async-done | bytes 262176 | tf_op jit(solution)/shard_map/all_to_all | solution.py:229
  77.2 7.3 %all-to-all-start.3 = ((bf16[8,128,128]{2,1,0:T(8,128)(2,1)}), bf16[8,128,128]{2,1,0:T(8,128)(2,1)S(1)}, u32[]{:S(2)}, u32[]{:S(2)}) async-start(bf16[8,128,128]{2,1,0:T(8,128)(2,1)} %get-tuple-element.10), calls=%async_computation.3 | async-start | bytes 524288 | tf_op jit(solution)/shard_map/all_to_all | solution.py:229
  84.5 2.2 %all-gather.1 = bf16[16,128,128]{2,1,0:T(8,128)(2,1)S(1)} all-gather(bf16[8,128,128]{2,1,0:T(8,128)(2,1)S(1)} %all-to-all-done.2), channel_id=3, replica_groups=mesh['b'=8,'zl'=2,'x'=4,'y'=8,'c'=2] {'c'}, dimensions={0}, use_global_device_ids=true | all-gather | bytes 786432 | tf_op jit(solution)/shard_map/all_gather | solution.py:291
  86.7 12.8 %all-gather.2 = bf16[8,8,32,128]{3,2,1,0:T(8,128)(2,1)S(1)} all-gather(bf16[2,8,32,128]{3,2,1,0:T(8,128)(2,1)S(1)} %constant_dynamic-slice_fusion), channel_id=4, replica_groups=mesh['b'=8,'zl'=2,'x'=4,'y'=8,'c'=2] {'x'}, dimensions={0}, use_global_device_ids=true | all-gather | bytes 655360 | tf_op jit(solution)/shard_map/all_gather | solution.py:296
  99.5 1.0 mix.1
  100.4 1.6 %all-to-all-done.3 = bf16[8,128,128]{2,1,0:T(8,128)(2,1)S(1)} async-done(((bf16[8,128,128]{2,1,0:T(8,128)(2,1)}), bf16[8,128,128]{2,1,0:T(8,128)(2,1)S(1)}, u32[]{:S(2)}, u32[]{:S(2)}) %all-to-all-start.3) | async-done | bytes 262176 | tf_op jit(solution)/shard_map/all_to_all | solution.py:229
  102.1 0.7 reduce_sum.12
  (1 shorter events, 0.0 us)
Async XLA Ops:
  3.2 18.8 %copy-start.1 = (bf16[128,128]{1,0:T(8,128)(2,1)S(1)}, bf16[128,128]{1,0:T(8,128)(2,1)}, u32[]{:S(2)}) copy-start(bf16[128,128]{1,0:T(8,128)(2,1)} %get-tuple-element.7) | copy-start | bytes 98308
  3.2 38.3 %all-to-all-start = ((bf16[8,128,128]{2,1,0:T(8,128)(2,1)}), bf16[8,128,128]{2,1,0:T(8,128)(2,1)S(1)}, u32[]{:S(2)}, u32[]{:S(2)}) async-start(bf16[8,128,128]{2,1,0:T(8,128)(2,1)} %get-tuple-element.8), calls=%async_computation | async-start | bytes 524288 | tf_op jit(solution)/shard_map/all_to_all | solution.py:229
  38.7 0.7 copy-start.2
  44.6 13.7 %copy-start = (bf16[1,64,4096]{2,1,0:T(8,128)(2,1)S(1)}, bf16[1,64,4096]{2,1,0:T(8,128)(2,1)}, u32[]{:S(2)}) copy-start(bf16[1,64,4096]{2,1,0:T(8,128)(2,1)} %param.7) | copy-start | bytes 1572868
  59.6 17.6 %all-to-all-start.2 = ((bf16[8,128,128]{2,1,0:T(8,128)(2,1)}), bf16[8,128,128]{2,1,0:T(8,128)(2,1)S(1)}, u32[]{:S(2)}, u32[]{:S(2)}) async-start(bf16[8,128,128]{2,1,0:T(8,128)(2,1)} %join_parts.1), calls=%async_computation.2 | async-start | bytes 524288 | tf_op jit(solution)/shard_map/all_to_all | solution.py:229
  77.2 24.9 %all-to-all-start.3 = ((bf16[8,128,128]{2,1,0:T(8,128)(2,1)}), bf16[8,128,128]{2,1,0:T(8,128)(2,1)S(1)}, u32[]{:S(2)}, u32[]{:S(2)}) async-start(bf16[8,128,128]{2,1,0:T(8,128)(2,1)} %get-tuple-element.10), calls=%async_computation.3 | async-start | bytes 524288 | tf_op jit(solution)/shard_map/all_to_all | solution.py:229

commit v8 on v7

--- a/solution.py
+++ b/solution.py
@@ -15,6 +15,7 @@
 STAT_ROWS = 32
 OUT_ROWS = STATS + STAT_ROWS
 QUARTERS = 4
+PIECES = 2
 WIDE = 8
 A = ("zl", "x")
 HEAD = ("y", "c")
@@ -126,20 +127,30 @@
 
 
 def prepare(
-    queries_hbm, kv_hbm, weight_hbm, grad_hbm, qg_ref, copies_ref, queries_t, kv, weight, grad, sems
+    queries_hbm, kv_hbm, weight_hbm, grad_hbm, qg_ref, copies_hbm, queries_t, weight, grad, sems
 ):
-    pairs = ((kv_hbm, kv), (weight_hbm, weight), (grad_hbm, grad), (queries_hbm, queries_t))
-    loads = [pltpu.make_async_copy(*pair, sems.at[k]) for k, pair in enumerate(pairs)]
-    for load in loads:
-        load.start()
+    spread = [
+        pltpu.make_async_copy(kv_hbm, copies_hbm.at[p], sems.at[p]) for p in range(GROUP)
+    ]
+    width = weight.shape[1] // PIECES
+    pieces = [pl.ds(k * width, width) for k in range(PIECES)]
+    pairs = [(queries_hbm, queries_t)]
+    for piece in pieces:
+        pairs.append((weight_hbm.at[:, piece], weight.at[:, piece]))
+        pairs.append((grad_hbm.at[:, piece], grad.at[:, piece]))
+    loads = [pltpu.make_async_copy(*pair, sems.at[GROUP + k]) for k, pair in enumerate(pairs)]
+    for copy in spread + loads:
+        copy.start()
     loads[0].wait()
-    for p in range(GROUP):
-        copies_ref[p] = kv[...]
-    for load in loads[1:]:
-        load.wait()
-    grad_att = nt(grad[...], weight[...])
     scaled = jnp.transpose(queries_t[...].astype(F32)) * HD**-0.5
+    grad_att = jnp.zeros((TOK, HD), F32)
+    for k, piece in enumerate(pieces):
+        loads[1 + 2 * k].wait()
+        loads[2 + 2 * k].wait()
+        grad_att += nt(grad[:, piece], weight[:, piece])
     qg_ref[...] = jnp.concatenate([scaled, grad_att], axis=1).astype(BF16)
+    for copy in spread:
+        copy.wait()
 
 
 def join_parts(order, parts_ref, weight_ref, out_ref, own):
@@ -243,13 +254,12 @@
             jax.ShapeDtypeStruct((GROUP, TOK, 2 * HD), BF16),
         ),
         in_specs=[pl.BlockSpec(memory_space=pltpu.HBM)] * 4,
-        out_specs=(vmem(), vmem()),
+        out_specs=(vmem(), pl.BlockSpec(memory_space=pltpu.HBM)),
         scratch_shapes=[
             pltpu.VMEM((HD, TOK), BF16),
-            pltpu.VMEM((TOK, 2 * HD), BF16),
             pltpu.VMEM(weight.shape, BF16),
             pltpu.VMEM(out_grad.shape, BF16),
-            pltpu.SemaphoreType.DMA((4,)),
+            pltpu.SemaphoreType.DMA((GROUP + 1 + 2 * PIECES,)),
         ],
         interpret=INTERPRET,
         name="prepare",

time: 104 us -> 111 us (1.067)
  Pallas kernels: 11.7 us -> 18.9 us
    pallas_call x1, Pallas kernels: 2.55 us -> 9.77 us  [local(): pl.pallas_call(prepare, out_shape=(jax.ShapeDtypeStruct((TOK, 2 * HD), BF...]
  transfers between devices with their start and end apart: 3 -> 3, of which waited for: 3 -> 3; matrix products, arithmetic and copies ran while one was open for 0% -> 0% of each run, Pallas kernels for 5% -> 4%
where the time goes in v8:
time: 111 us; the launch traced here: 110 us
  blocking collectives  45.4 us (41%)
  starting transfers between devices  33.2 us (30%)
  Pallas kernels  18.9 us (17%)
  waiting for transfers between devices  10.4 us (9%)
    all_to_all x3, starting transfers between devices, exchange(): return lax.all_to_all(value, axis, 0, 0, tiled=True)  33.2 us
    all_to_all x1, blocking collectives, exchange(): return lax.all_to_all(value, axis, 0, 0, tiled=True)  13.7 us
    all_gather x1, blocking collectives, local(): quarters = lax.all_gather(quarters, 'x')  12.8 us
    all_gather x2, blocking collectives, local(): lax.all_gather(qg_group, 'x', tiled=True, axis_index_groups=pairs)  10.7 us
    all_to_all x3, waiting for transfers between devices, exchange(): return lax.all_to_all(value, axis, 0, 0, tiled=True)  10.4 us
    pallas_call x1, Pallas kernels, local(): pl.pallas_call(prepare, out_shape=(jax.ShapeDtypeStruct((TOK, 2 * HD), BF...  9.77 us
    all_gather x1, blocking collectives, local(): qg_group = lax.all_gather(qg_group, 'zl')  6.06 us
    pallas_call x1, Pallas kernels, local(): pl.pallas_call(backward_tile, out_shape=(jax.ShapeDtypeStruct((GROUP, TOK...  3.71 us
  transfers between devices with their start and end apart: 3, of which 3 were waited for; matrix products, arithmetic and copies ran while one was open for 0% of the time, Pallas kernels for 4%

profile of v8, /device:TPU:6, one launch (start us, length us, event | category | flops | bytes accessed | tf_op | source)
XLA Modules:
  0.0 110.0 jit_solution(1001487214793089422)
XLA Ops:
  0.6 9.8 %prepare.1 = (bf16[128,128]{1,0:T(8,128)(2,1)}, bf16[8,128,128]{2,1,0:T(8,128)(2,1)}) custom-call(bf16[64,128]{1,0:T(8,128)(2,1)} %bitcast.24, bf16[128,128]{1,0:T(8,128)(2,1)} %bitcast.22, bf16[64,4096]{1,0:T(8,128)(2,1)} %bitcast.19, bf16[128,4096]{1,0:T(8,128)(2,1)} %grad_hbm.1), custom_call_target="tpu_custom_call" | custom-call | tf_op jit(solution)/shard_map/prepare/pallas_call | solution.py:250
  10.4 0.0 copy-start.1
  10.4 18.8 %all-to-all-start = ((bf16[8,128,128]{2,1,0:T(8,128)(2,1)}), bf16[8,128,128]{2,1,0:T(8,128)(2,1)S(1)}, u32[]{:S(2)}, u32[]{:S(2)}) async-start(bf16[8,128,128]{2,1,0:T(8,128)(2,1)} %get-tuple-element.8), calls=%async_computation | async-start | bytes 524288 | tf_op jit(solution)/shard_map/all_to_all | solution.py:240
  29.2 0.0 copy-done.1
  29.2 4.6 %all_gather.24 = bf16[256,128]{1,0:T(8,128)(2,1)S(1)} all-gather(bf16[128,128]{1,0:T(8,128)(2,1)S(1)} %copy-done.1), channel_id=1, replica_groups={{0,16},{32,48},{1,17},{33,49},{2,18},{34,50},{3,19},{35,51},{4,20},{36,..., dimensions={0}, use_global_device_ids=true | all-gather | bytes 98304 | tf_op jit(solution)/shard_map/all_gather | solution.py:270
  33.8 6.1 %all_gather.25 = bf16[512,128]{1,0:T(8,128)(2,1)S(1)} all-gather(bf16[256,128]{1,0:T(8,128)(2,1)S(1)} %all_gather.24), channel_id=1, replica_groups={{0,48},{16,32},{1,49},{17,33},{2,50},{18,34},{3,51},{19,35},{4,52},{20,..., dimensions={0}, use_global_device_ids=true | all-gather | bytes 196608 | tf_op jit(solution)/shard_map/all_gather | solution.py:270
  39.9 6.1 %all-gather = bf16[1024,128]{1,0:T(8,128)(2,1)S(1)} all-gather(bf16[512,128]{1,0:T(8,128)(2,1)S(1)} %all_gather.25), channel_id=2, replica_groups=mesh['b'=8,'zl'=2,'x'=4,'y'=8,'c'=2] {'zl'}, dimensions={0}, use_global_device_ids=true | all-gather | bytes 393216 | tf_op jit(solution)/shard_map/all_gather | solution.py:271
  46.0 0.0 copy-start.2
  46.0 0.7 copy-done.2
  46.6 0.1 pad_add_fusion.order
  46.7 2.0 %all-to-all-done.kv_ref = bf16[8,128,128]{2,1,0:T(8,128)(2,1)S(1)} async-done(((bf16[8,128,128]{2,1,0:T(8,128)(2,1)}), bf16[8,128,128]{2,1,0:T(8,128)(2,1)S(1)}, u32[]{:S(2)}, u32[]{:S(2)}) %all-to-all-start) | async-done | bytes 262176 | tf_op jit(solution)/shard_map/all_to_all | solution.py:240
  48.7 3.1 %forward_tile.1 = bf16[8,224,128]{2,1,0:T(8,128)(2,1)S(1)} custom-call(s32[67]{0:T(128)S(1)} %pad_add_fusion.order, bf16[8,128,128]{2,1,0:T(8,128)(2,1)S(1)} %bitcast.17, bf16[8,128,128]{2,1,0:T(8,128)(2,1)S(1)} %all-to-all-done.kv_ref), custom_call_target="tpu_custom_call" | custom-call | tf_op jit(solution)/shard_map/forward_tile/pallas_call | solution.py:273
  51.8 0.0 copy-start
  51.8 13.7 %all_to_all.20.parts_ref = bf16[8,224,128]{2,1,0:T(8,128)(2,1)S(1)} all-to-all(bf16[8,224,128]{2,1,0:T(8,128)(2,1)S(1)} %forward_tile.1), channel_id=1, replica_groups=mesh['b'=8,'zl'=2,'x'=4,'y'=8,'c'=2] {'zl','x'}, dimensions={0} | all-to-all | bytes 917504 | tf_op jit(solution)/shard_map/all_to_all | solution.py:240
  65.5 0.0 copy-done
  65.5 1.3 %join_parts.1 = bf16[8,128,128]{2,1,0:T(8,128)(2,1)} custom-call(s32[67]{0:T(128)S(1)} %pad_add_fusion.order, bf16[8,224,128]{2,1,0:T(8,128)(2,1)S(1)} %all_to_all.20.parts_ref, bf16[64,4096]{1,0:T(8,128)(2,1)S(1)} %bitcast.20), custom_call_target="tpu_custom_call" | custom-call | tf_op jit(solution)/shard_map/join_parts/pallas_call | solution.py:290
  66.8 7.1 %all-to-all-start.2 = ((bf16[8,128,128]{2,1,0:T(8,128)(2,1)}), bf16[8,128,128]{2,1,0:T(8,128)(2,1)S(1)}, u32[]{:S(2)}, u32[]{:S(2)}) async-start(bf16[8,128,128]{2,1,0:T(8,128)(2,1)} %join_parts.1), calls=%async_computation.2 | async-start | bytes 524288 | tf_op jit(solution)/shard_map/all_to_all | solution.py:240
  73.9 3.7 %backward_tile.1 = (bf16[8,128,128]{2,1,0:T(8,128)(2,1)}, bf16[64,128]{1,0:T(8,128)(2,1)}) custom-call(s32[67]{0:T(128)S(1)} %pad_add_fusion.order, bf16[8,128,128]{2,1,0:T(8,128)(2,1)S(1)} %bitcast.18, bf16[8,128,128]{2,1,0:T(8,128)(2,1)S(1)} %all-to-all-done.kv_ref, bf16[8,224,128]{2,1,0:T(8,128)(2,1)S(1)} %all_to_all.20.parts_ref), custom_call_target="tpu_custom_call" | custom-call | tf_op jit(solution)/shard_map/backward_tile/pallas_call | solution.py:317
  77.7 6.8 %all-to-all-done.2 = bf16[8,128,128]{2,1,0:T(8,128)(2,1)S(1)} async-done(((bf16[8,128,128]{2,1,0:T(8,128)(2,1)}), bf16[8,128,128]{2,1,0:T(8,128)(2,1)S(1)}, u32[]{:S(2)}, u32[]{:S(2)}) %all-to-all-start.2) | async-done | bytes 262176 | tf_op jit(solution)/shard_map/all_to_all | solution.py:240
  84.4 7.3 %all-to-all-start.3 = ((bf16[8,128,128]{2,1,0:T(8,128)(2,1)}), bf16[8,128,128]{2,1,0:T(8,128)(2,1)S(1)}, u32[]{:S(2)}, u32[]{:S(2)}) async-start(bf16[8,128,128]{2,1,0:T(8,128)(2,1)} %get-tuple-element.10), calls=%async_computation.3 | async-start | bytes 524288 | tf_op jit(solution)/shard_map/all_to_all | solution.py:240
  91.7 2.2 %all-gather.1 = bf16[16,128,128]{2,1,0:T(8,128)(2,1)S(1)} all-gather(bf16[8,128,128]{2,1,0:T(8,128)(2,1)S(1)} %all-to-all-done.2), channel_id=3, replica_groups=mesh['b'=8,'zl'=2,'x'=4,'y'=8,'c'=2] {'c'}, dimensions={0}, use_global_device_ids=true | all-gather | bytes 786432 | tf_op jit(solution)/shard_map/all_gather | solution.py:301
  93.9 12.8 %all-gather.2 = bf16[8,8,32,128]{3,2,1,0:T(8,128)(2,1)S(1)} all-gather(bf16[2,8,32,128]{3,2,1,0:T(8,128)(2,1)S(1)} %constant_dynamic-slice_fusion), channel_id=4, replica_groups=mesh['b'=8,'zl'=2,'x'=4,'y'=8,'c'=2] {'x'}, dimensions={0}, use_global_device_ids=true | all-gather | bytes 655360 | tf_op jit(solution)/shard_map/all_gather | solution.py:306
  106.7 1.0 mix.1
  107.6 1.7 %all-to-all-done.3 = bf16[8,128,128]{2,1,0:T(8,128)(2,1)S(1)} async-done(((bf16[8,128,128]{2,1,0:T(8,128)(2,1)}), bf16[8,128,128]{2,1,0:T(8,128)(2,1)S(1)}, u32[]{:S(2)}, u32[]{:S(2)}) %all-to-all-start.3) | async-done | bytes 262176 | tf_op jit(solution)/shard_map/all_to_all | solution.py:240
  109.3 0.7 reduce_sum.12
  (1 shorter events, 0.0 us)
Async XLA Ops:
  10.4 18.8 %copy-start.1 = (bf16[128,128]{1,0:T(8,128)(2,1)S(1)}, bf16[128,128]{1,0:T(8,128)(2,1)}, u32[]{:S(2)}) copy-start(bf16[128,128]{1,0:T(8,128)(2,1)} %get-tuple-element.7) | copy-start | bytes 98308
  10.4 38.3 %all-to-all-start = ((bf16[8,128,128]{2,1,0:T(8,128)(2,1)}), bf16[8,128,128]{2,1,0:T(8,128)(2,1)S(1)}, u32[]{:S(2)}, u32[]{:S(2)}) async-start(bf16[8,128,128]{2,1,0:T(8,128)(2,1)} %get-tuple-element.8), calls=%async_computation | async-start | bytes 524288 | tf_op jit(solution)/shard_map/all_to_all | solution.py:240
  46.0 0.7 copy-start.2
  51.8 13.7 %copy-start = (bf16[1,64,4096]{2,1,0:T(8,128)(2,1)S(1)}, bf16[1,64,4096]{2,1,0:T(8,128)(2,1)}, u32[]{:S(2)}) copy-start(bf16[1,64,4096]{2,1,0:T(8,128)(2,1)} %param.7) | copy-start | bytes 1572868
  66.8 17.6 %all-to-all-start.2 = ((bf16[8,128,128]{2,1,0:T(8,128)(2,1)}), bf16[8,128,128]{2,1,0:T(8,128)(2,1)S(1)}, u32[]{:S(2)}, u32[]{:S(2)}) async-start(bf16[8,128,128]{2,1,0:T(8,128)(2,1)} %join_parts.1), calls=%async_computation.2 | async-start | bytes 524288 | tf_op jit(solution)/shard_map/all_to_all | solution.py:240
  84.4 24.9 %all-to-all-start.3 = ((bf16[8,128,128]{2,1,0:T(8,128)(2,1)}), bf16[8,128,128]{2,1,0:T(8,128)(2,1)S(1)}, u32[]{:S(2)}, u32[]{:S(2)}) async-start(bf16[8,128,128]{2,1,0:T(8,128)(2,1)} %get-tuple-element.10), calls=%async_computation.3 | async-start | bytes 524288 | tf_op jit(solution)/shard_map/all_to_all | solution.py:240
